TPU v7x, 256 devices: a whole 4x4x8 slice. The times are simulated.
256 devices in a mesh: expert: 64 (over y, z, core), replica: 4 (over x).
Axes of the slice: x: 4, y: 4, z: 8, core: 2. Of those that a mesh axis runs over, the one named last changes fastest.
Arguments:
- tokens: bfloat16 [3072, 7168], P('expert', 'replica'), may hold values from -18 to 18
- expert_ids: int32 [3072, 8], P('expert'), may hold values from 0 to 63, all different within a row; in each aligned block of 48 rows (0 to 47, 48 to 95, ...) at most 12 rows name the same one
- route_weights: bfloat16 [3072, 8], P('expert'), may hold values from 0.1 to 1.5
- gate_weight: bfloat16 [64, 7168, 1024], P('expert', 'replica'), may hold values from -0.0625 to 0.0625
- up_weight: bfloat16 [64, 7168, 1024], P('expert', 'replica'), may hold values from -0.0625 to 0.0625
- down_weight: bfloat16 [64, 1024, 7168], P('expert', None, 'replica'), may hold values from -0.1875 to 0.1875
- bin_edges: float32 [16], replicated, may hold values from 0 to 20, as said below
Outputs:
- mixed: bfloat16 [3072, 7168], P('expert', 'replica')
- expert_load: float32 [64], P('expert')
Inputs may be any that keep to these rules, and one draw needn't show every extreme that they name: `expert_ids`: each row names 8 different experts; within the 48 rows of one index of expert no expert is named by more than 12 rows, a bound that some block reaches. `bin_edges`: strictly increasing and positive; the last edge is 20, above every token entry's magnitude.
All inputs are finite; a program needn't handle non-finite values.
Results may differ from a plain program's by a relative error of at most 0.019.
Values may be sent and summed in bfloat16 or wider, within the bound.
No kernel may reach another device: no remote copies, remote signals or barrier semaphores. Data moves between devices by JAX's collectives and lax.ppermute only.
A program may use at most 128 MiB of HBM per device.

v0:
```python
import functools

import jax
import jax.numpy as jnp
import numpy as np
from jax import lax
from jax.experimental import pallas as pl
from jax.experimental.pallas import tpu as pltpu
from jax.sharding import Mesh
from jax.sharding import PartitionSpec as P


FINE = 8
CLIP_PARTS = 8
CAP = 12
META = 128
NY, NZ, NC, NX = 4, 8, 2, 4
PEERS = NY * NC
EXPERT = ("y", "z", "c")
OWNERS = ("y", "c")
GROUPS = ((0, 1, 7, 2), (6, 3, 5, 4))

BF = jnp.bfloat16
F32 = jnp.float32
VMEM = pltpu.VMEM
SMEM = pltpu.SMEM


def whole(space=VMEM):
    return pl.BlockSpec(memory_space=space)


def lane_table(count):
    span = CAP * count
    lane = np.arange(PEERS * span)
    peer = lane // span
    table = np.zeros((8, PEERS * span), np.float32)
    table[0] = (peer // NC) * (NZ * NC) + peer % NC
    table[1] = (lane % span) // CAP
    table[2] = lane % CAP
    return table


def dispatch_kernel(count, others, z_ref, table_ref, *refs):
    blocks, extra = refs[:count], refs[count : count + others]
    rows_ref, combine_ref, map_ref, tokens_ref = refs[count + others :]
    tok, width = rows_ref.shape[2] and blocks[0].shape[0], rows_ref.shape[2]
    span = CAP * count
    lanes = PEERS * span
    z_part = (z_ref[0] * NC).astype(F32)
    expert = table_ref[0:1, :] + z_part
    place = table_ref[1:2, :]
    rank_wanted = table_ref[2:3, :]
    row = lax.broadcasted_iota(jnp.int32, (tok, tok), 0)
    col = lax.broadcasted_iota(jnp.int32, (tok, tok), 1)
    before = jnp.where(col < row, 1.0, 0.0).astype(BF)
    for i in range(count):
        meta = blocks[i][:, width : width + META].astype(F32)
        hit = jnp.zeros((tok, lanes), F32)
        weight = jnp.zeros((tok, lanes), F32)
        for k in range(8):
            same = meta[:, k : k + 1] == expert
            hit = jnp.where(same, 1.0, hit)
            weight = jnp.where(same, meta[:, 8 + k : 9 + k], weight)
        rank = jnp.dot(before, hit.astype(BF), preferred_element_type=F32)
        chosen = (hit > 0.0) & (rank == rank_wanted) & (place == float(i))
        map_ref[i * tok : (i + 1) * tok, :] = jnp.where(chosen, 1.0, 0.0).astype(BF)
        combine_ref[i * tok : (i + 1) * tok, :] = jnp.where(chosen, weight, 0.0).astype(BF)
        tokens_ref[i * tok : (i + 1) * tok, :] = blocks[i][:, :width]
    rows = lax.dot_general(
        map_ref[...], tokens_ref[...], (((0,), (0,)), ((), ())), preferred_element_type=F32
    ).astype(BF)
    for d in range(PEERS):
        rows_ref[d, 0:span, :] = rows[d * span : (d + 1) * span, :]
    if rows_ref.shape[1] > span:
        lane = lax.broadcasted_iota(jnp.int32, (1, META), 1)
        peer_expert = ((lane // NC) * (NZ * NC) + lane % NC).astype(F32) + z_part
        named = jnp.zeros((1, META), F32)
        load = jnp.zeros((1, META), F32)
        metas = [b[:, width : width + META] for b in blocks] + [b[...] for b in extra]
        for meta in metas:
            meta = meta.astype(F32)
            for k in range(8):
                same = meta[:, k : k + 1] == peer_expert
                named = named + jnp.sum(jnp.where(same, 1.0, 0.0), axis=0, keepdims=True)
                load = load + jnp.sum(
                    jnp.where(same, meta[:, 8 + k : 9 + k], 0.0), axis=0, keepdims=True
                )
        high = load.astype(BF).astype(F32)
        middle = (load - high).astype(BF).astype(F32)
        low = load - high - middle
        line = lax.broadcasted_iota(jnp.int32, (8, META), 0)
        pieces = jnp.where(
            line == 0, named, jnp.where(line == 1, high, jnp.where(line == 2, middle, jnp.where(line == 3, low, 0.0)))
        )
        for d in range(PEERS):
            rows_ref[d, span : span + 8, :] = jnp.broadcast_to(pieces[:, d : d + 1], (8, width)).astype(BF)


def dispatch(z, blocks, extra, last):
    count = len(blocks)
    tok, wide = blocks[0].shape
    width = wide - META
    span = CAP * count
    lanes = PEERS * span
    table = jnp.asarray(lane_table(count))
    side = pl.BlockSpec((tok, META), lambda i: (0, width // META))
    full = pl.BlockSpec((tok, wide), lambda i: (0, 0))
    tall = span + (8 if last else 0)
    return pl.pallas_call(
        functools.partial(dispatch_kernel, count, len(extra)),
        grid=(1,),
        in_specs=[whole(SMEM), pl.BlockSpec((8, lanes), lambda i: (0, 0))]
        + [full] * count
        + [side] * len(extra),
        out_specs=[
            pl.BlockSpec((PEERS, tall, width), lambda i: (0, 0, 0)),
            pl.BlockSpec((tok * count, lanes), lambda i: (0, 0)),
        ],
        out_shape=[
            jax.ShapeDtypeStruct((PEERS, tall, width), BF),
            jax.ShapeDtypeStruct((tok * count, lanes), BF),
        ],
        scratch_shapes=[VMEM((tok * count, lanes), BF), VMEM((tok * count, width), BF)],
        name="dispatch",
    )(z, table, *blocks, *extra)


STRIP = 256


def expert_kernel(spans, x_ref, edges_ref, gate_hbm, up_hbm, *refs):
    groups = len(spans)
    arrived = refs[:groups]
    outs = refs[groups : groups + 2 * NX * groups]
    load_ref = refs[groups + 2 * NX * groups]
    gate_ref, up_ref, clipped, sems = refs[groups + 2 * NX * groups + 1 :]
    width = clipped.shape[1]
    copies = [
        pltpu.make_async_copy(gate_hbm, gate_ref, sems.at[0]),
        pltpu.make_async_copy(up_hbm, up_ref, sems.at[1]),
    ]
    for copy in copies:
        copy.start()
    edges = [edges_ref[j] for j in range(16)]
    last, tail = arrived[-1], spans[-1]
    load = jnp.zeros((8, 128), F32)
    for d in range(PEERS):
        load = load + last[d, tail : tail + 8, 0:128].astype(F32)
    load_ref[...] = jnp.broadcast_to(load[1:2] + load[2:3] + load[3:4], (8, 128))

    def strip(s, carry):
        at = pl.ds(pl.multiple_of(s * STRIP, STRIP), STRIP)
        total = jnp.zeros((8, STRIP), F32)
        for d in range(PEERS):
            total = total + last[d, tail : tail + 8, at].astype(F32)
        limit = jnp.floor(total[0:1] / float(CLIP_PARTS))

        def more_above(level):
            near = level.astype(BF).astype(F32)
            above = (level * (1.0 + 2.0**-8)).astype(BF).astype(F32)
            bound = jnp.where(near >= level, near, above)
            bound = jnp.broadcast_to(bound, (16, STRIP)).astype(BF)
            count = jnp.zeros((16, STRIP), BF)
            for g in range(groups):
                for d in range(PEERS):
                    for r in range(0, spans[g], 16):
                        size = jnp.abs(arrived[g][d, r : r + 16, at])
                        count = count + jnp.where(size >= bound, jnp.ones_like(bound), jnp.zeros_like(bound))
            return jnp.sum(count.astype(F32), axis=0, keepdims=True) > limit

        def edge_at(place):
            value = jnp.zeros((1, STRIP), F32)
            for j in range(16):
                value = jnp.where(place == float(j), edges[j], value)
            return value

        m = jnp.zeros((1, STRIP), F32)
        for step in (8.0, 4.0, 2.0, 1.0):
            m = jnp.where(more_above(edge_at(m + (step - 1.0))), m + step, m)
        upper, lower = edge_at(m), edge_at(m - 1.0)
        n = jnp.zeros((1, STRIP), F32)
        for step in (4.0, 2.0, 1.0):
            level = lower + (upper - lower) * ((n + step) * (1.0 / FINE))
            n = jnp.where(more_above(level), n + step, n)
        scale = jnp.where(n == FINE - 1.0, upper, lower + (upper - lower) * ((n + 1.0) * (1.0 / FINE)))
        top = jnp.broadcast_to(scale, (16, STRIP)).astype(BF)
        base = 0
        for g in range(groups):
            share = PEERS * spans[g] // NX
            for d in range(PEERS):
                turn = lax.rem(d * NX // PEERS - x_ref[0] + NX, NX)
                start = base + turn * share + d % (PEERS // NX) * spans[g]
                for r in range(0, spans[g], 16):
                    clipped[pl.ds(pl.multiple_of(start + r, 16), 16), at] = jnp.minimum(
                        jnp.maximum(arrived[g][d, r : r + 16, at], -top), top
                    )
            base += PEERS * spans[g]
        return carry

    lax.fori_loop(0, width // STRIP, strip, 0)
    for copy in copies:
        copy.wait()
    base = PEERS * sum(spans)
    for g in reversed(range(groups)):
        share = PEERS * spans[g] // NX
        base -= share * NX
        block = clipped[base : base + share * NX, :]
        for side, weight in enumerate((gate_ref, up_ref)):
            product = jnp.dot(block, weight[...], preferred_element_type=F32).astype(BF)
            for j in range(NX):
                outs[2 * (NX * g + j) + side][...] = product[j * share : (j + 1) * share, :]


def expert_in(x, edges, gate, up, arrived, spans):
    width, hidden = gate.shape
    shapes = []
    for span in spans:
        shapes += [jax.ShapeDtypeStruct((PEERS * span // NX, hidden), BF)] * (2 * NX)
    shapes.append(jax.ShapeDtypeStruct((8, 128), F32))
    outs = pl.pallas_call(
        functools.partial(expert_kernel, spans),
        in_specs=[whole(SMEM), whole(SMEM), whole(pl.ANY), whole(pl.ANY)] + [whole()] * len(spans),
        out_specs=[whole()] * len(shapes),
        out_shape=shapes,
        scratch_shapes=[
            VMEM((width, hidden), BF),
            VMEM((width, hidden), BF),
            VMEM((PEERS * sum(spans), width), BF),
            pltpu.SemaphoreType.DMA((2,)),
        ],
        name="expert_in",
    )(x, edges, gate, up, *arrived)
    pieces = outs[:-1]
    step = 2 * NX
    return [pieces[g * step : (g + 1) * step] for g in range(len(spans))], outs[-1]


def down_kernel(x_ref, down_ref, *refs):
    out_ref, all_ref = refs[NX:]
    share = refs[0].shape[0]
    for j in range(NX):
        at = pl.multiple_of(lax.rem(x_ref[0] + j, NX) * share, 16)
        all_ref[pl.ds(at, share), :] = refs[j][...]
    out_ref[...] = jnp.dot(all_ref[...], down_ref[...], preferred_element_type=F32).astype(BF)


def expert_out(x, down, pieces):
    share, _ = pieces[0].shape
    return pl.pallas_call(
        down_kernel,
        in_specs=[whole(SMEM)] + [whole()] * (1 + NX),
        out_specs=whole(),
        out_shape=jax.ShapeDtypeStruct((share * NX, down.shape[1]), BF),
        scratch_shapes=[VMEM((share * NX, down.shape[0]), BF)],
        name="expert_out",
    )(x, down, *pieces)


def combine_kernel(count, combine_ref, back_ref, *outs):
    tok = outs[0].shape[0]
    total = jnp.dot(combine_ref[...], back_ref[...], preferred_element_type=F32).astype(BF)
    for i in range(count):
        outs[i][...] = total[i * tok : (i + 1) * tok, :]


def combined(combine, back, count):
    tok = combine.shape[0] // count
    return pl.pallas_call(
        functools.partial(combine_kernel, count),
        in_specs=[whole(), whole()],
        out_specs=[whole()] * count,
        out_shape=[jax.ShapeDtypeStruct((tok, back.shape[1]), BF)] * count,
        name="combine",
    )(combine, back)


def ring(value, axis, size, shift):
    if shift % size == 0:
        return value
    return lax.ppermute(value, axis, [(i, (i + shift) % size) for i in range(size)])


def body(tokens, expert_ids, route_weights, gate_weight, up_weight, down_weight, bin_edges):
    tok, width = tokens.shape
    z = lax.axis_index("z").astype(jnp.int32).reshape(1)
    x = lax.axis_index("x").astype(jnp.int32).reshape(1)
    side = jnp.concatenate([expert_ids.astype(BF), route_weights], axis=1)
    side = jnp.pad(side, ((0, 0), (0, META - side.shape[1])))
    wide = jnp.concatenate([tokens, side], axis=1)
    blocks = {}
    for group in GROUPS:
        for o in group:
            blocks[o] = ring(wide, "z", NZ, -o)
    arrived, combines, spans = [], [], []
    for number, group in enumerate(GROUPS):
        last = number == len(GROUPS) - 1
        extra = [blocks[o] for other in GROUPS[:-1] for o in other] if last else []
        rows, combine = dispatch(z, [blocks[o] for o in group], extra, last)
        arrived.append(lax.all_to_all(rows, OWNERS, 0, 0, tiled=True))
        combines.append(combine)
        spans.append(CAP * len(group))
    partials, load = expert_in(x, bin_edges, gate_weight[0], up_weight[0], arrived, tuple(spans))
    expert_load = load[0, 0:1] / (tok * expert_ids.shape[1])
    total = None
    for number in reversed(range(len(GROUPS))):
        group, pieces = GROUPS[number], partials[number]
        gates, ups = pieces[0::2], pieces[1::2]
        far_gate = ring(gates[2], "x", NX, 1)
        far_up = ring(ups[2], "x", NX, -1)
        near_up = ring(ups[1], "x", NX, 1)
        near_gate = ring(gates[3], "x", NX, -1)
        sum_gate = (gates[1].astype(F32) + far_gate.astype(F32)).astype(BF)
        sum_up = (ups[3].astype(F32) + far_up.astype(F32)).astype(BF)
        right_gate = ring(sum_gate, "x", NX, 1)
        left_up = ring(sum_up, "x", NX, -1)
        gate = gates[0].astype(F32) + right_gate.astype(F32) + near_gate.astype(F32)
        up = ups[0].astype(F32) + near_up.astype(F32) + left_up.astype(F32)
        hidden = (jax.nn.silu(gate) * up).astype(BF)
        shares = [ring(hidden, "x", NX, -j) for j in range(NX)]
        result = expert_out(x, down_weight[0], shares)
        result = result.reshape(PEERS, spans[number], width)
        back = lax.all_to_all(result, OWNERS, 0, 0, tiled=True).reshape(-1, width)
        sums = combined(combines[number], back, len(group))
        sums = [ring(part, "z", NZ, o) for o, part in zip(group, sums)]
        for part in sums:
            total = part.astype(F32) if total is None else total + part.astype(F32)
    return (total.astype(BF), expert_load)


def solution(mesh):
    finer = Mesh(mesh.devices.reshape(NY, NZ, NC, NX), ("y", "z", "c", "x"))
    placed = (
        P(EXPERT, "x"),
        P(EXPERT, None),
        P(EXPERT, None),
        P(EXPERT, "x", None),
        P(EXPERT, "x", None),
        P(EXPERT, None, "x"),
        P(),
    )
    return jax.shard_map(
        body,
        mesh=finer,
        in_specs=placed,
        out_specs=(P(EXPERT, "x"), P(EXPERT)),
        check_vma=False,
    )
```

profile of v0, /device:TPU:32, one launch (start us, length us, event | category | flops | bytes accessed | tf_op | source)
XLA Modules:
  0.0 251.6 jit_solution(9064392910919891373)
XLA Ops:
  2.1 0.9 fusion.1.refs_4_.refs_0_
  3.1 5.5 %collective-permute-start.6 = (bf16[48,1920]{1,0:T(8,128)(2,1)S(1)}, bf16[48,1920]{1,0:T(8,128)(2,1)S(1)}, u32[]{:S(2)}, u32[]{:S(2)}) collective-permute-start(bf16[48,1920]{1,0:T(8,128)(2,1)S(1)} %fusion.1.refs_4_.refs_0_), channel_id=1, source_target_pairs={{0,48},{8,56},{16,0},{24,8},{32,16},{40,24},{48,32},{56,40},{1,49}... | collective-permute-start | bytes 552968 | tf_op jit(solution)/shard_map/ppermute | solution.py:281
  8.5 2.0 collective-permute-start.4
  10.6 4.8 %collective-permute-done.6.refs_7_.refs_3_ = bf16[48,1920]{1,0:T(8,128)(2,1)S(1)} collective-permute-done((bf16[48,1920]{1,0:T(8,128)(2,1)S(1)}, bf16[48,1920]{1,0:T(8,128)(2,1)S(1)}, u32[]{:S(2)}, u32[]{:S(2)}) %collective-permute-start.6) | collective-permute-done | bytes 184352 | tf_op jit(solution)/shard_map/ppermute | solution.py:281
  15.3 3.5 %collective-permute-done.4.refs_5_.refs_1_ = bf16[48,1920]{1,0:T(8,128)(2,1)S(1)} collective-permute-done((bf16[48,1920]{1,0:T(8,128)(2,1)S(1)}, bf16[48,1920]{1,0:T(8,128)(2,1)S(1)}, u32[]{:S(2)}, u32[]{:S(2)}) %collective-permute-start.4) | collective-permute-done | bytes 184352 | tf_op jit(solution)/shard_map/ppermute | solution.py:281
  19.5 3.4 %dispatch.3 = (bf16[8,48,1792]{2,1,0:T(8,128)(2,1)}, bf16[192,384]{1,0:T(8,128)(2,1)}) custom-call(s32[1]{0:T(128)} %bitcast.z_ref, f32[8,384]{1,0:T(8,128)} %constant.21.clone.table_ref, bf16[48,1920]{1,0:T(8,128)(2,1)} %copy-done.4, bf16[48,1920]{1,0:T(8,128)(2,1)} %copy-done.10, bf16[48,1920]{1,0:T(8,128)(2,1)} %copy-done.9, bf16[48,1920]{1,0:T(8,128)(2,1)} %copy-done.8), custom_call_target="tpu_custom_call" | custom-call | tf_op jit(solution)/shard_map/dispatch/pallas_call | solution.py:110
  22.9 4.6 %all-to-all-start = ((bf16[8,48,1792]{2,1,0:T(8,128)(2,1)}), bf16[8,48,1792]{2,1,0:T(8,128)(2,1)S(1)}, u32[]{:S(2)}, u32[]{:S(2)}) async-start(bf16[8,48,1792]{2,1,0:T(8,128)(2,1)} %get-tuple-element.32), calls=%async_computation | async-start | bytes 2752512 | tf_op jit(solution)/shard_map/all_to_all | solution.py:300
  27.6 5.4 %collective-permute-start.3 = (bf16[48,1920]{1,0:T(8,128)(2,1)S(1)}, bf16[48,1920]{1,0:T(8,128)(2,1)S(1)}, u32[]{:S(2)}, u32[]{:S(2)}) collective-permute-start(bf16[48,1920]{1,0:T(8,128)(2,1)S(1)} %copy-done.5), channel_id=1, source_target_pairs={{0,32},{8,40},{16,48},{24,56},{32,0},{40,8},{48,16},{56,24},{1,33}... | collective-permute-start | bytes 552968 | tf_op jit(solution)/shard_map/ppermute | solution.py:281
  32.9 1.7 collective-permute-start.2
  34.6 3.4 %collective-permute-start.1 = (bf16[48,1920]{1,0:T(8,128)(2,1)S(1)}, bf16[48,1920]{1,0:T(8,128)(2,1)S(1)}, u32[]{:S(2)}, u32[]{:S(2)}) collective-permute-start(bf16[48,1920]{1,0:T(8,128)(2,1)S(1)} %copy-done.5), channel_id=1, source_target_pairs={{0,40},{8,48},{16,56},{24,0},{32,8},{40,16},{48,24},{56,32},{1,41}... | collective-permute-start | bytes 552968 | tf_op jit(solution)/shard_map/ppermute | solution.py:281
  37.9 1.5 collective-permute-start
  39.4 3.8 %collective-permute-done.3.refs_3_ = bf16[48,1920]{1,0:T(8,128)(2,1)S(1)} collective-permute-done((bf16[48,1920]{1,0:T(8,128)(2,1)S(1)}, bf16[48,1920]{1,0:T(8,128)(2,1)S(1)}, u32[]{:S(2)}, u32[]{:S(2)}) %collective-permute-start.3) | collective-permute-done | bytes 184352 | tf_op jit(solution)/shard_map/ppermute | solution.py:281
  43.2 10.4 %collective-permute-done.2.refs_2_ = bf16[48,1920]{1,0:T(8,128)(2,1)S(1)} collective-permute-done((bf16[48,1920]{1,0:T(8,128)(2,1)S(1)}, bf16[48,1920]{1,0:T(8,128)(2,1)S(1)}, u32[]{:S(2)}, u32[]{:S(2)}) %collective-permute-start.2) | collective-permute-done | bytes 184352 | tf_op jit(solution)/shard_map/ppermute | solution.py:281
  53.6 7.8 %collective-permute-done.refs_0_ = bf16[48,1920]{1,0:T(8,128)(2,1)S(1)} collective-permute-done((bf16[48,1920]{1,0:T(8,128)(2,1)S(1)}, bf16[48,1920]{1,0:T(8,128)(2,1)S(1)}, u32[]{:S(2)}, u32[]{:S(2)}) %collective-permute-start) | collective-permute-done | bytes 184352 | tf_op jit(solution)/shard_map/ppermute | solution.py:281
  62.1 4.0 %dispatch.2 = (bf16[8,56,1792]{2,1,0:T(8,128)(2,1)}, bf16[192,384]{1,0:T(8,128)(2,1)}) custom-call(s32[1]{0:T(128)} %bitcast.z_ref, f32[8,384]{1,0:T(8,128)} %constant.21.clone.table_ref, bf16[48,1920]{1,0:T(8,128)(2,1)} %copy-done.24, bf16[48,1920]{1,0:T(8,128)(2,1)} %copy-done.23, bf16[48,1920]{1,0:T(8,128)(2,1)} %copy-done.22, ...), custom_call_target="tpu_custom_call" | custom-call | tf_op jit(solution)/shard_map/dispatch/pallas_call | solution.py:110
  66.1 1.1 copy-done.3
  67.2 4.4 %all-to-all-start.1 = ((bf16[8,56,1792]{2,1,0:T(8,128)(2,1)}), bf16[8,56,1792]{2,1,0:T(8,128)(2,1)S(1)}, u32[]{:S(2)}, u32[]{:S(2)}) async-start(bf16[8,56,1792]{2,1,0:T(8,128)(2,1)} %get-tuple-element.33), calls=%async_computation.1 | async-start | bytes 3211264 | tf_op jit(solution)/shard_map/all_to_all | solution.py:300
  71.6 21.9 %all-to-all-done.1.refs_1_ = bf16[8,56,1792]{2,1,0:T(8,128)(2,1)S(1)} async-done(((bf16[8,56,1792]{2,1,0:T(8,128)(2,1)}), bf16[8,56,1792]{2,1,0:T(8,128)(2,1)S(1)}, u32[]{:S(2)}, u32[]{:S(2)}) %all-to-all-start.1) | async-done | bytes 1605664 | tf_op jit(solution)/shard_map/all_to_all | solution.py:300
  93.5 1.2 copy-done
  94.7 12.9 %expert_in.1 = (bf16[96,1024]{1,0:T(8,128)(2,1)}, bf16[96,1024]{1,0:T(8,128)(2,1)}, bf16[96,1024]{1,0:T(8,128)(2,1)}, bf16[96,1024]{1,0:T(8,128)(2,1)}, bf16[96,...) custom-call(s32[1]{0:T(128)} %bitcast.1.x_ref, ...), custom_call_target="tpu_custom_call" | custom-call | tf_op jit(solution)/shard_map/expert_in/pallas_call | solution.py:221
  107.7 1.7 collective-permute-start.20
  109.4 1.7 collective-permute-start.22
  111.4 3.0 %collective-permute-start.24 = (bf16[96,1024]{1,0:T(8,128)(2,1)}, bf16[96,1024]{1,0:T(8,128)(2,1)S(1)}, u32[]{:S(2)}, u32[]{:S(2)}) collective-permute-start(bf16[96,1024]{1,0:T(8,128)(2,1)} %get-tuple-element.54), channel_id=1, source_target_pairs={{0,3},{1,0},{2,1},{3,2},{4,7},{5,4},{6,5},{7,6},{8,11},{9,8},{10,9... | collective-permute-start | bytes 589832 | tf_op jit(solution)/shard_map/ppermute | solution.py:281
  114.4 2.7 %collective-permute-done.20 = bf16[96,1024]{1,0:T(8,128)(2,1)S(1)} collective-permute-done((bf16[96,1024]{1,0:T(8,128)(2,1)}, bf16[96,1024]{1,0:T(8,128)(2,1)S(1)}, u32[]{:S(2)}, u32[]{:S(2)}) %collective-permute-start.20) | collective-permute-done | bytes 196640 | tf_op jit(solution)/shard_map/ppermute | solution.py:281
  117.1 1.0 add_convert_fusion.1
  118.5 1.4 collective-permute-done.24
  119.9 1.0 add_convert_fusion
  120.9 3.0 %collective-permute-start.25 = (bf16[96,1024]{1,0:T(8,128)(2,1)S(1)}, bf16[96,1024]{1,0:T(8,128)(2,1)S(1)}, u32[]{:S(2)}, u32[]{:S(2)}) collective-permute-start(bf16[96,1024]{1,0:T(8,128)(2,1)S(1)} %add_convert_fusion), channel_id=1, source_target_pairs={{0,3},{1,0},{2,1},{3,2},{4,7},{5,4},{6,5},{7,6},{8,11},{9,8},{10,9... | collective-permute-start | bytes 589832 | tf_op jit(solution)/shard_map/ppermute | solution.py:281
  123.9 1.1 collective-permute-done.21
  125.1 2.1 collective-permute-done.25
  127.1 1.3 multiply_convert_fusion.refs_0_
  128.4 1.1 collective-permute-start.28
  129.5 4.1 %collective-permute-start.27 = (bf16[96,1024]{1,0:T(8,128)(2,1)S(1)}, bf16[96,1024]{1,0:T(8,128)(2,1)S(1)}, u32[]{:S(2)}, u32[]{:S(2)}) collective-permute-start(bf16[96,1024]{1,0:T(8,128)(2,1)S(1)} %multiply_convert_fusion.refs_0_), channel_id=1, source_target_pairs={{0,2},{1,3},{2,0},{3,1},{4,6},{5,7},{6,4},{7,5},{8,10},{9,11},{10,... | collective-permute-start | bytes 589832 | tf_op jit(solution)/shard_map/ppermute | solution.py:281
  133.6 2.0 collective-permute-start.7
  135.6 4.8 %collective-permute-done.28.refs_3_ = bf16[96,1024]{1,0:T(8,128)(2,1)S(1)} collective-permute-done((bf16[96,1024]{1,0:T(8,128)(2,1)S(1)}, bf16[96,1024]{1,0:T(8,128)(2,1)S(1)}, u32[]{:S(2)}, u32[]{:S(2)}) %collective-permute-start.28) | collective-permute-done | bytes 196640 | tf_op jit(solution)/shard_map/ppermute | solution.py:281
  140.4 1.9 collective-permute-done.27.refs_2_
  143.1 5.0 %expert_out.3 = bf16[384,1792]{1,0:T(8,128)(2,1)} custom-call(s32[1]{0:T(128)} %bitcast.1.x_ref, bf16[1024,1792]{1,0:T(8,128)(2,1)} %bitcast.10, bf16[96,1024]{1,0:T(8,128)(2,1)} %copy-done.6, bf16[96,1024]{1,0:T(8,128)(2,1)} %copy-done.14, bf16[96,1024]{1,0:T(8,128)(2,1)} %copy-done.12, bf16[96,1024]{1,0:T(8,128)(2,1)} %copy-done.11), custom_call_target="tpu_custom_call" | custom-call | tf_op jit(solution)/shard_map/expert_out/pallas_call | solution.py:250
  148.1 3.7 %all-to-all-start.3 = ((bf16[8,48,1792]{2,1,0:T(8,128)(2,1)}), bf16[8,48,1792]{2,1,0:T(8,128)(2,1)S(1)}, u32[]{:S(2)}, u32[]{:S(2)}) async-start(bf16[8,48,1792]{2,1,0:T(8,128)(2,1)} %bitcast.13), calls=%async_computation.3 | async-start | bytes 2752512 | tf_op jit(solution)/shard_map/all_to_all | solution.py:323
  152.0 2.0 collective-permute-start.10
  154.0 1.3 collective-permute-start.11
  156.1 7.1 %collective-permute-done.11 = bf16[96,1024]{1,0:T(8,128)(2,1)S(1)} collective-permute-done((bf16[96,1024]{1,0:T(8,128)(2,1)S(1)}, bf16[96,1024]{1,0:T(8,128)(2,1)S(1)}, u32[]{:S(2)}, u32[]{:S(2)}) %collective-permute-start.11) | collective-permute-done | bytes 196640 | tf_op jit(solution)/shard_map/ppermute | solution.py:281
  163.4 1.8 collective-permute-start.12
  165.2 4.8 %collective-permute-done.12 = bf16[96,1024]{1,0:T(8,128)(2,1)S(1)} collective-permute-done((bf16[96,1024]{1,0:T(8,128)(2,1)S(1)}, bf16[96,1024]{1,0:T(8,128)(2,1)S(1)}, u32[]{:S(2)}, u32[]{:S(2)}) %collective-permute-start.12) | collective-permute-done | bytes 196640 | tf_op jit(solution)/shard_map/ppermute | solution.py:281
  170.3 4.4 %collective-permute-start.14 = (bf16[96,1024]{1,0:T(8,128)(2,1)S(1)}, bf16[96,1024]{1,0:T(8,128)(2,1)S(1)}, u32[]{:S(2)}, u32[]{:S(2)}) collective-permute-start(bf16[96,1024]{1,0:T(8,128)(2,1)S(1)} %multiply_convert_fusion.1.refs_0_), channel_id=1, source_target_pairs={{0,2},{1,3},{2,0},{3,1},{4,6},{5,7},{6,4},{7,5},{8,10},{9,11},{10,... | collective-permute-start | bytes 589832 | tf_op jit(solution)/shard_map/ppermute | solution.py:281
  174.7 3.4 %collective-permute-done.15.refs_3_ = bf16[96,1024]{1,0:T(8,128)(2,1)S(1)} collective-permute-done((bf16[96,1024]{1,0:T(8,128)(2,1)S(1)}, bf16[96,1024]{1,0:T(8,128)(2,1)S(1)}, u32[]{:S(2)}, u32[]{:S(2)}) %collective-permute-start.15) | collective-permute-done | bytes 196640 | tf_op jit(solution)/shard_map/ppermute | solution.py:281
  178.1 4.5 %collective-permute-done.14.refs_2_ = bf16[96,1024]{1,0:T(8,128)(2,1)S(1)} collective-permute-done((bf16[96,1024]{1,0:T(8,128)(2,1)S(1)}, bf16[96,1024]{1,0:T(8,128)(2,1)S(1)}, u32[]{:S(2)}, u32[]{:S(2)}) %collective-permute-start.14) | collective-permute-done | bytes 196640 | tf_op jit(solution)/shard_map/ppermute | solution.py:281
  183.9 5.0 %expert_out.2 = bf16[384,1792]{1,0:T(8,128)(2,1)} custom-call(s32[1]{0:T(128)} %bitcast.1.x_ref, bf16[1024,1792]{1,0:T(8,128)(2,1)} %bitcast.11, bf16[96,1024]{1,0:T(8,128)(2,1)} %copy-done.7, bf16[96,1024]{1,0:T(8,128)(2,1)} %copy-done.16, bf16[96,1024]{1,0:T(8,128)(2,1)} %copy-done.15, bf16[96,1024]{1,0:T(8,128)(2,1)} %copy-done.13), custom_call_target="tpu_custom_call" | custom-call | tf_op jit(solution)/shard_map/expert_out/pallas_call | solution.py:250
  188.9 1.1 copy-done.1
  190.1 4.0 %all-to-all-start.2 = ((bf16[8,48,1792]{2,1,0:T(8,128)(2,1)}), bf16[8,48,1792]{2,1,0:T(8,128)(2,1)S(1)}, u32[]{:S(2)}, u32[]{:S(2)}) async-start(bf16[8,48,1792]{2,1,0:T(8,128)(2,1)} %bitcast.15), calls=%async_computation.2 | async-start | bytes 2752512 | tf_op jit(solution)/shard_map/all_to_all | solution.py:323
  194.1 2.8 %combine.3 = (bf16[48,1792]{1,0:T(8,128)(2,1)}, bf16[48,1792]{1,0:T(8,128)(2,1)}, bf16[48,1792]{1,0:T(8,128)(2,1)}, bf16[48,1792]{1,0:T(8,128)(2,1)}) custom-call(bf16[192,384]{1,0:T(8,128)(2,1)} %get-tuple-element.46.combine_ref, bf16[384,1792]{1,0:T(8,128)(2,1)} %bitcast.12), custom_call_target="tpu_custom_call" | custom-call | tf_op jit(solution)/shard_map/combine/pallas_call | solution.py:269
  196.9 1.6 collective-permute-start.29
  198.9 3.3 %collective-permute-start.31 = (bf16[48,1792]{1,0:T(8,128)(2,1)}, bf16[48,1792]{1,0:T(8,128)(2,1)S(1)}, u32[]{:S(2)}, u32[]{:S(2)}) collective-permute-start(bf16[48,1792]{1,0:T(8,128)(2,1)} %get-tuple-element.58), channel_id=1, source_target_pairs={{0,16},{8,24},{16,32},{24,40},{32,48},{40,56},{48,0},{56,8},{1,17}... | collective-permute-start | bytes 516104 | tf_op jit(solution)/shard_map/ppermute | solution.py:281
  202.2 11.3 %all-to-all-done.2 = bf16[8,48,1792]{2,1,0:T(8,128)(2,1)S(1)} async-done(((bf16[8,48,1792]{2,1,0:T(8,128)(2,1)}), bf16[8,48,1792]{2,1,0:T(8,128)(2,1)S(1)}, u32[]{:S(2)}, u32[]{:S(2)}) %all-to-all-start.2) | async-done | bytes 1376288 | tf_op jit(solution)/shard_map/all_to_all | solution.py:323
  213.6 1.1 copy-done.2
  214.7 2.8 %combine.2 = (bf16[48,1792]{1,0:T(8,128)(2,1)}, bf16[48,1792]{1,0:T(8,128)(2,1)}, bf16[48,1792]{1,0:T(8,128)(2,1)}, bf16[48,1792]{1,0:T(8,128)(2,1)}) custom-call(bf16[192,384]{1,0:T(8,128)(2,1)} %get-tuple-element.31.combine_ref, bf16[384,1792]{1,0:T(8,128)(2,1)} %bitcast.14), custom_call_target="tpu_custom_call" | custom-call | tf_op jit(solution)/shard_map/combine/pallas_call | solution.py:269
  217.5 3.4 %collective-permute-start.16 = (bf16[48,1792]{1,0:T(8,128)(2,1)}, bf16[48,1792]{1,0:T(8,128)(2,1)S(1)}, u32[]{:S(2)}, u32[]{:S(2)}) collective-permute-start(bf16[48,1792]{1,0:T(8,128)(2,1)} %get-tuple-element.42), channel_id=1, source_target_pairs={{0,48},{8,56},{16,0},{24,8},{32,16},{40,24},{48,32},{56,40},{1,49}... | collective-permute-start | bytes 516104 | tf_op jit(solution)/shard_map/ppermute | solution.py:281
  220.8 1.8 collective-permute-start.17
  222.6 3.3 %collective-permute-start.18 = (bf16[48,1792]{1,0:T(8,128)(2,1)}, bf16[48,1792]{1,0:T(8,128)(2,1)S(1)}, u32[]{:S(2)}, u32[]{:S(2)}) collective-permute-start(bf16[48,1792]{1,0:T(8,128)(2,1)} %get-tuple-element.44), channel_id=1, source_target_pairs={{0,40},{8,48},{16,56},{24,0},{32,8},{40,16},{48,24},{56,32},{1,41}... | collective-permute-start | bytes 516104 | tf_op jit(solution)/shard_map/ppermute | solution.py:281
  225.9 2.6 %collective-permute-start.19 = (bf16[48,1792]{1,0:T(8,128)(2,1)}, bf16[48,1792]{1,0:T(8,128)(2,1)S(1)}, u32[]{:S(2)}, u32[]{:S(2)}) collective-permute-start(bf16[48,1792]{1,0:T(8,128)(2,1)} %get-tuple-element.45), channel_id=1, source_target_pairs={{0,32},{8,40},{16,48},{24,56},{32,0},{40,8},{48,16},{56,24},{1,33}... | collective-permute-start | bytes 516104 | tf_op jit(solution)/shard_map/ppermute | solution.py:281
  228.5 1.2 slice.3
  230.3 3.4 %collective-permute-done.16 = bf16[48,1792]{1,0:T(8,128)(2,1)S(1)} collective-permute-done((bf16[48,1792]{1,0:T(8,128)(2,1)}, bf16[48,1792]{1,0:T(8,128)(2,1)S(1)}, u32[]{:S(2)}, u32[]{:S(2)}) %collective-permute-start.16) | collective-permute-done | bytes 172064 | tf_op jit(solution)/shard_map/ppermute | solution.py:281
  233.7 2.9 %collective-permute-done.17 = bf16[48,1792]{1,0:T(8,128)(2,1)S(1)} collective-permute-done((bf16[48,1792]{1,0:T(8,128)(2,1)}, bf16[48,1792]{1,0:T(8,128)(2,1)S(1)}, u32[]{:S(2)}, u32[]{:S(2)}) %collective-permute-start.17) | collective-permute-done | bytes 172064 | tf_op jit(solution)/shard_map/ppermute | solution.py:281
  236.6 4.3 %collective-permute-done.18 = bf16[48,1792]{1,0:T(8,128)(2,1)S(1)} collective-permute-done((bf16[48,1792]{1,0:T(8,128)(2,1)}, bf16[48,1792]{1,0:T(8,128)(2,1)S(1)}, u32[]{:S(2)}, u32[]{:S(2)}) %collective-permute-start.18) | collective-permute-done | bytes 172064 | tf_op jit(solution)/shard_map/ppermute | solution.py:281
  240.9 8.7 %collective-permute-done.19 = bf16[48,1792]{1,0:T(8,128)(2,1)S(1)} collective-permute-done((bf16[48,1792]{1,0:T(8,128)(2,1)}, bf16[48,1792]{1,0:T(8,128)(2,1)S(1)}, u32[]{:S(2)}, u32[]{:S(2)}) %collective-permute-start.19) | collective-permute-done | bytes 172064 | tf_op jit(solution)/shard_map/ppermute | solution.py:281
  (87 shorter events, 8.3 us)
Async XLA Ops:
  3.0 15.8 %copy-start.4 = (bf16[48,1920]{1,0:T(8,128)(2,1)}, bf16[48,1920]{1,0:T(8,128)(2,1)S(1)}, u32[]{:S(2)}) copy-start(bf16[48,1920]{1,0:T(8,128)(2,1)S(1)} %fusion.1.refs_4_.refs_0_) | copy-start | bytes 552964
  3.1 12.3 %collective-permute-start.6 = (bf16[48,1920]{1,0:T(8,128)(2,1)S(1)}, bf16[48,1920]{1,0:T(8,128)(2,1)S(1)}, u32[]{:S(2)}, u32[]{:S(2)}) collective-permute-start(bf16[48,1920]{1,0:T(8,128)(2,1)S(1)} %fusion.1.refs_4_.refs_0_), channel_id=1, source_target_pairs={{0,48},{8,56},{16,0},{24,8},{32,16},{40,24},{48,32},{56,40},{1,49}... | collective-permute-start | bytes 552968 | tf_op jit(solution)/shard_map/ppermute | solution.py:281
  8.5 6.8 %collective-permute-start.5 = (bf16[48,1920]{1,0:T(8,128)(2,1)S(1)}, bf16[48,1920]{1,0:T(8,128)(2,1)S(1)}, u32[]{:S(2)}, u32[]{:S(2)}) collective-permute-start(bf16[48,1920]{1,0:T(8,128)(2,1)S(1)} %fusion.1.refs_4_.refs_0_), channel_id=1, source_target_pairs={{0,8},{8,16},{16,24},{24,32},{32,40},{40,48},{48,56},{56,0},{1,9},... | collective-permute-start | bytes 552968 | tf_op jit(solution)/shard_map/ppermute | solution.py:281
  8.5 10.3 %collective-permute-start.4 = (bf16[48,1920]{1,0:T(8,128)(2,1)S(1)}, bf16[48,1920]{1,0:T(8,128)(2,1)S(1)}, u32[]{:S(2)}, u32[]{:S(2)}) collective-permute-start(bf16[48,1920]{1,0:T(8,128)(2,1)S(1)} %fusion.1.refs_4_.refs_0_), channel_id=1, source_target_pairs={{0,56},{8,0},{16,8},{24,16},{32,24},{40,32},{48,40},{56,48},{1,57}... | collective-permute-start | bytes 552968 | tf_op jit(solution)/shard_map/ppermute | solution.py:281
  15.3 3.5 %copy-start.8 = (bf16[48,1920]{1,0:T(8,128)(2,1)}, bf16[48,1920]{1,0:T(8,128)(2,1)S(1)}, u32[]{:S(2)}) copy-start(bf16[48,1920]{1,0:T(8,128)(2,1)S(1)} %collective-permute-done.6.refs_7_.refs_3_) | copy-start | bytes 552964
  15.3 3.5 %copy-start.9 = (bf16[48,1920]{1,0:T(8,128)(2,1)}, bf16[48,1920]{1,0:T(8,128)(2,1)S(1)}, u32[]{:S(2)}) copy-start(bf16[48,1920]{1,0:T(8,128)(2,1)S(1)} %collective-permute-done.5.refs_6_.refs_2_) | copy-start | bytes 552964
  22.9 4.6 %copy-start.5 = (bf16[48,1920]{1,0:T(8,128)(2,1)S(1)}, bf16[48,1920]{1,0:T(8,128)(2,1)}, u32[]{:S(2)}) copy-start(bf16[48,1920]{1,0:T(8,128)(2,1)} %copy-done.4) | copy-start | bytes 552964
  22.9 43.2 %all-to-all-start = ((bf16[8,48,1792]{2,1,0:T(8,128)(2,1)}), bf16[8,48,1792]{2,1,0:T(8,128)(2,1)S(1)}, u32[]{:S(2)}, u32[]{:S(2)}) async-start(bf16[8,48,1792]{2,1,0:T(8,128)(2,1)} %get-tuple-element.32), calls=%async_computation | async-start | bytes 2752512 | tf_op jit(solution)/shard_map/all_to_all | solution.py:300
  27.6 15.7 %collective-permute-start.3 = (bf16[48,1920]{1,0:T(8,128)(2,1)S(1)}, bf16[48,1920]{1,0:T(8,128)(2,1)S(1)}, u32[]{:S(2)}, u32[]{:S(2)}) collective-permute-start(bf16[48,1920]{1,0:T(8,128)(2,1)S(1)} %copy-done.5), channel_id=1, source_target_pairs={{0,32},{8,40},{16,48},{24,56},{32,0},{40,8},{48,16},{56,24},{1,33}... | collective-permute-start | bytes 552968 | tf_op jit(solution)/shard_map/ppermute | solution.py:281
  32.9 20.7 %collective-permute-start.2 = (bf16[48,1920]{1,0:T(8,128)(2,1)S(1)}, bf16[48,1920]{1,0:T(8,128)(2,1)S(1)}, u32[]{:S(2)}, u32[]{:S(2)}) collective-permute-start(bf16[48,1920]{1,0:T(8,128)(2,1)S(1)} %copy-done.5), channel_id=1, source_target_pairs={{0,24},{8,32},{16,40},{24,48},{32,56},{40,0},{48,8},{56,16},{1,25}... | collective-permute-start | bytes 552968 | tf_op jit(solution)/shard_map/ppermute | solution.py:281
  34.6 19.0 %collective-permute-start.1 = (bf16[48,1920]{1,0:T(8,128)(2,1)S(1)}, bf16[48,1920]{1,0:T(8,128)(2,1)S(1)}, u32[]{:S(2)}, u32[]{:S(2)}) collective-permute-start(bf16[48,1920]{1,0:T(8,128)(2,1)S(1)} %copy-done.5), channel_id=1, source_target_pairs={{0,40},{8,48},{16,56},{24,0},{32,8},{40,16},{48,24},{56,32},{1,41}... | collective-permute-start | bytes 552968 | tf_op jit(solution)/shard_map/ppermute | solution.py:281
  37.9 23.5 %collective-permute-start = (bf16[48,1920]{1,0:T(8,128)(2,1)S(1)}, bf16[48,1920]{1,0:T(8,128)(2,1)S(1)}, u32[]{:S(2)}, u32[]{:S(2)}) collective-permute-start(bf16[48,1920]{1,0:T(8,128)(2,1)S(1)} %copy-done.5), channel_id=1, source_target_pairs={{0,16},{8,24},{16,32},{24,40},{32,48},{40,56},{48,0},{56,8},{1,17}... | collective-permute-start | bytes 552968 | tf_op jit(solution)/shard_map/ppermute | solution.py:281
  43.2 18.2 %copy-start.21 = (bf16[48,1920]{1,0:T(8,128)(2,1)}, bf16[48,1920]{1,0:T(8,128)(2,1)S(1)}, u32[]{:S(2)}) copy-start(bf16[48,1920]{1,0:T(8,128)(2,1)S(1)} %collective-permute-done.3.refs_3_) | copy-start | bytes 552964
  53.6 7.8 %copy-start.22 = (bf16[48,1920]{1,0:T(8,128)(2,1)}, bf16[48,1920]{1,0:T(8,128)(2,1)S(1)}, u32[]{:S(2)}) copy-start(bf16[48,1920]{1,0:T(8,128)(2,1)S(1)} %collective-permute-done.2.refs_2_) | copy-start | bytes 552964
  53.6 7.8 %copy-start.23 = (bf16[48,1920]{1,0:T(8,128)(2,1)}, bf16[48,1920]{1,0:T(8,128)(2,1)S(1)}, u32[]{:S(2)}) copy-start(bf16[48,1920]{1,0:T(8,128)(2,1)S(1)} %collective-permute-done.1.refs_1_) | copy-start | bytes 552964
  61.4 0.7 copy-start.24
  66.1 1.1 copy-start.3
  67.2 26.3 %all-to-all-start.1 = ((bf16[8,56,1792]{2,1,0:T(8,128)(2,1)}), bf16[8,56,1792]{2,1,0:T(8,128)(2,1)S(1)}, u32[]{:S(2)}, u32[]{:S(2)}) async-start(bf16[8,56,1792]{2,1,0:T(8,128)(2,1)} %get-tuple-element.33), calls=%async_computation.1 | async-start | bytes 3211264 | tf_op jit(solution)/shard_map/all_to_all | solution.py:300
  93.5 1.2 copy-start
  107.7 26.0 %copy-start.29 = (bf16[96,1024]{1,0:T(8,128)(2,1)S(1)}, bf16[96,1024]{1,0:T(8,128)(2,1)}, u32[]{:S(2)}) copy-start(bf16[96,1024]{1,0:T(8,128)(2,1)} %get-tuple-element.36) | copy-start | bytes 589828
  107.7 9.5 %collective-permute-start.20 = (bf16[96,1024]{1,0:T(8,128)(2,1)}, bf16[96,1024]{1,0:T(8,128)(2,1)S(1)}, u32[]{:S(2)}, u32[]{:S(2)}) collective-permute-start(bf16[96,1024]{1,0:T(8,128)(2,1)} %get-tuple-element.49), channel_id=1, source_target_pairs={{0,1},{1,2},{2,3},{3,0},{4,5},{5,6},{6,7},{7,4},{8,9},{9,10},{10,1... | collective-permute-start | bytes 589832 | tf_op jit(solution)/shard_map/ppermute | solution.py:281
  109.4 14.5 %collective-permute-start.22 = (bf16[96,1024]{1,0:T(8,128)(2,1)}, bf16[96,1024]{1,0:T(8,128)(2,1)S(1)}, u32[]{:S(2)}, u32[]{:S(2)}) collective-permute-start(bf16[96,1024]{1,0:T(8,128)(2,1)} %get-tuple-element.50), channel_id=1, source_target_pairs={{0,3},{1,0},{2,1},{3,2},{4,7},{5,4},{6,5},{7,6},{8,11},{9,8},{10,9... | collective-permute-start | bytes 589832 | tf_op jit(solution)/shard_map/ppermute | solution.py:281
  111.2 12.8 %collective-permute-start.23 = (bf16[96,1024]{1,0:T(8,128)(2,1)}, bf16[96,1024]{1,0:T(8,128)(2,1)S(1)}, u32[]{:S(2)}, u32[]{:S(2)}) collective-permute-start(bf16[96,1024]{1,0:T(8,128)(2,1)} %get-tuple-element.52), channel_id=1, source_target_pairs={{0,1},{1,2},{2,3},{3,0},{4,5},{5,6},{6,7},{7,4},{8,9},{9,10},{10,1... | collective-permute-start | bytes 589832 | tf_op jit(solution)/shard_map/ppermute | solution.py:281
  111.4 8.5 %collective-permute-start.24 = (bf16[96,1024]{1,0:T(8,128)(2,1)}, bf16[96,1024]{1,0:T(8,128)(2,1)S(1)}, u32[]{:S(2)}, u32[]{:S(2)}) collective-permute-start(bf16[96,1024]{1,0:T(8,128)(2,1)} %get-tuple-element.54), channel_id=1, source_target_pairs={{0,3},{1,0},{2,1},{3,2},{4,7},{5,4},{6,5},{7,6},{8,11},{9,8},{10,9... | collective-permute-start | bytes 589832 | tf_op jit(solution)/shard_map/ppermute | solution.py:281
  118.1 7.0 %collective-permute-start.21 = (bf16[96,1024]{1,0:T(8,128)(2,1)S(1)}, bf16[96,1024]{1,0:T(8,128)(2,1)S(1)}, u32[]{:S(2)}, u32[]{:S(2)}) collective-permute-start(bf16[96,1024]{1,0:T(8,128)(2,1)S(1)} %add_convert_fusion.1), channel_id=1, source_target_pairs={{0,1},{1,2},{2,3},{3,0},{4,5},{5,6},{6,7},{7,4},{8,9},{9,10},{10,1... | collective-permute-start | bytes 589832 | tf_op jit(solution)/shard_map/ppermute | solution.py:281
  120.9 6.2 %collective-permute-start.25 = (bf16[96,1024]{1,0:T(8,128)(2,1)S(1)}, bf16[96,1024]{1,0:T(8,128)(2,1)S(1)}, u32[]{:S(2)}, u32[]{:S(2)}) collective-permute-start(bf16[96,1024]{1,0:T(8,128)(2,1)S(1)} %add_convert_fusion), channel_id=1, source_target_pairs={{0,3},{1,0},{2,1},{3,2},{4,7},{5,4},{6,5},{7,6},{8,11},{9,8},{10,9... | collective-permute-start | bytes 589832 | tf_op jit(solution)/shard_map/ppermute | solution.py:281
  128.4 13.9 %copy-start.6 = (bf16[96,1024]{1,0:T(8,128)(2,1)}, bf16[96,1024]{1,0:T(8,128)(2,1)S(1)}, u32[]{:S(2)}) copy-start(bf16[96,1024]{1,0:T(8,128)(2,1)S(1)} %multiply_convert_fusion.refs_0_) | copy-start | bytes 589828
  128.4 12.0 %collective-permute-start.28 = (bf16[96,1024]{1,0:T(8,128)(2,1)S(1)}, bf16[96,1024]{1,0:T(8,128)(2,1)S(1)}, u32[]{:S(2)}, u32[]{:S(2)}) collective-permute-start(bf16[96,1024]{1,0:T(8,128)(2,1)S(1)} %multiply_convert_fusion.refs_0_), channel_id=1, source_target_pairs={{0,1},{1,2},{2,3},{3,0},{4,5},{5,6},{6,7},{7,4},{8,9},{9,10},{10,1... | collective-permute-start | bytes 589832 | tf_op jit(solution)/shard_map/ppermute | solution.py:281
  129.5 12.8 %collective-permute-start.27 = (bf16[96,1024]{1,0:T(8,128)(2,1)S(1)}, bf16[96,1024]{1,0:T(8,128)(2,1)S(1)}, u32[]{:S(2)}, u32[]{:S(2)}) collective-permute-start(bf16[96,1024]{1,0:T(8,128)(2,1)S(1)} %multiply_convert_fusion.refs_0_), channel_id=1, source_target_pairs={{0,2},{1,3},{2,0},{3,1},{4,6},{5,7},{6,4},{7,5},{8,10},{9,11},{10,... | collective-permute-start | bytes 589832 | tf_op jit(solution)/shard_map/ppermute | solution.py:281
  133.6 8.7 %collective-permute-start.26 = (bf16[96,1024]{1,0:T(8,128)(2,1)S(1)}, bf16[96,1024]{1,0:T(8,128)(2,1)S(1)}, u32[]{:S(2)}, u32[]{:S(2)}) collective-permute-start(bf16[96,1024]{1,0:T(8,128)(2,1)S(1)} %multiply_convert_fusion.refs_0_), channel_id=1, source_target_pairs={{0,3},{1,0},{2,1},{3,2},{4,7},{5,4},{6,5},{7,6},{8,11},{9,8},{10,9... | collective-permute-start | bytes 589832 | tf_op jit(solution)/shard_map/ppermute | solution.py:281
  133.6 21.7 %collective-permute-start.7 = (bf16[96,1024]{1,0:T(8,128)(2,1)S(1)}, bf16[96,1024]{1,0:T(8,128)(2,1)S(1)}, u32[]{:S(2)}, u32[]{:S(2)}) collective-permute-start(bf16[96,1024]{1,0:T(8,128)(2,1)S(1)} %copy-done.29), channel_id=1, source_target_pairs={{0,1},{1,2},{2,3},{3,0},{4,5},{5,6},{6,7},{7,4},{8,9},{9,10},{10,1... | collective-permute-start | bytes 589832 | tf_op jit(solution)/shard_map/ppermute | solution.py:281
  140.4 1.9 copy-start.11
  142.3 0.7 copy-start.12
  142.3 0.8 copy-start.14
  148.1 3.8 %copy-start.27 = (bf16[96,1024]{1,0:T(8,128)(2,1)S(1)}, bf16[96,1024]{1,0:T(8,128)(2,1)}, u32[]{:S(2)}) copy-start(bf16[96,1024]{1,0:T(8,128)(2,1)} %get-tuple-element.37) | copy-start | bytes 589828
  148.1 3.9 %copy-start.26 = (bf16[96,1024]{1,0:T(8,128)(2,1)S(1)}, bf16[96,1024]{1,0:T(8,128)(2,1)}, u32[]{:S(2)}) copy-start(bf16[96,1024]{1,0:T(8,128)(2,1)} %get-tuple-element.39) | copy-start | bytes 589828
  148.1 5.9 %copy-start.28 = (bf16[96,1024]{1,0:T(8,128)(2,1)S(1)}, bf16[96,1024]{1,0:T(8,128)(2,1)}, u32[]{:S(2)}) copy-start(bf16[96,1024]{1,0:T(8,128)(2,1)} %get-tuple-element.41) | copy-start | bytes 589828
  148.1 7.2 %copy-start.18 = (bf16[96,1024]{1,0:T(8,128)(2,1)S(1)}, bf16[96,1024]{1,0:T(8,128)(2,1)}, u32[]{:S(2)}) copy-start(bf16[96,1024]{1,0:T(8,128)(2,1)} %get-tuple-element.35) | copy-start | bytes 589828
  148.1 15.2 %copy-start.17 = (bf16[96,1024]{1,0:T(8,128)(2,1)S(1)}, bf16[96,1024]{1,0:T(8,128)(2,1)}, u32[]{:S(2)}) copy-start(bf16[96,1024]{1,0:T(8,128)(2,1)} %get-tuple-element.40) | copy-start | bytes 589828
  148.1 21.8 %copy-start.19 = (bf16[96,1024]{1,0:T(8,128)(2,1)S(1)}, bf16[96,1024]{1,0:T(8,128)(2,1)}, u32[]{:S(2)}) copy-start(bf16[96,1024]{1,0:T(8,128)(2,1)} %get-tuple-element.34) | copy-start | bytes 589828
  148.1 21.8 %copy-start.20 = (bf16[96,1024]{1,0:T(8,128)(2,1)S(1)}, bf16[96,1024]{1,0:T(8,128)(2,1)}, u32[]{:S(2)}) copy-start(bf16[96,1024]{1,0:T(8,128)(2,1)} %get-tuple-element.38) | copy-start | bytes 589828
  148.1 40.8 %all-to-all-start.3 = ((bf16[8,48,1792]{2,1,0:T(8,128)(2,1)}), bf16[8,48,1792]{2,1,0:T(8,128)(2,1)S(1)}, u32[]{:S(2)}, u32[]{:S(2)}) async-start(bf16[8,48,1792]{2,1,0:T(8,128)(2,1)} %bitcast.13), calls=%async_computation.3 | async-start | bytes 2752512 | tf_op jit(solution)/shard_map/all_to_all | solution.py:323
  151.9 13.3 %collective-permute-start.9 = (bf16[96,1024]{1,0:T(8,128)(2,1)S(1)}, bf16[96,1024]{1,0:T(8,128)(2,1)S(1)}, u32[]{:S(2)}, u32[]{:S(2)}) collective-permute-start(bf16[96,1024]{1,0:T(8,128)(2,1)S(1)} %copy-done.27), channel_id=1, source_target_pairs={{0,3},{1,0},{2,1},{3,2},{4,7},{5,4},{6,5},{7,6},{8,11},{9,8},{10,9... | collective-permute-start | bytes 589832 | tf_op jit(solution)/shard_map/ppermute | solution.py:281
  152.0 13.2 %collective-permute-start.10 = (bf16[96,1024]{1,0:T(8,128)(2,1)S(1)}, bf16[96,1024]{1,0:T(8,128)(2,1)S(1)}, u32[]{:S(2)}, u32[]{:S(2)}) collective-permute-start(bf16[96,1024]{1,0:T(8,128)(2,1)S(1)} %copy-done.26), channel_id=1, source_target_pairs={{0,1},{1,2},{2,3},{3,0},{4,5},{5,6},{6,7},{7,4},{8,9},{9,10},{10,1... | collective-permute-start | bytes 589832 | tf_op jit(solution)/shard_map/ppermute | solution.py:281
  154.0 9.3 %collective-permute-start.11 = (bf16[96,1024]{1,0:T(8,128)(2,1)S(1)}, bf16[96,1024]{1,0:T(8,128)(2,1)S(1)}, u32[]{:S(2)}, u32[]{:S(2)}) collective-permute-start(bf16[96,1024]{1,0:T(8,128)(2,1)S(1)} %copy-done.28), channel_id=1, source_target_pairs={{0,3},{1,0},{2,1},{3,2},{4,7},{5,4},{6,5},{7,6},{8,11},{9,8},{10,9... | collective-permute-start | bytes 589832 | tf_op jit(solution)/shard_map/ppermute | solution.py:281
  155.4 9.8 %collective-permute-start.8 = (bf16[96,1024]{1,0:T(8,128)(2,1)S(1)}, bf16[96,1024]{1,0:T(8,128)(2,1)S(1)}, u32[]{:S(2)}, u32[]{:S(2)}) collective-permute-start(bf16[96,1024]{1,0:T(8,128)(2,1)S(1)} %add_convert_fusion.3), channel_id=1, source_target_pairs={{0,1},{1,2},{2,3},{3,0},{4,5},{5,6},{6,7},{7,4},{8,9},{9,10},{10,1... | collective-permute-start | bytes 589832 | tf_op jit(solution)/shard_map/ppermute | solution.py:281
  163.4 6.6 %collective-permute-start.12 = (bf16[96,1024]{1,0:T(8,128)(2,1)S(1)}, bf16[96,1024]{1,0:T(8,128)(2,1)S(1)}, u32[]{:S(2)}, u32[]{:S(2)}) collective-permute-start(bf16[96,1024]{1,0:T(8,128)(2,1)S(1)} %add_convert_fusion.2), channel_id=1, source_target_pairs={{0,3},{1,0},{2,1},{3,2},{4,7},{5,4},{6,5},{7,6},{8,11},{9,8},{10,9... | collective-permute-start | bytes 589832 | tf_op jit(solution)/shard_map/ppermute | solution.py:281
  170.2 12.4 %copy-start.7 = (bf16[96,1024]{1,0:T(8,128)(2,1)}, bf16[96,1024]{1,0:T(8,128)(2,1)S(1)}, u32[]{:S(2)}) copy-start(bf16[96,1024]{1,0:T(8,128)(2,1)S(1)} %multiply_convert_fusion.1.refs_0_) | copy-start | bytes 589828
  170.2 7.9 %collective-permute-start.15 = (bf16[96,1024]{1,0:T(8,128)(2,1)S(1)}, bf16[96,1024]{1,0:T(8,128)(2,1)S(1)}, u32[]{:S(2)}, u32[]{:S(2)}) collective-permute-start(bf16[96,1024]{1,0:T(8,128)(2,1)S(1)} %multiply_convert_fusion.1.refs_0_), channel_id=1, source_target_pairs={{0,1},{1,2},{2,3},{3,0},{4,5},{5,6},{6,7},{7,4},{8,9},{9,10},{10,1... | collective-permute-start | bytes 589832 | tf_op jit(solution)/shard_map/ppermute | solution.py:281
  170.3 12.3 %collective-permute-start.14 = (bf16[96,1024]{1,0:T(8,128)(2,1)S(1)}, bf16[96,1024]{1,0:T(8,128)(2,1)S(1)}, u32[]{:S(2)}, u32[]{:S(2)}) collective-permute-start(bf16[96,1024]{1,0:T(8,128)(2,1)S(1)} %multiply_convert_fusion.1.refs_0_), channel_id=1, source_target_pairs={{0,2},{1,3},{2,0},{3,1},{4,6},{5,7},{6,4},{7,5},{8,10},{9,11},{10,... | collective-permute-start | bytes 589832 | tf_op jit(solution)/shard_map/ppermute | solution.py:281
  174.7 7.9 %collective-permute-start.13 = (bf16[96,1024]{1,0:T(8,128)(2,1)S(1)}, bf16[96,1024]{1,0:T(8,128)(2,1)S(1)}, u32[]{:S(2)}, u32[]{:S(2)}) collective-permute-start(bf16[96,1024]{1,0:T(8,128)(2,1)S(1)} %multiply_convert_fusion.1.refs_0_), channel_id=1, source_target_pairs={{0,3},{1,0},{2,1},{3,2},{4,7},{5,4},{6,5},{7,6},{8,11},{9,8},{10,9... | collective-permute-start | bytes 589832 | tf_op jit(solution)/shard_map/ppermute | solution.py:281
  178.1 4.5 %copy-start.13 = (bf16[96,1024]{1,0:T(8,128)(2,1)}, bf16[96,1024]{1,0:T(8,128)(2,1)S(1)}, u32[]{:S(2)}) copy-start(bf16[96,1024]{1,0:T(8,128)(2,1)S(1)} %collective-permute-done.15.refs_3_) | copy-start | bytes 589828
  182.6 0.7 copy-start.15
  188.9 1.1 copy-start.1
  190.1 23.5 %all-to-all-start.2 = ((bf16[8,48,1792]{2,1,0:T(8,128)(2,1)}), bf16[8,48,1792]{2,1,0:T(8,128)(2,1)S(1)}, u32[]{:S(2)}, u32[]{:S(2)}) async-start(bf16[8,48,1792]{2,1,0:T(8,128)(2,1)} %bitcast.15), calls=%async_computation.2 | async-start | bytes 2752512 | tf_op jit(solution)/shard_map/all_to_all | solution.py:323
  196.9 52.8 %copy-start.25 = (bf16[48,1792]{1,0:T(8,128)(2,1)S(1)}, bf16[48,1792]{1,0:T(8,128)(2,1)}, u32[]{:S(2)}) copy-start(bf16[48,1792]{1,0:T(8,128)(2,1)} %get-tuple-element.55) | copy-start | bytes 516100
  196.9 25.7 %collective-permute-start.29 = (bf16[48,1792]{1,0:T(8,128)(2,1)}, bf16[48,1792]{1,0:T(8,128)(2,1)S(1)}, u32[]{:S(2)}, u32[]{:S(2)}) collective-permute-start(bf16[48,1792]{1,0:T(8,128)(2,1)} %get-tuple-element.56), channel_id=1, source_target_pairs={{0,8},{8,16},{16,24},{24,32},{32,40},{40,48},{48,56},{56,0},{1,9},... | collective-permute-start | bytes 516104 | tf_op jit(solution)/shard_map/ppermute | solution.py:281
  198.4 27.4 %collective-permute-start.30 = (bf16[48,1792]{1,0:T(8,128)(2,1)}, bf16[48,1792]{1,0:T(8,128)(2,1)S(1)}, u32[]{:S(2)}, u32[]{:S(2)}) collective-permute-start(bf16[48,1792]{1,0:T(8,128)(2,1)} %get-tuple-element.57), channel_id=1, source_target_pairs={{0,56},{8,0},{16,8},{24,16},{32,24},{40,32},{48,40},{56,48},{1,57}... | collective-permute-start | bytes 516104 | tf_op jit(solution)/shard_map/ppermute | solution.py:281
  198.9 31.4 %collective-permute-start.31 = (bf16[48,1792]{1,0:T(8,128)(2,1)}, bf16[48,1792]{1,0:T(8,128)(2,1)S(1)}, u32[]{:S(2)}, u32[]{:S(2)}) collective-permute-start(bf16[48,1792]{1,0:T(8,128)(2,1)} %get-tuple-element.58), channel_id=1, source_target_pairs={{0,16},{8,24},{16,32},{24,40},{32,48},{40,56},{48,0},{56,8},{1,17}... | collective-permute-start | bytes 516104 | tf_op jit(solution)/shard_map/ppermute | solution.py:281
  213.6 1.1 copy-start.2
  217.5 16.2 %collective-permute-start.16 = (bf16[48,1792]{1,0:T(8,128)(2,1)}, bf16[48,1792]{1,0:T(8,128)(2,1)S(1)}, u32[]{:S(2)}, u32[]{:S(2)}) collective-permute-start(bf16[48,1792]{1,0:T(8,128)(2,1)} %get-tuple-element.42), channel_id=1, source_target_pairs={{0,48},{8,56},{16,0},{24,8},{32,16},{40,24},{48,32},{56,40},{1,49}... | collective-permute-start | bytes 516104 | tf_op jit(solution)/shard_map/ppermute | solution.py:281
  220.8 15.8 %collective-permute-start.17 = (bf16[48,1792]{1,0:T(8,128)(2,1)}, bf16[48,1792]{1,0:T(8,128)(2,1)S(1)}, u32[]{:S(2)}, u32[]{:S(2)}) collective-permute-start(bf16[48,1792]{1,0:T(8,128)(2,1)} %get-tuple-element.43), channel_id=1, source_target_pairs={{0,24},{8,32},{16,40},{24,48},{32,56},{40,0},{48,8},{56,16},{1,25}... | collective-permute-start | bytes 516104 | tf_op jit(solution)/shard_map/ppermute | solution.py:281
  222.6 18.3 %collective-permute-start.18 = (bf16[48,1792]{1,0:T(8,128)(2,1)}, bf16[48,1792]{1,0:T(8,128)(2,1)S(1)}, u32[]{:S(2)}, u32[]{:S(2)}) collective-permute-start(bf16[48,1792]{1,0:T(8,128)(2,1)} %get-tuple-element.44), channel_id=1, source_target_pairs={{0,40},{8,48},{16,56},{24,0},{32,8},{40,16},{48,24},{56,32},{1,41}... | collective-permute-start | bytes 516104 | tf_op jit(solution)/shard_map/ppermute | solution.py:281
  225.9 23.8 %collective-permute-start.19 = (bf16[48,1792]{1,0:T(8,128)(2,1)}, bf16[48,1792]{1,0:T(8,128)(2,1)S(1)}, u32[]{:S(2)}, u32[]{:S(2)}) collective-permute-start(bf16[48,1792]{1,0:T(8,128)(2,1)} %get-tuple-element.45), channel_id=1, source_target_pairs={{0,32},{8,40},{16,48},{24,56},{32,0},{40,8},{48,16},{56,24},{1,33}... | collective-permute-start | bytes 516104 | tf_op jit(solution)/shard_map/ppermute | solution.py:281
  (2 other events, 1.3 us)
where the time goes:
time: 252 us
  waiting for transfers between devices  117 us (46%)
  starting transfers between devices  80.4 us (32%)
  Pallas kernels  35.9 us (14%)
  local copies, waits for them, and re-layouts  9.28 us (4%)
  other arithmetic  6.72 us (3%)
  between operations  2.67 us (1%)
    ppermute x32, waiting for transfers between devices, ring(): lax.ppermute(value, axis, [(i, (i + shift) % size) for i in range(size)])  83.4 us
    ppermute x32, starting transfers between devices, ring(): lax.ppermute(value, axis, [(i, (i + shift) % size) for i in range(size)])  63.6 us
    all_to_all x2, waiting for transfers between devices, body(): arrived.append(lax.all_to_all(rows, OWNERS, 0, 0, tiled=True))  21.9 us
    pallas_call x1, Pallas kernels, expert_in(): pl.pallas_call(functools.partial(expert_kernel, spans), in_specs=[whole(S...  12.9 us
    all_to_all x2, waiting for transfers between devices, body(): back = lax.all_to_all(result, OWNERS, 0, 0, tiled=True).reshape(-1, width)  11.3 us
    pallas_call x2, Pallas kernels, expert_out(): pl.pallas_call(down_kernel, in_specs=[whole(SMEM)] + [whole()] * (1 + NX)...  10.1 us
    all_to_all x2, starting transfers between devices, body(): arrived.append(lax.all_to_all(rows, OWNERS, 0, 0, tiled=True))  9.02 us
    unnamed x60, local copies, waits for them, and re-layouts  8 us
  transfers between devices with their start and end apart: 36, of which 21 were waited for; matrix products, arithmetic and copies ran while one was open for 1% of the time, Pallas kernels for 8%

commit v1 on v0

v1 whole, which is shorter than its diff:
```python
import functools

import jax
import jax.numpy as jnp
import numpy as np
from jax import lax
from jax.experimental import pallas as pl
from jax.experimental.pallas import tpu as pltpu
from jax.sharding import Mesh
from jax.sharding import PartitionSpec as P


FINE = 8
CLIP_PARTS = 8
CAP = 12
META = 128
NY, NZ, NC, NX = 4, 8, 2, 4
PEERS = NY * NC
EXPERT = ("y", "z", "c")
OWNERS = ("y", "c")
NEAR = ((0, 1), (7, 2))
FAR = ((6, 3), (5, 4))
PAIR = 2
SPAN = CAP * PAIR
LANES = PEERS * SPAN
HALF = SPAN * PAIR
ROWS = PEERS * HALF
SHARE = ROWS // NX
STRIP = 256
WIDE = 512

BF = jnp.bfloat16
F32 = jnp.float32
VMEM = pltpu.VMEM
SMEM = pltpu.SMEM


def whole(space=VMEM):
    return pl.BlockSpec(memory_space=space)


def shape_of(*shape):
    return jax.ShapeDtypeStruct(shape, BF)


def lane_table():
    lane = np.arange(LANES)
    table = np.zeros((8, LANES), np.float32)
    table[0] = lane // SPAN // NC
    table[1] = lane // SPAN % NC
    table[2] = lane % SPAN // CAP
    table[3] = lane % CAP
    return table


def peer(place, k, sign):
    dy, dc = k // NC, k % NC
    core = place[3] if dc == 0 else 1 - place[3]
    return lax.rem(place[1] + sign * dy + NY, NY) * NC + core


def dispatch_kernel(relative, place_ref, table_ref, *refs):
    tok = refs[0].shape[0]
    width = refs[0].shape[1] - META
    blocks = refs[: 2 * PAIR]
    extra = refs[2 * PAIR : 2 * PAIR + (2 * PAIR if relative else 0)]
    outs = refs[len(blocks) + len(extra) :]
    rows_refs, combine_refs, (map_ref, tokens_ref) = outs[:-4], outs[-4:-2], outs[-2:]

    def numbers(y, core):
        if relative:
            y = y + place_ref[1].astype(F32)
            y = jnp.where(y >= float(NY), y - float(NY), y)
            own = place_ref[3].astype(F32)
            core = own + core - 2.0 * own * core
        return y * float(NZ * NC) + core + place_ref[2].astype(F32) * float(NC)

    expert = numbers(table_ref[0:1, :], table_ref[1:2, :])
    spot = table_ref[2:3, :]
    rank_wanted = table_ref[3:4, :]
    row = lax.broadcasted_iota(jnp.int32, (tok, tok), 0)
    col = lax.broadcasted_iota(jnp.int32, (tok, tok), 1)
    before = jnp.where(col < row, 1.0, 0.0).astype(BF)
    for s in range(2):
        for i in range(PAIR):
            block = blocks[PAIR * s + i]
            meta = block[:, width : width + META].astype(F32)
            hit = jnp.zeros((tok, LANES), F32)
            weight = jnp.zeros((tok, LANES), F32)
            for k in range(8):
                same = meta[:, k : k + 1] == expert
                hit = jnp.where(same, 1.0, hit)
                weight = jnp.where(same, meta[:, 8 + k : 9 + k], weight)
            rank = jnp.dot(before, hit.astype(BF), preferred_element_type=F32)
            chosen = (hit > 0.0) & (rank == rank_wanted) & (spot == float(i))
            map_ref[i * tok : (i + 1) * tok, :] = jnp.where(chosen, 1.0, 0.0).astype(BF)
            combine_refs[s][i * tok : (i + 1) * tok, :] = jnp.where(chosen, weight, 0.0).astype(BF)
            tokens_ref[i * tok : (i + 1) * tok, :] = block[:, :width]
        rows = lax.dot_general(
            map_ref[...], tokens_ref[...], (((0,), (0,)), ((), ())), preferred_element_type=F32
        )
        for d in range(PEERS):
            part = rows[d * SPAN : (d + 1) * SPAN, :].astype(BF)
            if relative:
                rows_refs[d][s * SPAN : (s + 1) * SPAN, :] = part
            else:
                rows_refs[0][d, s * SPAN : (s + 1) * SPAN, :] = part
    if relative:
        lane = lax.broadcasted_iota(jnp.int32, (1, META), 1)
        peer_expert = numbers((lane // NC).astype(F32), (lane % NC).astype(F32))
        named = jnp.zeros((1, META), F32)
        load = jnp.zeros((1, META), F32)
        metas = [b[:, width : width + META] for b in blocks] + [b[...] for b in extra]
        for meta in metas:
            meta = meta.astype(F32)
            for k in range(8):
                same = meta[:, k : k + 1] == peer_expert
                named = named + jnp.sum(jnp.where(same, 1.0, 0.0), axis=0, keepdims=True)
                load = load + jnp.sum(
                    jnp.where(same, meta[:, 8 + k : 9 + k], 0.0), axis=0, keepdims=True
                )
        high = load.astype(BF).astype(F32)
        middle = (load - high).astype(BF).astype(F32)
        low = load - high - middle
        line = lax.broadcasted_iota(jnp.int32, (8, META), 0)
        pieces = jnp.where(line == 2, middle, jnp.where(line == 3, low, 0.0))
        pieces = jnp.where(line == 0, named, jnp.where(line == 1, high, pieces))
        for d in range(PEERS):
            rows_refs[d][HALF : HALF + 8, :] = jnp.broadcast_to(pieces[:, d : d + 1], (8, width)).astype(BF)


def dispatch(place, blocks, extra):
    tok, wide = blocks[0].shape
    width = wide - META
    side = pl.BlockSpec((tok, META), lambda i: (0, width // META))
    full = pl.BlockSpec((tok, wide), lambda i: (0, 0))
    flat = pl.BlockSpec((PAIR * tok, LANES), lambda i: (0, 0))
    if extra:
        specs = [pl.BlockSpec((HALF + 8, width), lambda i: (0, 0))] * PEERS
        shapes = [shape_of(HALF + 8, width)] * PEERS
    else:
        specs = [pl.BlockSpec((PEERS, HALF, width), lambda i: (0, 0, 0))]
        shapes = [shape_of(PEERS, HALF, width)]
    outs = pl.pallas_call(
        functools.partial(dispatch_kernel, bool(extra)),
        grid=(1,),
        in_specs=[whole(SMEM), pl.BlockSpec((8, LANES), lambda i: (0, 0))]
        + [full] * len(blocks)
        + [side] * len(extra),
        out_specs=specs + [flat] * 2,
        out_shape=shapes + [shape_of(PAIR * tok, LANES)] * 2,
        scratch_shapes=[VMEM((PAIR * tok, LANES), BF), VMEM((PAIR * tok, width), BF)],
        name="dispatch",
    )(place, jnp.asarray(lane_table()), *blocks, *extra)
    return outs[:-2], outs[-2:]


def products(block_ref, gate_ref, up_ref, outs):
    right, left, gate_own, up_own, gate_next, up_last = outs

    def columns(n, carry):
        at = pl.ds(pl.multiple_of(n * WIDE, WIDE), WIDE)
        gate = jnp.dot(block_ref[...], gate_ref[:, at], preferred_element_type=F32).astype(BF)
        right[:SHARE, at] = gate[2 * SHARE : 3 * SHARE, :]
        left[SHARE:, at] = gate[3 * SHARE :, :]
        gate_own[:, at] = gate[:SHARE, :]
        gate_next[:, at] = gate[SHARE : 2 * SHARE, :]
        up = jnp.dot(block_ref[...], up_ref[:, at], preferred_element_type=F32).astype(BF)
        left[:SHARE, at] = up[2 * SHARE : 3 * SHARE, :]
        right[SHARE:, at] = up[SHARE : 2 * SHARE, :]
        up_own[:, at] = up[:SHARE, :]
        up_last[:, at] = up[3 * SHARE :, :]
        return carry

    lax.fori_loop(0, gate_ref.shape[1] // WIDE, columns, 0)


def product_shapes(hidden):
    return [shape_of(2 * SHARE, hidden)] * 2 + [shape_of(SHARE, hidden)] * 4


def fetch(gate_hbm, up_hbm, gate_ref, up_ref, sems):
    return [
        pltpu.make_async_copy(gate_hbm, gate_ref, sems.at[0]),
        pltpu.make_async_copy(up_hbm, up_ref, sems.at[1]),
    ]


def expert_kernel(count, place_ref, edges_ref, gate_hbm, up_hbm, near_ref, *refs):
    far = refs[:PEERS]
    outs = refs[PEERS : PEERS + 6]
    near_clipped, load_ref = refs[PEERS + 6 : PEERS + 8]
    gate_ref, up_ref, far_clipped, sems = refs[PEERS + 8 :]
    width = far_clipped.shape[1]
    copies = fetch(gate_hbm, up_hbm, gate_ref, up_ref, sems)
    for copy in copies:
        copy.start()
    edges = [edges_ref[j] for j in range(16)]
    load = jnp.zeros((8, 128), F32)
    for k in range(PEERS):
        load = load + far[k][HALF : HALF + 8, 0:128].astype(F32)
    load = (load[1:2] + load[2:3] + load[3:4]) / float(count)
    load_ref[0] = load[0, 0]

    def home(d):
        turn = lax.rem(d // NC - place_ref[0] + NX, NX)
        return turn * SHARE + lax.rem(d, NC) * HALF

    near_home = [home(d) for d in range(PEERS)]
    far_home = [home(peer(place_ref, k, -1)) for k in range(PEERS)]

    def strip(s, carry):
        at = pl.ds(pl.multiple_of(s * STRIP, STRIP), STRIP)
        total = jnp.zeros((8, STRIP), F32)
        for k in range(PEERS):
            total = total + far[k][HALF : HALF + 8, at].astype(F32)
        limit = jnp.floor(total[0:1] / float(CLIP_PARTS))

        def tiles():
            for d in range(PEERS):
                for r in range(0, HALF, 16):
                    yield near_ref[d, r : r + 16, at], near_clipped, near_home[d] + r
                    yield far[d][r : r + 16, at], far_clipped, far_home[d] + r

        def more_above(level):
            near = level.astype(BF).astype(F32)
            above = (level * (1.0 + 2.0**-8)).astype(BF).astype(F32)
            bound = jnp.where(near >= level, near, above)
            bound = jnp.broadcast_to(bound, (16, STRIP)).astype(BF)
            one, nil = jnp.ones_like(bound), jnp.zeros_like(bound)
            sums = [jnp.zeros((16, STRIP), BF)] * 2
            for i, (tile, _, _) in enumerate(tiles()):
                sums[i % 2] = sums[i % 2] + jnp.where(jnp.abs(tile) >= bound, one, nil)
            return jnp.sum((sums[0] + sums[1]).astype(F32), axis=0, keepdims=True) > limit

        def edge_at(at_edge):
            value = jnp.zeros((1, STRIP), F32)
            for j in range(16):
                value = jnp.where(at_edge == float(j), edges[j], value)
            return value

        def coarse(i, found):
            m, step = found
            return jnp.where(more_above(edge_at(m + (step - 1.0))), m + step, m), step * 0.5

        start = jnp.zeros((1, STRIP), F32)
        m, _ = lax.fori_loop(0, 4, coarse, (start, start + 8.0))
        upper, lower = edge_at(m), edge_at(m - 1.0)

        def finer(i, found):
            n, step = found
            level = lower + (upper - lower) * ((n + step) * (1.0 / FINE))
            return jnp.where(more_above(level), n + step, n), step * 0.5

        n, _ = lax.fori_loop(0, 3, finer, (start, start + 4.0))
        scale = jnp.where(n == FINE - 1.0, upper, lower + (upper - lower) * ((n + 1.0) * (1.0 / FINE)))
        top = jnp.broadcast_to(scale, (16, STRIP)).astype(BF)
        for tile, target, row in tiles():
            target[pl.ds(pl.multiple_of(row, 16), 16), at] = jnp.minimum(jnp.maximum(tile, -top), top)
        return carry

    lax.fori_loop(0, width // STRIP, strip, 0)
    for copy in copies:
        copy.wait()
    products(far_clipped, gate_ref, up_ref, outs)


def expert_in(place, edges, gate, up, near, far, count):
    width, hidden = gate.shape
    outs = pl.pallas_call(
        functools.partial(expert_kernel, count),
        in_specs=[whole(SMEM), whole(SMEM), whole(pl.ANY), whole(pl.ANY)] + [whole()] * (1 + PEERS),
        out_specs=[whole()] * 7 + [whole(SMEM)],
        out_shape=product_shapes(hidden) + [shape_of(ROWS, width), jax.ShapeDtypeStruct((1,), F32)],
        scratch_shapes=[
            VMEM((width, hidden), BF),
            VMEM((width, hidden), BF),
            VMEM((ROWS, width), BF),
            pltpu.SemaphoreType.DMA((2,)),
        ],
        name="expert_in",
    )(place, edges, gate, up, near, *far)
    return outs[:6], outs[6], outs[7]


def later_kernel(block_ref, gate_hbm, up_hbm, *refs):
    outs, (gate_ref, up_ref, sems) = refs[:6], refs[6:]
    copies = fetch(gate_hbm, up_hbm, gate_ref, up_ref, sems)
    for copy in copies:
        copy.start()
    for copy in copies:
        copy.wait()
    products(block_ref, gate_ref, up_ref, outs)


def expert_later(block, gate, up):
    width, hidden = gate.shape
    return pl.pallas_call(
        later_kernel,
        in_specs=[whole(), whole(pl.ANY), whole(pl.ANY)],
        out_specs=[whole()] * 6,
        out_shape=product_shapes(hidden),
        scratch_shapes=[
            VMEM((width, hidden), BF),
            VMEM((width, hidden), BF),
            pltpu.SemaphoreType.DMA((2,)),
        ],
        name="expert_later",
    )(block, gate, up)


def down_kernel(split, place_ref, down_ref, *refs):
    outs, all_ref = refs[NX:-1], refs[-1]
    for j in range(NX):
        at = pl.multiple_of(lax.rem(place_ref[0] + j, NX) * SHARE, 16)
        all_ref[pl.ds(at, SHARE), :] = refs[j][...]

    result = jnp.dot(all_ref[...], down_ref[...], preferred_element_type=F32)
    if not split:
        outs[0][...] = result.astype(BF)
        return
    for d in range(PEERS):
        for s in range(2):
            start = d * HALF + s * SPAN
            outs[s][d, :, :] = result[start : start + SPAN, :].astype(BF)


def expert_out(place, down, pieces, split):
    hidden, width = down.shape
    shapes = [shape_of(PEERS, SPAN, width)] * 2 if split else [shape_of(ROWS, width)]
    return pl.pallas_call(
        functools.partial(down_kernel, split),
        in_specs=[whole(SMEM)] + [whole()] * (1 + NX),
        out_specs=[whole()] * len(shapes),
        out_shape=shapes,
        scratch_shapes=[VMEM((ROWS, hidden), BF)],
        name="expert_out",
    )(place, down, *pieces)


def mix_far_kernel(place_ref, first_ref, second_ref, back_ref, *refs):
    outs, held = refs[:-1], refs[-1]
    tok = outs[0].shape[0]
    for s, combine_ref in enumerate((first_ref, second_ref)):
        for k in range(PEERS):
            held[k * SPAN : (k + 1) * SPAN, :] = back_ref[peer(place_ref, k, 1), s * SPAN : (s + 1) * SPAN, :]
        total = jnp.dot(combine_ref[...], held[...], preferred_element_type=F32).astype(BF)
        for i in range(PAIR):
            outs[PAIR * s + i][...] = total[i * tok : (i + 1) * tok, :]


def mix_far(place, combines, back):
    width = back.shape[2]
    tok = combines[0].shape[0] // PAIR
    return pl.pallas_call(
        mix_far_kernel,
        in_specs=[whole(SMEM)] + [whole()] * 3,
        out_specs=[whole()] * (2 * PAIR),
        out_shape=[shape_of(tok, width)] * (2 * PAIR),
        scratch_shapes=[VMEM((LANES, width), BF)],
        name="mix_far",
    )(place, *combines, back)


def mix_kernel(combine_ref, back_ref, *outs):
    tok = outs[0].shape[0]
    total = jnp.dot(combine_ref[...], back_ref[...], preferred_element_type=F32).astype(BF)
    for i in range(PAIR):
        outs[i][...] = total[i * tok : (i + 1) * tok, :]


def mix(combine, back):
    width = back.shape[1]
    tok = combine.shape[0] // PAIR
    return pl.pallas_call(
        mix_kernel,
        in_specs=[whole()] * 2,
        out_specs=[whole()] * PAIR,
        out_shape=[shape_of(tok, width)] * PAIR,
        name="mix",
    )(combine, back)


def ring(value, axis, size, shift):
    if shift % size == 0:
        return value
    return lax.ppermute(value, axis, [(i, (i + shift) % size) for i in range(size)])


def to_peer(value, k):
    if k == 0:
        return value
    dy, dc = k // NC, k % NC
    pairs = [
        (y * NC + c, (y + dy) % NY * NC + (c + dc) % NC) for y in range(NY) for c in range(NC)
    ]
    return lax.ppermute(value, OWNERS, pairs)


def swap_rows(rows):
    back = lax.all_to_all(rows, OWNERS, 0, 0, tiled=True)
    return back


def summed(pieces):
    right, left = pieces[:2]
    return ring(right, "x", NX, 1), ring(left, "x", NX, -1)


def activated(pieces, hops):
    gate_own, up_own, gate_next, up_last = pieces[2:]
    right, left = hops
    gate_sum = (gate_next.astype(F32) + right[:SHARE].astype(F32)).astype(BF)
    up_sum = (up_last.astype(F32) + left[:SHARE].astype(F32)).astype(BF)
    gate_sum = ring(gate_sum, "x", NX, 1)
    up_sum = ring(up_sum, "x", NX, -1)
    gate = gate_own.astype(F32) + gate_sum.astype(F32) + left[SHARE:].astype(F32)
    up = up_own.astype(F32) + up_sum.astype(F32) + right[SHARE:].astype(F32)
    return (jax.nn.silu(gate) * up).astype(BF)


def spread(hidden):
    return [ring(hidden, "x", NX, -j) for j in range(NX)]


def body(tokens, expert_ids, route_weights, gate_weight, up_weight, down_weight, bin_edges):
    tok, width = tokens.shape
    place = jnp.stack([lax.axis_index(a) for a in ("x", "y", "z", "c")]).astype(jnp.int32)
    side = jnp.concatenate([expert_ids.astype(BF), route_weights], axis=1)
    side = jnp.pad(side, ((0, 0), (0, META - side.shape[1])))
    wide = jnp.concatenate([tokens, side], axis=1)
    near_offsets = [o for pair in NEAR for o in pair]
    far_offsets = [o for pair in FAR for o in pair]
    near_blocks = [ring(wide, "z", NZ, -o) for o in near_offsets]
    far_blocks = [ring(wide, "z", NZ, -o) for o in far_offsets]
    (rows,), near_maps = dispatch(place, near_blocks, [])
    near = swap_rows(rows)
    rows, far_maps = dispatch(place, far_blocks, near_blocks)
    far = [to_peer(r, k) for k, r in enumerate(rows)]
    gate, up, down = gate_weight[0], up_weight[0], down_weight[0]
    far_pieces, clipped, expert_load = expert_in(
        place, bin_edges, gate, up, near, far, tok * expert_ids.shape[1]
    )
    far_hops = summed(far_pieces)
    near_pieces = expert_later(clipped, gate, up)
    hidden = activated(far_pieces, far_hops)
    near_hops = summed(near_pieces)
    shares = spread(hidden)
    (result,) = expert_out(place, down, shares, False)
    far_back = swap_rows(result.reshape(PEERS, HALF, width))
    hidden = activated(near_pieces, near_hops)
    shares = spread(hidden)
    results = expert_out(place, down, shares, True)
    second_back = swap_rows(results[1]).reshape(LANES, width)
    first_back = swap_rows(results[0]).reshape(LANES, width)
    sums = mix_far(place, far_maps, far_back)
    sums = [ring(part, "z", NZ, o) for o, part in zip(far_offsets, sums)]
    more = mix(near_maps[1], second_back)
    sums += [ring(part, "z", NZ, o) for o, part in zip(NEAR[1], more)]
    more = mix(near_maps[0], first_back)
    sums += [ring(part, "z", NZ, o) for o, part in zip(NEAR[0], more)]
    total = sums[0].astype(F32)
    for part in sums[1:]:
        total = total + part.astype(F32)
    return (total.astype(BF), expert_load)


def solution(mesh):
    finer = Mesh(mesh.devices.reshape(NY, NZ, NC, NX), ("y", "z", "c", "x"))
    placed = (
        P(EXPERT, "x"),
        P(EXPERT, None),
        P(EXPERT, None),
        P(EXPERT, "x", None),
        P(EXPERT, "x", None),
        P(EXPERT, None, "x"),
        P(),
    )
    return jax.shard_map(
        body,
        mesh=finer,
        in_specs=placed,
        out_specs=(P(EXPERT, "x"), P(EXPERT)),
        check_vma=False,
    )
```

time: 252 us -> 257 us (1.020)
  Pallas kernels: 35.9 us -> 44.6 us
  local copies, waits for them, and re-layouts: 9.28 us -> 6.14 us
    ppermute x0 -> x7, waiting for transfers between devices: none -> 15.2 us  [to_peer(): return lax.ppermute(value, OWNERS, pairs)]
    all_to_all x4, waiting for transfers between devices: 33.2 us -> 18.2 us  [swap_rows(): back = lax.all_to_all(rows, OWNERS, 0, 0, tiled=True)]
    pallas_call x7 -> x9, Pallas kernels: 35.9 us -> 44.6 us  [the longest x1 11.4 us: expert_in(): pl.pallas_call(functools.partial(expert_kernel, count), in_specs=[whole(S...]
    ppermute x0 -> x7, starting transfers between devices: none -> 8.27 us  [to_peer(): return lax.ppermute(value, OWNERS, pairs)]
    ppermute x32 -> x28, starting transfers between devices: 63.6 us -> 55.5 us  [ring(): lax.ppermute(value, axis, [(i, (i + shift) % size) for i in range(size)])]
    unnamed x60 -> x68, local copies, waits for them, and re-layouts: 8 us -> 6.05 us
    ppermute x32 -> x28, waiting for transfers between devices: 83.4 us -> 83.2 us  [ring(): lax.ppermute(value, axis, [(i, (i + shift) % size) for i in range(size)])]
  transfers between devices with their start and end apart: 36 -> 39, of which waited for: 21 -> 22; matrix products, arithmetic and copies ran while one was open for 1% -> 2% of each run, Pallas kernels for 8% -> 8%
where the time goes in v1:
time: 257 us; the launch traced here: 256 us
  waiting for transfers between devices  117 us (46%)
  starting transfers between devices  80.4 us (31%)
  Pallas kernels  44.6 us (17%)
  other arithmetic  7.35 us (3%)
  local copies, waits for them, and re-layouts  6.14 us (2%)
    ppermute x28, waiting for transfers between devices, ring(): lax.ppermute(value, axis, [(i, (i + shift) % size) for i in range(size)])  83.2 us
    ppermute x28, starting transfers between devices, ring(): lax.ppermute(value, axis, [(i, (i + shift) % size) for i in range(size)])  55.5 us
    all_to_all x4, waiting for transfers between devices, swap_rows(): back = lax.all_to_all(rows, OWNERS, 0, 0, tiled=True)  18.2 us
    all_to_all x4, starting transfers between devices, swap_rows(): back = lax.all_to_all(rows, OWNERS, 0, 0, tiled=True)  16.7 us
    ppermute x7, waiting for transfers between devices, to_peer(): return lax.ppermute(value, OWNERS, pairs)  15.2 us
    pallas_call x1, Pallas kernels, expert_in(): pl.pallas_call(functools.partial(expert_kernel, count), in_specs=[whole(S...  11.4 us
    pallas_call x2, Pallas kernels, expert_out(): pl.pallas_call(functools.partial(down_kernel, split), in_specs=[whole(SME...  10.1 us
    pallas_call x1, Pallas kernels, expert_later(): pl.pallas_call(later_kernel, in_specs=[whole(), whole(pl.ANY), whole(pl.A...  8.79 us
  transfers between devices with their start and end apart: 39, of which 22 were waited for; matrix products, arithmetic and copies ran while one was open for 2% of the time, Pallas kernels for 8%

profile of v1, /device:TPU:32, one launch (start us, length us, event | category | flops | bytes accessed | tf_op | source)
XLA Modules:
  0.0 256.0 jit_solution(12530635107242845217)
XLA Ops:
  2.1 0.9 fusion.1.refs_4_.refs_0_
  3.1 5.5 %collective-permute-start.6 = (bf16[48,1920]{1,0:T(8,128)(2,1)S(1)}, bf16[48,1920]{1,0:T(8,128)(2,1)S(1)}, u32[]{:S(2)}, u32[]{:S(2)}) collective-permute-start(bf16[48,1920]{1,0:T(8,128)(2,1)S(1)} %fusion.1.refs_4_.refs_0_), channel_id=1, source_target_pairs={{0,48},{8,56},{16,0},{24,8},{32,16},{40,24},{48,32},{56,40},{1,49}... | collective-permute-start | bytes 552968 | tf_op jit(solution)/shard_map/ppermute | solution.py:387
  8.5 2.0 collective-permute-start.4
  11.2 4.1 %collective-permute-done.6.refs_7_.refs_3_ = bf16[48,1920]{1,0:T(8,128)(2,1)S(1)} collective-permute-done((bf16[48,1920]{1,0:T(8,128)(2,1)S(1)}, bf16[48,1920]{1,0:T(8,128)(2,1)S(1)}, u32[]{:S(2)}, u32[]{:S(2)}) %collective-permute-start.6) | collective-permute-done | bytes 184352 | tf_op jit(solution)/shard_map/ppermute | solution.py:387
  15.3 3.5 %collective-permute-done.4.refs_5_.refs_1_ = bf16[48,1920]{1,0:T(8,128)(2,1)S(1)} collective-permute-done((bf16[48,1920]{1,0:T(8,128)(2,1)S(1)}, bf16[48,1920]{1,0:T(8,128)(2,1)S(1)}, u32[]{:S(2)}, u32[]{:S(2)}) %collective-permute-start.4) | collective-permute-done | bytes 184352 | tf_op jit(solution)/shard_map/ppermute | solution.py:387
  19.6 3.5 %dispatch.3 = (bf16[8,48,1792]{2,1,0:T(8,128)(2,1)}, bf16[96,192]{1,0:T(8,128)(2,1)}, bf16[96,192]{1,0:T(8,128)(2,1)}) custom-call(s32[4]{0:T(128)} %pad_add_fusion.place_ref, f32[8,192]{1,0:T(8,128)} %constant.26.clone.table_ref, bf16[48,1920]{1,0:T(8,128)(2,1)} %copy-done.4, bf16[48,1920]{1,0:T(8,128)(2,1)} %copy-done.10, bf16[48,1920]{1,0:T(8,128)(2,1)} %copy-done.9, ...), custom_call_target="tpu_custom_call" | custom-call | tf_op jit(solution)/shard_map/dispatch/pallas_call | solution.py:144
  23.1 4.6 %all-to-all-start = ((bf16[8,48,1792]{2,1,0:T(8,128)(2,1)}), bf16[8,48,1792]{2,1,0:T(8,128)(2,1)S(1)}, u32[]{:S(2)}, u32[]{:S(2)}) async-start(bf16[8,48,1792]{2,1,0:T(8,128)(2,1)} %get-tuple-element.41), calls=%async_computation | async-start | bytes 2752512 | tf_op jit(solution)/shard_map/all_to_all | solution.py:401
  27.7 5.4 %collective-permute-start.3 = (bf16[48,1920]{1,0:T(8,128)(2,1)S(1)}, bf16[48,1920]{1,0:T(8,128)(2,1)S(1)}, u32[]{:S(2)}, u32[]{:S(2)}) collective-permute-start(bf16[48,1920]{1,0:T(8,128)(2,1)S(1)} %copy-done.5), channel_id=1, source_target_pairs={{0,32},{8,40},{16,48},{24,56},{32,0},{40,8},{48,16},{56,24},{1,33}... | collective-permute-start | bytes 552968 | tf_op jit(solution)/shard_map/ppermute | solution.py:387
  33.0 1.7 collective-permute-start.2
  34.7 3.4 %collective-permute-start.1 = (bf16[48,1920]{1,0:T(8,128)(2,1)S(1)}, bf16[48,1920]{1,0:T(8,128)(2,1)S(1)}, u32[]{:S(2)}, u32[]{:S(2)}) collective-permute-start(bf16[48,1920]{1,0:T(8,128)(2,1)S(1)} %copy-done.5), channel_id=1, source_target_pairs={{0,40},{8,48},{16,56},{24,0},{32,8},{40,16},{48,24},{56,32},{1,41}... | collective-permute-start | bytes 552968 | tf_op jit(solution)/shard_map/ppermute | solution.py:387
  38.1 1.5 collective-permute-start
  39.6 3.8 %collective-permute-done.3.refs_3_ = bf16[48,1920]{1,0:T(8,128)(2,1)S(1)} collective-permute-done((bf16[48,1920]{1,0:T(8,128)(2,1)S(1)}, bf16[48,1920]{1,0:T(8,128)(2,1)S(1)}, u32[]{:S(2)}, u32[]{:S(2)}) %collective-permute-start.3) | collective-permute-done | bytes 184352 | tf_op jit(solution)/shard_map/ppermute | solution.py:387
  43.4 10.4 %collective-permute-done.2.refs_2_ = bf16[48,1920]{1,0:T(8,128)(2,1)S(1)} collective-permute-done((bf16[48,1920]{1,0:T(8,128)(2,1)S(1)}, bf16[48,1920]{1,0:T(8,128)(2,1)S(1)}, u32[]{:S(2)}, u32[]{:S(2)}) %collective-permute-start.2) | collective-permute-done | bytes 184352 | tf_op jit(solution)/shard_map/ppermute | solution.py:387
  53.8 7.8 %collective-permute-done.refs_0_ = bf16[48,1920]{1,0:T(8,128)(2,1)S(1)} collective-permute-done((bf16[48,1920]{1,0:T(8,128)(2,1)S(1)}, bf16[48,1920]{1,0:T(8,128)(2,1)S(1)}, u32[]{:S(2)}, u32[]{:S(2)}) %collective-permute-start) | collective-permute-done | bytes 184352 | tf_op jit(solution)/shard_map/ppermute | solution.py:387
  62.3 4.1 %dispatch.2 = (bf16[56,1792]{1,0:T(8,128)(2,1)}, bf16[56,1792]{1,0:T(8,128)(2,1)}, bf16[56,1792]{1,0:T(8,128)(2,1)}, bf16[56,1792]{1,0:T(8,128)(2,1)}, bf16[56,1...) custom-call(s32[4]{0:T(128)} %pad_add_fusion.place_ref, ...), custom_call_target="tpu_custom_call" | custom-call | tf_op jit(solution)/shard_map/dispatch/pallas_call | solution.py:144
  66.4 1.7 collective-permute-start.8
  68.1 1.2 collective-permute-start.9
  69.3 1.6 collective-permute-start.10
  70.9 1.6 collective-permute-start.11
  72.6 1.8 collective-permute-start.12
  74.3 1.4 collective-permute-done.8.refs_2_
  76.0 2.9 %collective-permute-done.9.refs_3_ = bf16[56,1792]{1,0:T(8,128)(2,1)S(1)} collective-permute-done((bf16[56,1792]{1,0:T(8,128)(2,1)}, bf16[56,1792]{1,0:T(8,128)(2,1)S(1)}, u32[]{:S(2)}, u32[]{:S(2)}) %collective-permute-start.9) | collective-permute-done | bytes 200736 | tf_op jit(solution)/shard_map/ppermute | solution.py:397
  79.0 6.5 %collective-permute-done.10.refs_4_ = bf16[56,1792]{1,0:T(8,128)(2,1)S(1)} collective-permute-done((bf16[56,1792]{1,0:T(8,128)(2,1)}, bf16[56,1792]{1,0:T(8,128)(2,1)S(1)}, u32[]{:S(2)}, u32[]{:S(2)}) %collective-permute-start.10) | collective-permute-done | bytes 200736 | tf_op jit(solution)/shard_map/ppermute | solution.py:397
  85.5 3.2 %collective-permute-done.11.refs_5_ = bf16[56,1792]{1,0:T(8,128)(2,1)S(1)} collective-permute-done((bf16[56,1792]{1,0:T(8,128)(2,1)}, bf16[56,1792]{1,0:T(8,128)(2,1)S(1)}, u32[]{:S(2)}, u32[]{:S(2)}) %collective-permute-start.11) | collective-permute-done | bytes 200736 | tf_op jit(solution)/shard_map/ppermute | solution.py:397
  88.7 1.1 collective-permute-done.13.refs_7_
  90.9 11.4 %expert_in.1 = (bf16[192,1024]{1,0:T(8,128)(2,1)}, bf16[192,1024]{1,0:T(8,128)(2,1)}, bf16[96,1024]{1,0:T(8,128)(2,1)}, bf16[96,1024]{1,0:T(8,128)(2,1)}, bf16[9...) custom-call(s32[4]{0:T(128)} %pad_add_fusion.place_ref, f32[16]{0:T(128)} %edges_ref.1, ...), custom_call_target="tpu_custom_call" | custom-call | tf_op jit(solution)/shard_map/expert_in/pallas_call | solution.py:270
  102.3 8.8 %expert_later.1 = (bf16[192,1024]{1,0:T(8,128)(2,1)}, bf16[192,1024]{1,0:T(8,128)(2,1)}, bf16[96,1024]{1,0:T(8,128)(2,1)}, bf16[96,1024]{1,0:T(8,128)(2,1)}, bf1...) custom-call(bf16[384,1792]{1,0:T(8,128)(2,1)} %get-tuple-element.61.block_ref, bf16[1792,1024]{1,0:T(8,128)(2,1)} %bitcast.11, ...), custom_call_target="tpu_custom_call" | custom-call | tf_op jit(solution)/shard_map/expert_later/pallas_call | solution.py:298
  111.1 1.6 collective-permute-start.25
  112.7 1.7 collective-permute-start.27
  114.4 9.6 %collective-permute-done.25 = bf16[192,1024]{1,0:T(8,128)(2,1)S(1)} collective-permute-done((bf16[192,1024]{1,0:T(8,128)(2,1)}, bf16[192,1024]{1,0:T(8,128)(2,1)S(1)}, u32[]{:S(2)}, u32[]{:S(2)}) %collective-permute-start.25) | collective-permute-done | bytes 393248 | tf_op jit(solution)/shard_map/ppermute | solution.py:387
  124.1 1.0 add_convert_fusion.1
  125.4 1.0 add_convert_fusion
  126.4 3.0 %collective-permute-start.28 = (bf16[96,1024]{1,0:T(8,128)(2,1)S(1)}, bf16[96,1024]{1,0:T(8,128)(2,1)S(1)}, u32[]{:S(2)}, u32[]{:S(2)}) collective-permute-start(bf16[96,1024]{1,0:T(8,128)(2,1)S(1)} %add_convert_fusion), channel_id=1, source_target_pairs={{0,3},{1,0},{2,1},{3,2},{4,7},{5,4},{6,5},{7,6},{8,11},{9,8},{10,9... | collective-permute-start | bytes 589832 | tf_op jit(solution)/shard_map/ppermute | solution.py:387
  129.4 3.5 %collective-permute-done.26 = bf16[96,1024]{1,0:T(8,128)(2,1)S(1)} collective-permute-done((bf16[96,1024]{1,0:T(8,128)(2,1)S(1)}, bf16[96,1024]{1,0:T(8,128)(2,1)S(1)}, u32[]{:S(2)}, u32[]{:S(2)}) %collective-permute-start.26) | collective-permute-done | bytes 196640 | tf_op jit(solution)/shard_map/ppermute | solution.py:387
  133.0 1.2 multiply_convert_fusion.refs_0_
  134.3 1.1 collective-permute-start.31
  135.4 4.1 %collective-permute-start.30 = (bf16[96,1024]{1,0:T(8,128)(2,1)S(1)}, bf16[96,1024]{1,0:T(8,128)(2,1)S(1)}, u32[]{:S(2)}, u32[]{:S(2)}) collective-permute-start(bf16[96,1024]{1,0:T(8,128)(2,1)S(1)} %multiply_convert_fusion.refs_0_), channel_id=1, source_target_pairs={{0,2},{1,3},{2,0},{3,1},{4,6},{5,7},{6,4},{7,5},{8,10},{9,11},{10,... | collective-permute-start | bytes 589832 | tf_op jit(solution)/shard_map/ppermute | solution.py:387
  140.1 9.5 %collective-permute-done.31.refs_3_ = bf16[96,1024]{1,0:T(8,128)(2,1)S(1)} collective-permute-done((bf16[96,1024]{1,0:T(8,128)(2,1)S(1)}, bf16[96,1024]{1,0:T(8,128)(2,1)S(1)}, u32[]{:S(2)}, u32[]{:S(2)}) %collective-permute-start.31) | collective-permute-done | bytes 196640 | tf_op jit(solution)/shard_map/ppermute | solution.py:387
  150.4 5.0 %expert_out.3 = (bf16[8,24,1792]{2,1,0:T(8,128)(2,1)}, bf16[8,24,1792]{2,1,0:T(8,128)(2,1)}) custom-call(s32[4]{0:T(128)} %pad_add_fusion.place_ref, bf16[1024,1792]{1,0:T(8,128)(2,1)} %bitcast.14, bf16[96,1024]{1,0:T(8,128)(2,1)} %copy-done.6, bf16[96,1024]{1,0:T(8,128)(2,1)} %copy-done.20, bf16[96,1024]{1,0:T(8,128)(2,1)} %copy-done.19, ...), custom_call_target="tpu_custom_call" | custom-call | tf_op jit(solution)/shard_map/expert_out/pallas_call | solution.py:331
  155.4 4.1 %all-to-all-start.2 = ((bf16[8,24,1792]{2,1,0:T(8,128)(2,1)}), bf16[8,24,1792]{2,1,0:T(8,128)(2,1)S(1)}, u32[]{:S(2)}, u32[]{:S(2)}) async-start(bf16[8,24,1792]{2,1,0:T(8,128)(2,1)} %get-tuple-element.68), calls=%async_computation.2 | async-start | bytes 1376256 | tf_op jit(solution)/shard_map/all_to_all | solution.py:401
  159.8 3.5 %collective-permute-start.17 = (bf16[96,1024]{1,0:T(8,128)(2,1)S(1)}, bf16[96,1024]{1,0:T(8,128)(2,1)S(1)}, u32[]{:S(2)}, u32[]{:S(2)}) collective-permute-start(bf16[96,1024]{1,0:T(8,128)(2,1)S(1)} %add_convert_fusion.2), channel_id=1, source_target_pairs={{0,3},{1,0},{2,1},{3,2},{4,7},{5,4},{6,5},{7,6},{8,11},{9,8},{10,9... | collective-permute-start | bytes 589832 | tf_op jit(solution)/shard_map/ppermute | solution.py:387
  163.3 8.3 %all-to-all-done.2 = bf16[8,24,1792]{2,1,0:T(8,128)(2,1)S(1)} async-done(((bf16[8,24,1792]{2,1,0:T(8,128)(2,1)}), bf16[8,24,1792]{2,1,0:T(8,128)(2,1)S(1)}, u32[]{:S(2)}, u32[]{:S(2)}) %all-to-all-start.2) | async-done | bytes 688160 | tf_op jit(solution)/shard_map/all_to_all | solution.py:401
  171.6 3.5 %all-to-all-start.3 = ((bf16[8,24,1792]{2,1,0:T(8,128)(2,1)}), bf16[8,24,1792]{2,1,0:T(8,128)(2,1)S(1)}, u32[]{:S(2)}, u32[]{:S(2)}) async-start(bf16[8,24,1792]{2,1,0:T(8,128)(2,1)} %get-tuple-element.72), calls=%async_computation.3 | async-start | bytes 1376256 | tf_op jit(solution)/shard_map/all_to_all | solution.py:401
  175.5 1.8 collective-permute-start.19
  177.4 1.8 collective-permute-start.18
  179.1 9.0 %collective-permute-done.20.refs_3_ = bf16[96,1024]{1,0:T(8,128)(2,1)S(1)} collective-permute-done((bf16[96,1024]{1,0:T(8,128)(2,1)S(1)}, bf16[96,1024]{1,0:T(8,128)(2,1)S(1)}, u32[]{:S(2)}, u32[]{:S(2)}) %collective-permute-start.20) | collective-permute-done | bytes 196640 | tf_op jit(solution)/shard_map/ppermute | solution.py:387
  189.6 5.0 %expert_out.2 = bf16[384,1792]{1,0:T(8,128)(2,1)} custom-call(s32[4]{0:T(128)} %pad_add_fusion.place_ref, bf16[1024,1792]{1,0:T(8,128)(2,1)} %bitcast.15, bf16[96,1024]{1,0:T(8,128)(2,1)} %copy-done.7, bf16[96,1024]{1,0:T(8,128)(2,1)} %copy-done.23, bf16[96,1024]{1,0:T(8,128)(2,1)} %copy-done.22, bf16[96,1024]{1,0:T(8,128)(2,1)} %copy-done.21), custom_call_target="tpu_custom_call" | custom-call | tf_op jit(solution)/shard_map/expert_out/pallas_call | solution.py:331
  195.4 4.4 %all-to-all-start.1 = ((bf16[8,48,1792]{2,1,0:T(8,128)(2,1)}), bf16[8,48,1792]{2,1,0:T(8,128)(2,1)S(1)}, u32[]{:S(2)}, u32[]{:S(2)}) async-start(bf16[8,48,1792]{2,1,0:T(8,128)(2,1)} %bitcast.16), calls=%async_computation.1 | async-start | bytes 2752512 | tf_op jit(solution)/shard_map/all_to_all | solution.py:401
  199.9 2.1 mix.3
  202.0 1.6 collective-permute-start.34
  203.5 2.1 mix.2
  206.1 3.3 %collective-permute-start.33 = (bf16[48,1792]{1,0:T(8,128)(2,1)}, bf16[48,1792]{1,0:T(8,128)(2,1)S(1)}, u32[]{:S(2)}, u32[]{:S(2)}) collective-permute-start(bf16[48,1792]{1,0:T(8,128)(2,1)} %get-tuple-element.70), channel_id=1, source_target_pairs={{0,16},{8,24},{16,32},{24,40},{32,48},{40,56},{48,0},{56,8},{1,17}... | collective-permute-start | bytes 516104 | tf_op jit(solution)/shard_map/ppermute | solution.py:387
  209.5 9.9 %all-to-all-done.1.back_ref = bf16[8,48,1792]{2,1,0:T(8,128)(2,1)S(1)} async-done(((bf16[8,48,1792]{2,1,0:T(8,128)(2,1)}), bf16[8,48,1792]{2,1,0:T(8,128)(2,1)S(1)}, u32[]{:S(2)}, u32[]{:S(2)}) %all-to-all-start.1) | async-done | bytes 1376288 | tf_op jit(solution)/shard_map/all_to_all | solution.py:401
  219.3 1.1 copy-done
  220.4 2.5 mix_far.1
  222.9 3.3 %collective-permute-start.21 = (bf16[48,1792]{1,0:T(8,128)(2,1)}, bf16[48,1792]{1,0:T(8,128)(2,1)S(1)}, u32[]{:S(2)}, u32[]{:S(2)}) collective-permute-start(bf16[48,1792]{1,0:T(8,128)(2,1)} %get-tuple-element.56), channel_id=1, source_target_pairs={{0,48},{8,56},{16,0},{24,8},{32,16},{40,24},{48,32},{56,40},{1,49}... | collective-permute-start | bytes 516104 | tf_op jit(solution)/shard_map/ppermute | solution.py:387
  226.3 1.8 collective-permute-start.22
  228.1 3.3 %collective-permute-start.23 = (bf16[48,1792]{1,0:T(8,128)(2,1)}, bf16[48,1792]{1,0:T(8,128)(2,1)S(1)}, u32[]{:S(2)}, u32[]{:S(2)}) collective-permute-start(bf16[48,1792]{1,0:T(8,128)(2,1)} %get-tuple-element.58), channel_id=1, source_target_pairs={{0,40},{8,48},{16,56},{24,0},{32,8},{40,16},{48,24},{56,32},{1,41}... | collective-permute-start | bytes 516104 | tf_op jit(solution)/shard_map/ppermute | solution.py:387
  231.3 2.6 %collective-permute-start.24 = (bf16[48,1792]{1,0:T(8,128)(2,1)}, bf16[48,1792]{1,0:T(8,128)(2,1)S(1)}, u32[]{:S(2)}, u32[]{:S(2)}) collective-permute-start(bf16[48,1792]{1,0:T(8,128)(2,1)} %get-tuple-element.59), channel_id=1, source_target_pairs={{0,32},{8,40},{16,48},{24,56},{32,0},{40,8},{48,16},{56,24},{1,33}... | collective-permute-start | bytes 516104 | tf_op jit(solution)/shard_map/ppermute | solution.py:387
  233.9 5.2 %collective-permute-done.21 = bf16[48,1792]{1,0:T(8,128)(2,1)S(1)} collective-permute-done((bf16[48,1792]{1,0:T(8,128)(2,1)}, bf16[48,1792]{1,0:T(8,128)(2,1)S(1)}, u32[]{:S(2)}, u32[]{:S(2)}) %collective-permute-start.21) | collective-permute-done | bytes 172064 | tf_op jit(solution)/shard_map/ppermute | solution.py:387
  239.1 3.0 %collective-permute-done.22 = bf16[48,1792]{1,0:T(8,128)(2,1)S(1)} collective-permute-done((bf16[48,1792]{1,0:T(8,128)(2,1)}, bf16[48,1792]{1,0:T(8,128)(2,1)S(1)}, u32[]{:S(2)}, u32[]{:S(2)}) %collective-permute-start.22) | collective-permute-done | bytes 172064 | tf_op jit(solution)/shard_map/ppermute | solution.py:387
  242.1 4.3 %collective-permute-done.23 = bf16[48,1792]{1,0:T(8,128)(2,1)S(1)} collective-permute-done((bf16[48,1792]{1,0:T(8,128)(2,1)}, bf16[48,1792]{1,0:T(8,128)(2,1)S(1)}, u32[]{:S(2)}, u32[]{:S(2)}) %collective-permute-start.23) | collective-permute-done | bytes 172064 | tf_op jit(solution)/shard_map/ppermute | solution.py:387
  246.4 8.8 %collective-permute-done.24 = bf16[48,1792]{1,0:T(8,128)(2,1)S(1)} collective-permute-done((bf16[48,1792]{1,0:T(8,128)(2,1)}, bf16[48,1792]{1,0:T(8,128)(2,1)S(1)}, u32[]{:S(2)}, u32[]{:S(2)}) %collective-permute-start.24) | collective-permute-done | bytes 172064 | tf_op jit(solution)/shard_map/ppermute | solution.py:387
  255.1 0.9 add_convert_fusion.4
  (103 shorter events, 10.1 us)
Async XLA Ops:
  3.0 15.8 %copy-start.4 = (bf16[48,1920]{1,0:T(8,128)(2,1)}, bf16[48,1920]{1,0:T(8,128)(2,1)S(1)}, u32[]{:S(2)}) copy-start(bf16[48,1920]{1,0:T(8,128)(2,1)S(1)} %fusion.1.refs_4_.refs_0_) | copy-start | bytes 552964
  3.1 12.3 %collective-permute-start.6 = (bf16[48,1920]{1,0:T(8,128)(2,1)S(1)}, bf16[48,1920]{1,0:T(8,128)(2,1)S(1)}, u32[]{:S(2)}, u32[]{:S(2)}) collective-permute-start(bf16[48,1920]{1,0:T(8,128)(2,1)S(1)} %fusion.1.refs_4_.refs_0_), channel_id=1, source_target_pairs={{0,48},{8,56},{16,0},{24,8},{32,16},{40,24},{48,32},{56,40},{1,49}... | collective-permute-start | bytes 552968 | tf_op jit(solution)/shard_map/ppermute | solution.py:387
  8.5 6.8 %collective-permute-start.5 = (bf16[48,1920]{1,0:T(8,128)(2,1)S(1)}, bf16[48,1920]{1,0:T(8,128)(2,1)S(1)}, u32[]{:S(2)}, u32[]{:S(2)}) collective-permute-start(bf16[48,1920]{1,0:T(8,128)(2,1)S(1)} %fusion.1.refs_4_.refs_0_), channel_id=1, source_target_pairs={{0,8},{8,16},{16,24},{24,32},{32,40},{40,48},{48,56},{56,0},{1,9},... | collective-permute-start | bytes 552968 | tf_op jit(solution)/shard_map/ppermute | solution.py:387
  8.5 10.3 %collective-permute-start.4 = (bf16[48,1920]{1,0:T(8,128)(2,1)S(1)}, bf16[48,1920]{1,0:T(8,128)(2,1)S(1)}, u32[]{:S(2)}, u32[]{:S(2)}) collective-permute-start(bf16[48,1920]{1,0:T(8,128)(2,1)S(1)} %fusion.1.refs_4_.refs_0_), channel_id=1, source_target_pairs={{0,56},{8,0},{16,8},{24,16},{32,24},{40,32},{48,40},{56,48},{1,57}... | collective-permute-start | bytes 552968 | tf_op jit(solution)/shard_map/ppermute | solution.py:387
  15.3 3.5 %copy-start.8 = (bf16[48,1920]{1,0:T(8,128)(2,1)}, bf16[48,1920]{1,0:T(8,128)(2,1)S(1)}, u32[]{:S(2)}) copy-start(bf16[48,1920]{1,0:T(8,128)(2,1)S(1)} %collective-permute-done.6.refs_7_.refs_3_) | copy-start | bytes 552964
  15.3 3.5 %copy-start.9 = (bf16[48,1920]{1,0:T(8,128)(2,1)}, bf16[48,1920]{1,0:T(8,128)(2,1)S(1)}, u32[]{:S(2)}) copy-start(bf16[48,1920]{1,0:T(8,128)(2,1)S(1)} %collective-permute-done.5.refs_6_.refs_2_) | copy-start | bytes 552964
  23.1 4.6 %copy-start.5 = (bf16[48,1920]{1,0:T(8,128)(2,1)S(1)}, bf16[48,1920]{1,0:T(8,128)(2,1)}, u32[]{:S(2)}) copy-start(bf16[48,1920]{1,0:T(8,128)(2,1)} %copy-done.4) | copy-start | bytes 552964
  23.1 66.7 %all-to-all-start = ((bf16[8,48,1792]{2,1,0:T(8,128)(2,1)}), bf16[8,48,1792]{2,1,0:T(8,128)(2,1)S(1)}, u32[]{:S(2)}, u32[]{:S(2)}) async-start(bf16[8,48,1792]{2,1,0:T(8,128)(2,1)} %get-tuple-element.41), calls=%async_computation | async-start | bytes 2752512 | tf_op jit(solution)/shard_map/all_to_all | solution.py:401
  27.7 15.7 %collective-permute-start.3 = (bf16[48,1920]{1,0:T(8,128)(2,1)S(1)}, bf16[48,1920]{1,0:T(8,128)(2,1)S(1)}, u32[]{:S(2)}, u32[]{:S(2)}) collective-permute-start(bf16[48,1920]{1,0:T(8,128)(2,1)S(1)} %copy-done.5), channel_id=1, source_target_pairs={{0,32},{8,40},{16,48},{24,56},{32,0},{40,8},{48,16},{56,24},{1,33}... | collective-permute-start | bytes 552968 | tf_op jit(solution)/shard_map/ppermute | solution.py:387
  33.0 20.7 %collective-permute-start.2 = (bf16[48,1920]{1,0:T(8,128)(2,1)S(1)}, bf16[48,1920]{1,0:T(8,128)(2,1)S(1)}, u32[]{:S(2)}, u32[]{:S(2)}) collective-permute-start(bf16[48,1920]{1,0:T(8,128)(2,1)S(1)} %copy-done.5), channel_id=1, source_target_pairs={{0,24},{8,32},{16,40},{24,48},{32,56},{40,0},{48,8},{56,16},{1,25}... | collective-permute-start | bytes 552968 | tf_op jit(solution)/shard_map/ppermute | solution.py:387
  34.7 19.0 %collective-permute-start.1 = (bf16[48,1920]{1,0:T(8,128)(2,1)S(1)}, bf16[48,1920]{1,0:T(8,128)(2,1)S(1)}, u32[]{:S(2)}, u32[]{:S(2)}) collective-permute-start(bf16[48,1920]{1,0:T(8,128)(2,1)S(1)} %copy-done.5), channel_id=1, source_target_pairs={{0,40},{8,48},{16,56},{24,0},{32,8},{40,16},{48,24},{56,32},{1,41}... | collective-permute-start | bytes 552968 | tf_op jit(solution)/shard_map/ppermute | solution.py:387
  38.1 23.5 %collective-permute-start = (bf16[48,1920]{1,0:T(8,128)(2,1)S(1)}, bf16[48,1920]{1,0:T(8,128)(2,1)S(1)}, u32[]{:S(2)}, u32[]{:S(2)}) collective-permute-start(bf16[48,1920]{1,0:T(8,128)(2,1)S(1)} %copy-done.5), channel_id=1, source_target_pairs={{0,16},{8,24},{16,32},{24,40},{32,48},{40,56},{48,0},{56,8},{1,17}... | collective-permute-start | bytes 552968 | tf_op jit(solution)/shard_map/ppermute | solution.py:387
  43.4 18.2 %copy-start.28 = (bf16[48,1920]{1,0:T(8,128)(2,1)}, bf16[48,1920]{1,0:T(8,128)(2,1)S(1)}, u32[]{:S(2)}) copy-start(bf16[48,1920]{1,0:T(8,128)(2,1)S(1)} %collective-permute-done.3.refs_3_) | copy-start | bytes 552964
  53.8 7.8 %copy-start.29 = (bf16[48,1920]{1,0:T(8,128)(2,1)}, bf16[48,1920]{1,0:T(8,128)(2,1)S(1)}, u32[]{:S(2)}) copy-start(bf16[48,1920]{1,0:T(8,128)(2,1)S(1)} %collective-permute-done.2.refs_2_) | copy-start | bytes 552964
  53.8 7.8 %copy-start.30 = (bf16[48,1920]{1,0:T(8,128)(2,1)}, bf16[48,1920]{1,0:T(8,128)(2,1)S(1)}, u32[]{:S(2)}) copy-start(bf16[48,1920]{1,0:T(8,128)(2,1)S(1)} %collective-permute-done.1.refs_1_) | copy-start | bytes 552964
  66.3 6.2 %collective-permute-start.7 = (bf16[56,1792]{1,0:T(8,128)(2,1)}, bf16[56,1792]{1,0:T(8,128)(2,1)S(1)}, u32[]{:S(2)}, u32[]{:S(2)}) collective-permute-start(bf16[56,1792]{1,0:T(8,128)(2,1)} %get-tuple-element.43), channel_id=1, source_target_pairs={{0,4},{4,0},{64,68},{68,64},{128,132},{132,128},{192,196},{196,192... | collective-permute-start | bytes 602120 | tf_op jit(solution)/shard_map/ppermute | solution.py:397
  66.4 9.3 %collective-permute-start.8 = (bf16[56,1792]{1,0:T(8,128)(2,1)}, bf16[56,1792]{1,0:T(8,128)(2,1)S(1)}, u32[]{:S(2)}, u32[]{:S(2)}) collective-permute-start(bf16[56,1792]{1,0:T(8,128)(2,1)} %get-tuple-element.44), channel_id=1, source_target_pairs={{0,64},{4,68},{64,128},{68,132},{128,192},{132,196},{192,0},{196,4... | collective-permute-start | bytes 602120 | tf_op jit(solution)/shard_map/ppermute | solution.py:397
  68.1 10.8 %collective-permute-start.9 = (bf16[56,1792]{1,0:T(8,128)(2,1)}, bf16[56,1792]{1,0:T(8,128)(2,1)S(1)}, u32[]{:S(2)}, u32[]{:S(2)}) collective-permute-start(bf16[56,1792]{1,0:T(8,128)(2,1)} %get-tuple-element.45), channel_id=1, source_target_pairs={{0,68},{4,64},{64,132},{68,128},{128,196},{132,192},{192,4},{196,0... | collective-permute-start | bytes 602120 | tf_op jit(solution)/shard_map/ppermute | solution.py:397
  69.3 16.1 %collective-permute-start.10 = (bf16[56,1792]{1,0:T(8,128)(2,1)}, bf16[56,1792]{1,0:T(8,128)(2,1)S(1)}, u32[]{:S(2)}, u32[]{:S(2)}) collective-permute-start(bf16[56,1792]{1,0:T(8,128)(2,1)} %get-tuple-element.46), channel_id=1, source_target_pairs={{0,128},{4,132},{64,192},{68,196},{128,0},{132,4},{192,64},{196,68... | collective-permute-start | bytes 602120 | tf_op jit(solution)/shard_map/ppermute | solution.py:397
  70.9 17.7 %collective-permute-start.11 = (bf16[56,1792]{1,0:T(8,128)(2,1)}, bf16[56,1792]{1,0:T(8,128)(2,1)S(1)}, u32[]{:S(2)}, u32[]{:S(2)}) collective-permute-start(bf16[56,1792]{1,0:T(8,128)(2,1)} %get-tuple-element.47), channel_id=1, source_target_pairs={{0,132},{4,128},{64,196},{68,192},{128,4},{132,0},{192,68},{196,64... | collective-permute-start | bytes 602120 | tf_op jit(solution)/shard_map/ppermute | solution.py:397
  72.6 17.2 %copy-start.11 = (bf16[56,1792]{1,0:T(8,128)(2,1)}, bf16[56,1792]{1,0:T(8,128)(2,1)S(1)}, u32[]{:S(2)}) copy-start(bf16[56,1792]{1,0:T(8,128)(2,1)S(1)} %collective-permute-done.7.refs_1_) | copy-start | bytes 602116
  72.6 16.1 %collective-permute-start.12 = (bf16[56,1792]{1,0:T(8,128)(2,1)}, bf16[56,1792]{1,0:T(8,128)(2,1)S(1)}, u32[]{:S(2)}, u32[]{:S(2)}) collective-permute-start(bf16[56,1792]{1,0:T(8,128)(2,1)} %get-tuple-element.48), channel_id=1, source_target_pairs={{0,192},{4,196},{64,0},{68,4},{128,64},{132,68},{192,128},{196,132... | collective-permute-start | bytes 602120 | tf_op jit(solution)/shard_map/ppermute | solution.py:397
  75.8 14.0 %copy-start.12 = (bf16[56,1792]{1,0:T(8,128)(2,1)}, bf16[56,1792]{1,0:T(8,128)(2,1)S(1)}, u32[]{:S(2)}) copy-start(bf16[56,1792]{1,0:T(8,128)(2,1)S(1)} %collective-permute-done.8.refs_2_) | copy-start | bytes 602116
  75.8 14.0 %collective-permute-start.13 = (bf16[56,1792]{1,0:T(8,128)(2,1)}, bf16[56,1792]{1,0:T(8,128)(2,1)S(1)}, u32[]{:S(2)}, u32[]{:S(2)}) collective-permute-start(bf16[56,1792]{1,0:T(8,128)(2,1)} %get-tuple-element.49), channel_id=1, source_target_pairs={{0,196},{4,192},{64,4},{68,0},{128,68},{132,64},{192,132},{196,128... | collective-permute-start | bytes 602120 | tf_op jit(solution)/shard_map/ppermute | solution.py:397
  79.0 10.8 %copy-start.13 = (bf16[56,1792]{1,0:T(8,128)(2,1)}, bf16[56,1792]{1,0:T(8,128)(2,1)S(1)}, u32[]{:S(2)}) copy-start(bf16[56,1792]{1,0:T(8,128)(2,1)S(1)} %collective-permute-done.9.refs_3_) | copy-start | bytes 602116
  85.5 4.3 %copy-start.14 = (bf16[56,1792]{1,0:T(8,128)(2,1)}, bf16[56,1792]{1,0:T(8,128)(2,1)S(1)}, u32[]{:S(2)}) copy-start(bf16[56,1792]{1,0:T(8,128)(2,1)S(1)} %collective-permute-done.10.refs_4_) | copy-start | bytes 602116
  88.7 1.2 copy-start.15
  88.7 1.2 copy-start.16
  89.8 1.1 copy-start.1
  111.1 28.4 %copy-start.33 = (bf16[192,1024]{1,0:T(8,128)(2,1)S(1)}, bf16[192,1024]{1,0:T(8,128)(2,1)}, u32[]{:S(2)}) copy-start(bf16[192,1024]{1,0:T(8,128)(2,1)} %get-tuple-element.53) | copy-start | bytes 1179652
  111.1 12.9 %collective-permute-start.25 = (bf16[192,1024]{1,0:T(8,128)(2,1)}, bf16[192,1024]{1,0:T(8,128)(2,1)S(1)}, u32[]{:S(2)}, u32[]{:S(2)}) collective-permute-start(bf16[192,1024]{1,0:T(8,128)(2,1)} %get-tuple-element.64), channel_id=1, source_target_pairs={{0,1},{1,2},{2,3},{3,0},{4,5},{5,6},{6,7},{7,4},{8,9},{9,10},{10,1... | collective-permute-start | bytes 1179656 | tf_op jit(solution)/shard_map/ppermute | solution.py:387
  112.7 12.7 %collective-permute-start.27 = (bf16[192,1024]{1,0:T(8,128)(2,1)}, bf16[192,1024]{1,0:T(8,128)(2,1)S(1)}, u32[]{:S(2)}, u32[]{:S(2)}) collective-permute-start(bf16[192,1024]{1,0:T(8,128)(2,1)} %get-tuple-element.65), channel_id=1, source_target_pairs={{0,3},{1,0},{2,1},{3,2},{4,7},{5,4},{6,5},{7,6},{8,11},{9,8},{10,9... | collective-permute-start | bytes 1179656 | tf_op jit(solution)/shard_map/ppermute | solution.py:387
  125.0 7.9 %collective-permute-start.26 = (bf16[96,1024]{1,0:T(8,128)(2,1)S(1)}, bf16[96,1024]{1,0:T(8,128)(2,1)S(1)}, u32[]{:S(2)}, u32[]{:S(2)}) collective-permute-start(bf16[96,1024]{1,0:T(8,128)(2,1)S(1)} %add_convert_fusion.1), channel_id=1, source_target_pairs={{0,1},{1,2},{2,3},{3,0},{4,5},{5,6},{6,7},{7,4},{8,9},{9,10},{10,1... | collective-permute-start | bytes 589832 | tf_op jit(solution)/shard_map/ppermute | solution.py:387
  126.4 6.6 %collective-permute-start.28 = (bf16[96,1024]{1,0:T(8,128)(2,1)S(1)}, bf16[96,1024]{1,0:T(8,128)(2,1)S(1)}, u32[]{:S(2)}, u32[]{:S(2)}) collective-permute-start(bf16[96,1024]{1,0:T(8,128)(2,1)S(1)} %add_convert_fusion), channel_id=1, source_target_pairs={{0,3},{1,0},{2,1},{3,2},{4,7},{5,4},{6,5},{7,6},{8,11},{9,8},{10,9... | collective-permute-start | bytes 589832 | tf_op jit(solution)/shard_map/ppermute | solution.py:387
  129.4 30.1 %collective-permute-start.14 = (bf16[192,1024]{1,0:T(8,128)(2,1)}, bf16[192,1024]{1,0:T(8,128)(2,1)S(1)}, u32[]{:S(2)}, u32[]{:S(2)}) collective-permute-start(bf16[192,1024]{1,0:T(8,128)(2,1)} %get-tuple-element.52), channel_id=1, source_target_pairs={{0,1},{1,2},{2,3},{3,0},{4,5},{5,6},{6,7},{7,4},{8,9},{9,10},{10,1... | collective-permute-start | bytes 1179656 | tf_op jit(solution)/shard_map/ppermute | solution.py:387
  134.3 15.3 %copy-start.6 = (bf16[96,1024]{1,0:T(8,128)(2,1)}, bf16[96,1024]{1,0:T(8,128)(2,1)S(1)}, u32[]{:S(2)}) copy-start(bf16[96,1024]{1,0:T(8,128)(2,1)S(1)} %multiply_convert_fusion.refs_0_) | copy-start | bytes 589828
  134.3 15.3 %collective-permute-start.31 = (bf16[96,1024]{1,0:T(8,128)(2,1)S(1)}, bf16[96,1024]{1,0:T(8,128)(2,1)S(1)}, u32[]{:S(2)}, u32[]{:S(2)}) collective-permute-start(bf16[96,1024]{1,0:T(8,128)(2,1)S(1)} %multiply_convert_fusion.refs_0_), channel_id=1, source_target_pairs={{0,1},{1,2},{2,3},{3,0},{4,5},{5,6},{6,7},{7,4},{8,9},{9,10},{10,1... | collective-permute-start | bytes 589832 | tf_op jit(solution)/shard_map/ppermute | solution.py:387
  135.4 14.2 %collective-permute-start.30 = (bf16[96,1024]{1,0:T(8,128)(2,1)S(1)}, bf16[96,1024]{1,0:T(8,128)(2,1)S(1)}, u32[]{:S(2)}, u32[]{:S(2)}) collective-permute-start(bf16[96,1024]{1,0:T(8,128)(2,1)S(1)} %multiply_convert_fusion.refs_0_), channel_id=1, source_target_pairs={{0,2},{1,3},{2,0},{3,1},{4,6},{5,7},{6,4},{7,5},{8,10},{9,11},{10,... | collective-permute-start | bytes 589832 | tf_op jit(solution)/shard_map/ppermute | solution.py:387
  139.5 10.0 %collective-permute-start.29 = (bf16[96,1024]{1,0:T(8,128)(2,1)S(1)}, bf16[96,1024]{1,0:T(8,128)(2,1)S(1)}, u32[]{:S(2)}, u32[]{:S(2)}) collective-permute-start(bf16[96,1024]{1,0:T(8,128)(2,1)S(1)} %multiply_convert_fusion.refs_0_), channel_id=1, source_target_pairs={{0,3},{1,0},{2,1},{3,2},{4,7},{5,4},{6,5},{7,6},{8,11},{9,8},{10,9... | collective-permute-start | bytes 589832 | tf_op jit(solution)/shard_map/ppermute | solution.py:387
  139.5 20.2 %collective-permute-start.16 = (bf16[192,1024]{1,0:T(8,128)(2,1)S(1)}, bf16[192,1024]{1,0:T(8,128)(2,1)S(1)}, u32[]{:S(2)}, u32[]{:S(2)}) collective-permute-start(bf16[192,1024]{1,0:T(8,128)(2,1)S(1)} %copy-done.33), channel_id=1, source_target_pairs={{0,3},{1,0},{2,1},{3,2},{4,7},{5,4},{6,5},{7,6},{8,11},{9,8},{10,9... | collective-permute-start | bytes 1179656 | tf_op jit(solution)/shard_map/ppermute | solution.py:387
  155.4 4.1 %copy-start.25 = (bf16[96,1024]{1,0:T(8,128)(2,1)S(1)}, bf16[96,1024]{1,0:T(8,128)(2,1)}, u32[]{:S(2)}) copy-start(bf16[96,1024]{1,0:T(8,128)(2,1)} %get-tuple-element.51) | copy-start | bytes 589828
  155.4 4.3 %copy-start.24 = (bf16[96,1024]{1,0:T(8,128)(2,1)S(1)}, bf16[96,1024]{1,0:T(8,128)(2,1)}, u32[]{:S(2)}) copy-start(bf16[96,1024]{1,0:T(8,128)(2,1)} %get-tuple-element.55) | copy-start | bytes 589828
  155.4 16.2 %all-to-all-start.2 = ((bf16[8,24,1792]{2,1,0:T(8,128)(2,1)}), bf16[8,24,1792]{2,1,0:T(8,128)(2,1)S(1)}, u32[]{:S(2)}, u32[]{:S(2)}) async-start(bf16[8,24,1792]{2,1,0:T(8,128)(2,1)} %get-tuple-element.68), calls=%async_computation.2 | async-start | bytes 1376256 | tf_op jit(solution)/shard_map/all_to_all | solution.py:401
  159.5 15.6 %copy-start.26 = (bf16[96,1024]{1,0:T(8,128)(2,1)S(1)}, bf16[96,1024]{1,0:T(8,128)(2,1)}, u32[]{:S(2)}) copy-start(bf16[96,1024]{1,0:T(8,128)(2,1)} %get-tuple-element.50) | copy-start | bytes 589828
  159.5 15.7 %copy-start.27 = (bf16[96,1024]{1,0:T(8,128)(2,1)S(1)}, bf16[96,1024]{1,0:T(8,128)(2,1)}, u32[]{:S(2)}) copy-start(bf16[96,1024]{1,0:T(8,128)(2,1)} %get-tuple-element.54) | copy-start | bytes 589828
  159.6 15.5 %collective-permute-start.15 = (bf16[96,1024]{1,0:T(8,128)(2,1)S(1)}, bf16[96,1024]{1,0:T(8,128)(2,1)S(1)}, u32[]{:S(2)}, u32[]{:S(2)}) collective-permute-start(bf16[96,1024]{1,0:T(8,128)(2,1)S(1)} %add_convert_fusion.3), channel_id=1, source_target_pairs={{0,1},{1,2},{2,3},{3,0},{4,5},{5,6},{6,7},{7,4},{8,9},{9,10},{10,1... | collective-permute-start | bytes 589832 | tf_op jit(solution)/shard_map/ppermute | solution.py:387
  159.8 15.4 %collective-permute-start.17 = (bf16[96,1024]{1,0:T(8,128)(2,1)S(1)}, bf16[96,1024]{1,0:T(8,128)(2,1)S(1)}, u32[]{:S(2)}, u32[]{:S(2)}) collective-permute-start(bf16[96,1024]{1,0:T(8,128)(2,1)S(1)} %add_convert_fusion.2), channel_id=1, source_target_pairs={{0,3},{1,0},{2,1},{3,2},{4,7},{5,4},{6,5},{7,6},{8,11},{9,8},{10,9... | collective-permute-start | bytes 589832 | tf_op jit(solution)/shard_map/ppermute | solution.py:387
  171.6 3.8 %copy-start.2 = (bf16[8,24,1792]{2,1,0:T(8,128)(2,1)}, bf16[8,24,1792]{2,1,0:T(8,128)(2,1)S(1)}, u32[]{:S(2)}) copy-start(bf16[8,24,1792]{2,1,0:T(8,128)(2,1)S(1)} %all-to-all-done.2) | copy-start | bytes 2064388
  171.6 23.0 %all-to-all-start.3 = ((bf16[8,24,1792]{2,1,0:T(8,128)(2,1)}), bf16[8,24,1792]{2,1,0:T(8,128)(2,1)S(1)}, u32[]{:S(2)}, u32[]{:S(2)}) async-start(bf16[8,24,1792]{2,1,0:T(8,128)(2,1)} %get-tuple-element.72), calls=%async_computation.3 | async-start | bytes 1376256 | tf_op jit(solution)/shard_map/all_to_all | solution.py:401
  175.4 13.3 %copy-start.7 = (bf16[96,1024]{1,0:T(8,128)(2,1)}, bf16[96,1024]{1,0:T(8,128)(2,1)S(1)}, u32[]{:S(2)}) copy-start(bf16[96,1024]{1,0:T(8,128)(2,1)S(1)} %multiply_convert_fusion.1.refs_0_) | copy-start | bytes 589828
  175.4 12.7 %collective-permute-start.20 = (bf16[96,1024]{1,0:T(8,128)(2,1)S(1)}, bf16[96,1024]{1,0:T(8,128)(2,1)S(1)}, u32[]{:S(2)}, u32[]{:S(2)}) collective-permute-start(bf16[96,1024]{1,0:T(8,128)(2,1)S(1)} %multiply_convert_fusion.1.refs_0_), channel_id=1, source_target_pairs={{0,1},{1,2},{2,3},{3,0},{4,5},{5,6},{6,7},{7,4},{8,9},{9,10},{10,1... | collective-permute-start | bytes 589832 | tf_op jit(solution)/shard_map/ppermute | solution.py:387
  175.5 12.6 %collective-permute-start.19 = (bf16[96,1024]{1,0:T(8,128)(2,1)S(1)}, bf16[96,1024]{1,0:T(8,128)(2,1)S(1)}, u32[]{:S(2)}, u32[]{:S(2)}) collective-permute-start(bf16[96,1024]{1,0:T(8,128)(2,1)S(1)} %multiply_convert_fusion.1.refs_0_), channel_id=1, source_target_pairs={{0,2},{1,3},{2,0},{3,1},{4,6},{5,7},{6,4},{7,5},{8,10},{9,11},{10,... | collective-permute-start | bytes 589832 | tf_op jit(solution)/shard_map/ppermute | solution.py:387
  177.4 11.4 %collective-permute-start.18 = (bf16[96,1024]{1,0:T(8,128)(2,1)S(1)}, bf16[96,1024]{1,0:T(8,128)(2,1)S(1)}, u32[]{:S(2)}, u32[]{:S(2)}) collective-permute-start(bf16[96,1024]{1,0:T(8,128)(2,1)S(1)} %multiply_convert_fusion.1.refs_0_), channel_id=1, source_target_pairs={{0,3},{1,0},{2,1},{3,2},{4,7},{5,4},{6,5},{7,6},{8,11},{9,8},{10,9... | collective-permute-start | bytes 589832 | tf_op jit(solution)/shard_map/ppermute | solution.py:387
  194.6 0.8 copy-start.3
  195.4 23.9 %all-to-all-start.1 = ((bf16[8,48,1792]{2,1,0:T(8,128)(2,1)}), bf16[8,48,1792]{2,1,0:T(8,128)(2,1)S(1)}, u32[]{:S(2)}, u32[]{:S(2)}) async-start(bf16[8,48,1792]{2,1,0:T(8,128)(2,1)} %bitcast.16), calls=%async_computation.1 | async-start | bytes 2752512 | tf_op jit(solution)/shard_map/all_to_all | solution.py:401
  202.0 53.1 %copy-start.32 = (bf16[48,1792]{1,0:T(8,128)(2,1)S(1)}, bf16[48,1792]{1,0:T(8,128)(2,1)}, u32[]{:S(2)}) copy-start(bf16[48,1792]{1,0:T(8,128)(2,1)} %get-tuple-element.73) | copy-start | bytes 516100
  202.0 26.1 %collective-permute-start.34 = (bf16[48,1792]{1,0:T(8,128)(2,1)}, bf16[48,1792]{1,0:T(8,128)(2,1)S(1)}, u32[]{:S(2)}, u32[]{:S(2)}) collective-permute-start(bf16[48,1792]{1,0:T(8,128)(2,1)} %get-tuple-element.74), channel_id=1, source_target_pairs={{0,8},{8,16},{16,24},{24,32},{32,40},{40,48},{48,56},{56,0},{1,9},... | collective-permute-start | bytes 516104 | tf_op jit(solution)/shard_map/ppermute | solution.py:387
  205.7 25.7 %collective-permute-start.32 = (bf16[48,1792]{1,0:T(8,128)(2,1)}, bf16[48,1792]{1,0:T(8,128)(2,1)S(1)}, u32[]{:S(2)}, u32[]{:S(2)}) collective-permute-start(bf16[48,1792]{1,0:T(8,128)(2,1)} %get-tuple-element.69), channel_id=1, source_target_pairs={{0,56},{8,0},{16,8},{24,16},{32,24},{40,32},{48,40},{56,48},{1,57}... | collective-permute-start | bytes 516104 | tf_op jit(solution)/shard_map/ppermute | solution.py:387
  206.1 27.8 %collective-permute-start.33 = (bf16[48,1792]{1,0:T(8,128)(2,1)}, bf16[48,1792]{1,0:T(8,128)(2,1)S(1)}, u32[]{:S(2)}, u32[]{:S(2)}) collective-permute-start(bf16[48,1792]{1,0:T(8,128)(2,1)} %get-tuple-element.70), channel_id=1, source_target_pairs={{0,16},{8,24},{16,32},{24,40},{32,48},{40,56},{48,0},{56,8},{1,17}... | collective-permute-start | bytes 516104 | tf_op jit(solution)/shard_map/ppermute | solution.py:387
  219.3 1.1 copy-start
  222.9 16.2 %collective-permute-start.21 = (bf16[48,1792]{1,0:T(8,128)(2,1)}, bf16[48,1792]{1,0:T(8,128)(2,1)S(1)}, u32[]{:S(2)}, u32[]{:S(2)}) collective-permute-start(bf16[48,1792]{1,0:T(8,128)(2,1)} %get-tuple-element.56), channel_id=1, source_target_pairs={{0,48},{8,56},{16,0},{24,8},{32,16},{40,24},{48,32},{56,40},{1,49}... | collective-permute-start | bytes 516104 | tf_op jit(solution)/shard_map/ppermute | solution.py:387
  226.3 15.8 %collective-permute-start.22 = (bf16[48,1792]{1,0:T(8,128)(2,1)}, bf16[48,1792]{1,0:T(8,128)(2,1)S(1)}, u32[]{:S(2)}, u32[]{:S(2)}) collective-permute-start(bf16[48,1792]{1,0:T(8,128)(2,1)} %get-tuple-element.57), channel_id=1, source_target_pairs={{0,24},{8,32},{16,40},{24,48},{32,56},{40,0},{48,8},{56,16},{1,25}... | collective-permute-start | bytes 516104 | tf_op jit(solution)/shard_map/ppermute | solution.py:387
  228.1 18.3 %collective-permute-start.23 = (bf16[48,1792]{1,0:T(8,128)(2,1)}, bf16[48,1792]{1,0:T(8,128)(2,1)S(1)}, u32[]{:S(2)}, u32[]{:S(2)}) collective-permute-start(bf16[48,1792]{1,0:T(8,128)(2,1)} %get-tuple-element.58), channel_id=1, source_target_pairs={{0,40},{8,48},{16,56},{24,0},{32,8},{40,16},{48,24},{56,32},{1,41}... | collective-permute-start | bytes 516104 | tf_op jit(solution)/shard_map/ppermute | solution.py:387
  231.3 23.8 %collective-permute-start.24 = (bf16[48,1792]{1,0:T(8,128)(2,1)}, bf16[48,1792]{1,0:T(8,128)(2,1)S(1)}, u32[]{:S(2)}, u32[]{:S(2)}) collective-permute-start(bf16[48,1792]{1,0:T(8,128)(2,1)} %get-tuple-element.59), channel_id=1, source_target_pairs={{0,32},{8,40},{16,48},{24,56},{32,0},{40,8},{48,16},{56,24},{1,33}... | collective-permute-start | bytes 516104 | tf_op jit(solution)/shard_map/ppermute | solution.py:387
  (9 other events, 6.4 us)

commit v2 on v1

--- a/solution.py
+++ b/solution.py
@@ -311,9 +311,12 @@
 
 def down_kernel(split, place_ref, down_ref, *refs):
     outs, all_ref = refs[NX:-1], refs[-1]
-    for j in range(NX):
-        at = pl.multiple_of(lax.rem(place_ref[0] + j, NX) * SHARE, 16)
-        all_ref[pl.ds(at, SHARE), :] = refs[j][...]
+
+    @pl.when(pl.program_id(0) == 0)
+    def _():
+        for j in range(NX):
+            at = pl.multiple_of(lax.rem(place_ref[0] + j, NX) * SHARE, 16)
+            all_ref[pl.ds(at, SHARE), :] = refs[j][...]
 
     result = jnp.dot(all_ref[...], down_ref[...], preferred_element_type=F32)
     if not split:
@@ -327,11 +330,19 @@
 
 def expert_out(place, down, pieces, split):
     hidden, width = down.shape
-    shapes = [shape_of(PEERS, SPAN, width)] * 2 if split else [shape_of(ROWS, width)]
+    part = width // 2
+    if split:
+        shapes = [shape_of(PEERS, SPAN, width)] * 2
+        specs = [pl.BlockSpec((PEERS, SPAN, part), lambda j: (0, 0, j))] * 2
+    else:
+        shapes = [shape_of(ROWS, width)]
+        specs = [pl.BlockSpec((ROWS, part), lambda j: (0, j))]
     return pl.pallas_call(
         functools.partial(down_kernel, split),
-        in_specs=[whole(SMEM)] + [whole()] * (1 + NX),
-        out_specs=[whole()] * len(shapes),
+        grid=(2,),
+        in_specs=[whole(SMEM), pl.BlockSpec((hidden, part), lambda j: (0, j))]
+        + [pl.BlockSpec((SHARE, hidden), lambda j: (0, 0))] * NX,
+        out_specs=specs,
         out_shape=shapes,
         scratch_shapes=[VMEM((ROWS, hidden), BF)],
         name="expert_out",

time: 257 us -> 256 us (level)
  no operation moved by 1% of the time
where the time goes in v2:
time: 256 us; the launch traced here: 255 us
  waiting for transfers between devices  117 us (46%)
  starting transfers between devices  80.4 us (31%)
  Pallas kernels  43.8 us (17%)
  other arithmetic  7.35 us (3%)
  local copies, waits for them, and re-layouts  6.14 us (2%)
    ppermute x28, waiting for transfers between devices, ring(): lax.ppermute(value, axis, [(i, (i + shift) % size) for i in range(size)])  83.2 us
    ppermute x28, starting transfers between devices, ring(): lax.ppermute(value, axis, [(i, (i + shift) % size) for i in range(size)])  55.5 us
    all_to_all x4, waiting for transfers between devices, swap_rows(): back = lax.all_to_all(rows, OWNERS, 0, 0, tiled=True)  18.2 us
    all_to_all x4, starting transfers between devices, swap_rows(): back = lax.all_to_all(rows, OWNERS, 0, 0, tiled=True)  16.7 us
    ppermute x7, waiting for transfers between devices, to_peer(): return lax.ppermute(value, OWNERS, pairs)  15.2 us
    pallas_call x1, Pallas kernels, expert_in(): pl.pallas_call(functools.partial(expert_kernel, count), in_specs=[whole(S...  11.4 us
    pallas_call x2, Pallas kernels, expert_out(): pl.pallas_call(functools.partial(down_kernel, split), grid=(2,), in_specs...  9.25 us
    pallas_call x1, Pallas kernels, expert_later(): pl.pallas_call(later_kernel, in_specs=[whole(), whole(pl.ANY), whole(pl.A...  8.79 us
  transfers between devices with their start and end apart: 39, of which 22 were waited for; matrix products, arithmetic and copies ran while one was open for 2% of the time, Pallas kernels for 8%

profile of v2, /device:TPU:32, one launch (start us, length us, event | category | flops | bytes accessed | tf_op | source)
XLA Modules:
  0.0 255.2 jit_solution(17136797561503938023)
XLA Ops:
  2.1 0.9 fusion.1.refs_4_.refs_0_
  3.1 5.5 %collective-permute-start.6 = (bf16[48,1920]{1,0:T(8,128)(2,1)S(1)}, bf16[48,1920]{1,0:T(8,128)(2,1)S(1)}, u32[]{:S(2)}, u32[]{:S(2)}) collective-permute-start(bf16[48,1920]{1,0:T(8,128)(2,1)S(1)} %fusion.1.refs_4_.refs_0_), channel_id=1, source_target_pairs={{0,48},{8,56},{16,0},{24,8},{32,16},{40,24},{48,32},{56,40},{1,49}... | collective-permute-start | bytes 552968 | tf_op jit(solution)/shard_map/ppermute | solution.py:398
  8.5 2.0 collective-permute-start.4
  11.2 4.1 %collective-permute-done.6.refs_7_.refs_3_ = bf16[48,1920]{1,0:T(8,128)(2,1)S(1)} collective-permute-done((bf16[48,1920]{1,0:T(8,128)(2,1)S(1)}, bf16[48,1920]{1,0:T(8,128)(2,1)S(1)}, u32[]{:S(2)}, u32[]{:S(2)}) %collective-permute-start.6) | collective-permute-done | bytes 184352 | tf_op jit(solution)/shard_map/ppermute | solution.py:398
  15.3 3.5 %collective-permute-done.4.refs_5_.refs_1_ = bf16[48,1920]{1,0:T(8,128)(2,1)S(1)} collective-permute-done((bf16[48,1920]{1,0:T(8,128)(2,1)S(1)}, bf16[48,1920]{1,0:T(8,128)(2,1)S(1)}, u32[]{:S(2)}, u32[]{:S(2)}) %collective-permute-start.4) | collective-permute-done | bytes 184352 | tf_op jit(solution)/shard_map/ppermute | solution.py:398
  19.6 3.5 %dispatch.3 = (bf16[8,48,1792]{2,1,0:T(8,128)(2,1)}, bf16[96,192]{1,0:T(8,128)(2,1)}, bf16[96,192]{1,0:T(8,128)(2,1)}) custom-call(s32[4]{0:T(128)} %pad_add_fusion.place_ref, f32[8,192]{1,0:T(8,128)} %constant.26.clone.table_ref, bf16[48,1920]{1,0:T(8,128)(2,1)} %copy-done.4, bf16[48,1920]{1,0:T(8,128)(2,1)} %copy-done.10, bf16[48,1920]{1,0:T(8,128)(2,1)} %copy-done.9, ...), custom_call_target="tpu_custom_call" | custom-call | tf_op jit(solution)/shard_map/dispatch/pallas_call | solution.py:144
  23.1 4.6 %all-to-all-start = ((bf16[8,48,1792]{2,1,0:T(8,128)(2,1)}), bf16[8,48,1792]{2,1,0:T(8,128)(2,1)S(1)}, u32[]{:S(2)}, u32[]{:S(2)}) async-start(bf16[8,48,1792]{2,1,0:T(8,128)(2,1)} %get-tuple-element.41), calls=%async_computation | async-start | bytes 2752512 | tf_op jit(solution)/shard_map/all_to_all | solution.py:412
  27.7 5.4 %collective-permute-start.3 = (bf16[48,1920]{1,0:T(8,128)(2,1)S(1)}, bf16[48,1920]{1,0:T(8,128)(2,1)S(1)}, u32[]{:S(2)}, u32[]{:S(2)}) collective-permute-start(bf16[48,1920]{1,0:T(8,128)(2,1)S(1)} %copy-done.5), channel_id=1, source_target_pairs={{0,32},{8,40},{16,48},{24,56},{32,0},{40,8},{48,16},{56,24},{1,33}... | collective-permute-start | bytes 552968 | tf_op jit(solution)/shard_map/ppermute | solution.py:398
  33.0 1.7 collective-permute-start.2
  34.7 3.4 %collective-permute-start.1 = (bf16[48,1920]{1,0:T(8,128)(2,1)S(1)}, bf16[48,1920]{1,0:T(8,128)(2,1)S(1)}, u32[]{:S(2)}, u32[]{:S(2)}) collective-permute-start(bf16[48,1920]{1,0:T(8,128)(2,1)S(1)} %copy-done.5), channel_id=1, source_target_pairs={{0,40},{8,48},{16,56},{24,0},{32,8},{40,16},{48,24},{56,32},{1,41}... | collective-permute-start | bytes 552968 | tf_op jit(solution)/shard_map/ppermute | solution.py:398
  38.1 1.5 collective-permute-start
  39.6 3.8 %collective-permute-done.3.refs_3_ = bf16[48,1920]{1,0:T(8,128)(2,1)S(1)} collective-permute-done((bf16[48,1920]{1,0:T(8,128)(2,1)S(1)}, bf16[48,1920]{1,0:T(8,128)(2,1)S(1)}, u32[]{:S(2)}, u32[]{:S(2)}) %collective-permute-start.3) | collective-permute-done | bytes 184352 | tf_op jit(solution)/shard_map/ppermute | solution.py:398
  43.4 10.4 %collective-permute-done.2.refs_2_ = bf16[48,1920]{1,0:T(8,128)(2,1)S(1)} collective-permute-done((bf16[48,1920]{1,0:T(8,128)(2,1)S(1)}, bf16[48,1920]{1,0:T(8,128)(2,1)S(1)}, u32[]{:S(2)}, u32[]{:S(2)}) %collective-permute-start.2) | collective-permute-done | bytes 184352 | tf_op jit(solution)/shard_map/ppermute | solution.py:398
  53.8 7.8 %collective-permute-done.refs_0_ = bf16[48,1920]{1,0:T(8,128)(2,1)S(1)} collective-permute-done((bf16[48,1920]{1,0:T(8,128)(2,1)S(1)}, bf16[48,1920]{1,0:T(8,128)(2,1)S(1)}, u32[]{:S(2)}, u32[]{:S(2)}) %collective-permute-start) | collective-permute-done | bytes 184352 | tf_op jit(solution)/shard_map/ppermute | solution.py:398
  62.3 4.1 %dispatch.2 = (bf16[56,1792]{1,0:T(8,128)(2,1)}, bf16[56,1792]{1,0:T(8,128)(2,1)}, bf16[56,1792]{1,0:T(8,128)(2,1)}, bf16[56,1792]{1,0:T(8,128)(2,1)}, bf16[56,1...) custom-call(s32[4]{0:T(128)} %pad_add_fusion.place_ref, ...), custom_call_target="tpu_custom_call" | custom-call | tf_op jit(solution)/shard_map/dispatch/pallas_call | solution.py:144
  66.4 1.7 collective-permute-start.8
  68.1 1.2 collective-permute-start.9
  69.3 1.6 collective-permute-start.10
  70.9 1.6 collective-permute-start.11
  72.6 1.8 collective-permute-start.12
  74.3 1.4 collective-permute-done.8.refs_2_
  76.0 2.9 %collective-permute-done.9.refs_3_ = bf16[56,1792]{1,0:T(8,128)(2,1)S(1)} collective-permute-done((bf16[56,1792]{1,0:T(8,128)(2,1)}, bf16[56,1792]{1,0:T(8,128)(2,1)S(1)}, u32[]{:S(2)}, u32[]{:S(2)}) %collective-permute-start.9) | collective-permute-done | bytes 200736 | tf_op jit(solution)/shard_map/ppermute | solution.py:408
  79.0 6.5 %collective-permute-done.10.refs_4_ = bf16[56,1792]{1,0:T(8,128)(2,1)S(1)} collective-permute-done((bf16[56,1792]{1,0:T(8,128)(2,1)}, bf16[56,1792]{1,0:T(8,128)(2,1)S(1)}, u32[]{:S(2)}, u32[]{:S(2)}) %collective-permute-start.10) | collective-permute-done | bytes 200736 | tf_op jit(solution)/shard_map/ppermute | solution.py:408
  85.5 3.2 %collective-permute-done.11.refs_5_ = bf16[56,1792]{1,0:T(8,128)(2,1)S(1)} collective-permute-done((bf16[56,1792]{1,0:T(8,128)(2,1)}, bf16[56,1792]{1,0:T(8,128)(2,1)S(1)}, u32[]{:S(2)}, u32[]{:S(2)}) %collective-permute-start.11) | collective-permute-done | bytes 200736 | tf_op jit(solution)/shard_map/ppermute | solution.py:408
  88.7 1.1 collective-permute-done.13.refs_7_
  90.9 11.4 %expert_in.1 = (bf16[192,1024]{1,0:T(8,128)(2,1)}, bf16[192,1024]{1,0:T(8,128)(2,1)}, bf16[96,1024]{1,0:T(8,128)(2,1)}, bf16[96,1024]{1,0:T(8,128)(2,1)}, bf16[9...) custom-call(s32[4]{0:T(128)} %pad_add_fusion.place_ref, f32[16]{0:T(128)} %edges_ref.1, ...), custom_call_target="tpu_custom_call" | custom-call | tf_op jit(solution)/shard_map/expert_in/pallas_call | solution.py:270
  102.3 8.8 %expert_later.1 = (bf16[192,1024]{1,0:T(8,128)(2,1)}, bf16[192,1024]{1,0:T(8,128)(2,1)}, bf16[96,1024]{1,0:T(8,128)(2,1)}, bf16[96,1024]{1,0:T(8,128)(2,1)}, bf1...) custom-call(bf16[384,1792]{1,0:T(8,128)(2,1)} %get-tuple-element.61.block_ref, bf16[1792,1024]{1,0:T(8,128)(2,1)} %bitcast.11, ...), custom_call_target="tpu_custom_call" | custom-call | tf_op jit(solution)/shard_map/expert_later/pallas_call | solution.py:298
  111.1 1.6 collective-permute-start.25
  112.7 1.7 collective-permute-start.27
  114.4 9.6 %collective-permute-done.25 = bf16[192,1024]{1,0:T(8,128)(2,1)S(1)} collective-permute-done((bf16[192,1024]{1,0:T(8,128)(2,1)}, bf16[192,1024]{1,0:T(8,128)(2,1)S(1)}, u32[]{:S(2)}, u32[]{:S(2)}) %collective-permute-start.25) | collective-permute-done | bytes 393248 | tf_op jit(solution)/shard_map/ppermute | solution.py:398
  124.1 1.0 add_convert_fusion.1
  125.4 1.0 add_convert_fusion
  126.4 3.0 %collective-permute-start.28 = (bf16[96,1024]{1,0:T(8,128)(2,1)S(1)}, bf16[96,1024]{1,0:T(8,128)(2,1)S(1)}, u32[]{:S(2)}, u32[]{:S(2)}) collective-permute-start(bf16[96,1024]{1,0:T(8,128)(2,1)S(1)} %add_convert_fusion), channel_id=1, source_target_pairs={{0,3},{1,0},{2,1},{3,2},{4,7},{5,4},{6,5},{7,6},{8,11},{9,8},{10,9... | collective-permute-start | bytes 589832 | tf_op jit(solution)/shard_map/ppermute | solution.py:398
  129.4 3.5 %collective-permute-done.26 = bf16[96,1024]{1,0:T(8,128)(2,1)S(1)} collective-permute-done((bf16[96,1024]{1,0:T(8,128)(2,1)S(1)}, bf16[96,1024]{1,0:T(8,128)(2,1)S(1)}, u32[]{:S(2)}, u32[]{:S(2)}) %collective-permute-start.26) | collective-permute-done | bytes 196640 | tf_op jit(solution)/shard_map/ppermute | solution.py:398
  133.0 1.2 multiply_convert_fusion.refs_0_
  134.3 1.1 collective-permute-start.31
  135.4 4.1 %collective-permute-start.30 = (bf16[96,1024]{1,0:T(8,128)(2,1)S(1)}, bf16[96,1024]{1,0:T(8,128)(2,1)S(1)}, u32[]{:S(2)}, u32[]{:S(2)}) collective-permute-start(bf16[96,1024]{1,0:T(8,128)(2,1)S(1)} %multiply_convert_fusion.refs_0_), channel_id=1, source_target_pairs={{0,2},{1,3},{2,0},{3,1},{4,6},{5,7},{6,4},{7,5},{8,10},{9,11},{10,... | collective-permute-start | bytes 589832 | tf_op jit(solution)/shard_map/ppermute | solution.py:398
  140.1 9.5 %collective-permute-done.31.refs_3_ = bf16[96,1024]{1,0:T(8,128)(2,1)S(1)} collective-permute-done((bf16[96,1024]{1,0:T(8,128)(2,1)S(1)}, bf16[96,1024]{1,0:T(8,128)(2,1)S(1)}, u32[]{:S(2)}, u32[]{:S(2)}) %collective-permute-start.31) | collective-permute-done | bytes 196640 | tf_op jit(solution)/shard_map/ppermute | solution.py:398
  150.4 4.6 %expert_out.3 = (bf16[8,24,1792]{2,1,0:T(8,128)(2,1)}, bf16[8,24,1792]{2,1,0:T(8,128)(2,1)}) custom-call(s32[4]{0:T(128)} %pad_add_fusion.place_ref, bf16[1024,1792]{1,0:T(8,128)(2,1)} %bitcast.14, bf16[96,1024]{1,0:T(8,128)(2,1)} %copy-done.6, bf16[96,1024]{1,0:T(8,128)(2,1)} %copy-done.20, bf16[96,1024]{1,0:T(8,128)(2,1)} %copy-done.19, ...), custom_call_target="tpu_custom_call" | custom-call | tf_op jit(solution)/shard_map/expert_out/pallas_call | solution.py:340
  155.0 4.1 %all-to-all-start.2 = ((bf16[8,24,1792]{2,1,0:T(8,128)(2,1)}), bf16[8,24,1792]{2,1,0:T(8,128)(2,1)S(1)}, u32[]{:S(2)}, u32[]{:S(2)}) async-start(bf16[8,24,1792]{2,1,0:T(8,128)(2,1)} %get-tuple-element.68), calls=%async_computation.2 | async-start | bytes 1376256 | tf_op jit(solution)/shard_map/all_to_all | solution.py:412
  159.4 3.5 %collective-permute-start.17 = (bf16[96,1024]{1,0:T(8,128)(2,1)S(1)}, bf16[96,1024]{1,0:T(8,128)(2,1)S(1)}, u32[]{:S(2)}, u32[]{:S(2)}) collective-permute-start(bf16[96,1024]{1,0:T(8,128)(2,1)S(1)} %add_convert_fusion.2), channel_id=1, source_target_pairs={{0,3},{1,0},{2,1},{3,2},{4,7},{5,4},{6,5},{7,6},{8,11},{9,8},{10,9... | collective-permute-start | bytes 589832 | tf_op jit(solution)/shard_map/ppermute | solution.py:398
  162.9 8.3 %all-to-all-done.2 = bf16[8,24,1792]{2,1,0:T(8,128)(2,1)S(1)} async-done(((bf16[8,24,1792]{2,1,0:T(8,128)(2,1)}), bf16[8,24,1792]{2,1,0:T(8,128)(2,1)S(1)}, u32[]{:S(2)}, u32[]{:S(2)}) %all-to-all-start.2) | async-done | bytes 688160 | tf_op jit(solution)/shard_map/all_to_all | solution.py:412
  171.2 3.5 %all-to-all-start.3 = ((bf16[8,24,1792]{2,1,0:T(8,128)(2,1)}), bf16[8,24,1792]{2,1,0:T(8,128)(2,1)S(1)}, u32[]{:S(2)}, u32[]{:S(2)}) async-start(bf16[8,24,1792]{2,1,0:T(8,128)(2,1)} %get-tuple-element.72), calls=%async_computation.3 | async-start | bytes 1376256 | tf_op jit(solution)/shard_map/all_to_all | solution.py:412
  175.1 1.8 collective-permute-start.19
  177.0 1.8 collective-permute-start.18
  178.7 9.0 %collective-permute-done.20.refs_3_ = bf16[96,1024]{1,0:T(8,128)(2,1)S(1)} collective-permute-done((bf16[96,1024]{1,0:T(8,128)(2,1)S(1)}, bf16[96,1024]{1,0:T(8,128)(2,1)S(1)}, u32[]{:S(2)}, u32[]{:S(2)}) %collective-permute-start.20) | collective-permute-done | bytes 196640 | tf_op jit(solution)/shard_map/ppermute | solution.py:398
  189.2 4.6 %expert_out.2 = bf16[384,1792]{1,0:T(8,128)(2,1)} custom-call(s32[4]{0:T(128)} %pad_add_fusion.place_ref, bf16[1024,1792]{1,0:T(8,128)(2,1)} %bitcast.15, bf16[96,1024]{1,0:T(8,128)(2,1)} %copy-done.7, bf16[96,1024]{1,0:T(8,128)(2,1)} %copy-done.23, bf16[96,1024]{1,0:T(8,128)(2,1)} %copy-done.22, bf16[96,1024]{1,0:T(8,128)(2,1)} %copy-done.21), custom_call_target="tpu_custom_call" | custom-call | tf_op jit(solution)/shard_map/expert_out/pallas_call | solution.py:340
  194.6 4.4 %all-to-all-start.1 = ((bf16[8,48,1792]{2,1,0:T(8,128)(2,1)}), bf16[8,48,1792]{2,1,0:T(8,128)(2,1)S(1)}, u32[]{:S(2)}, u32[]{:S(2)}) async-start(bf16[8,48,1792]{2,1,0:T(8,128)(2,1)} %bitcast.16), calls=%async_computation.1 | async-start | bytes 2752512 | tf_op jit(solution)/shard_map/all_to_all | solution.py:412
  199.1 2.1 mix.3
  201.2 1.6 collective-permute-start.34
  202.7 2.1 mix.2
  205.3 3.3 %collective-permute-start.33 = (bf16[48,1792]{1,0:T(8,128)(2,1)}, bf16[48,1792]{1,0:T(8,128)(2,1)S(1)}, u32[]{:S(2)}, u32[]{:S(2)}) collective-permute-start(bf16[48,1792]{1,0:T(8,128)(2,1)} %get-tuple-element.70), channel_id=1, source_target_pairs={{0,16},{8,24},{16,32},{24,40},{32,48},{40,56},{48,0},{56,8},{1,17}... | collective-permute-start | bytes 516104 | tf_op jit(solution)/shard_map/ppermute | solution.py:398
  208.7 9.9 %all-to-all-done.1.back_ref = bf16[8,48,1792]{2,1,0:T(8,128)(2,1)S(1)} async-done(((bf16[8,48,1792]{2,1,0:T(8,128)(2,1)}), bf16[8,48,1792]{2,1,0:T(8,128)(2,1)S(1)}, u32[]{:S(2)}, u32[]{:S(2)}) %all-to-all-start.1) | async-done | bytes 1376288 | tf_op jit(solution)/shard_map/all_to_all | solution.py:412
  218.5 1.1 copy-done
  219.6 2.5 mix_far.1
  222.2 3.3 %collective-permute-start.21 = (bf16[48,1792]{1,0:T(8,128)(2,1)}, bf16[48,1792]{1,0:T(8,128)(2,1)S(1)}, u32[]{:S(2)}, u32[]{:S(2)}) collective-permute-start(bf16[48,1792]{1,0:T(8,128)(2,1)} %get-tuple-element.56), channel_id=1, source_target_pairs={{0,48},{8,56},{16,0},{24,8},{32,16},{40,24},{48,32},{56,40},{1,49}... | collective-permute-start | bytes 516104 | tf_op jit(solution)/shard_map/ppermute | solution.py:398
  225.5 1.8 collective-permute-start.22
  227.3 3.3 %collective-permute-start.23 = (bf16[48,1792]{1,0:T(8,128)(2,1)}, bf16[48,1792]{1,0:T(8,128)(2,1)S(1)}, u32[]{:S(2)}, u32[]{:S(2)}) collective-permute-start(bf16[48,1792]{1,0:T(8,128)(2,1)} %get-tuple-element.58), channel_id=1, source_target_pairs={{0,40},{8,48},{16,56},{24,0},{32,8},{40,16},{48,24},{56,32},{1,41}... | collective-permute-start | bytes 516104 | tf_op jit(solution)/shard_map/ppermute | solution.py:398
  230.5 2.6 %collective-permute-start.24 = (bf16[48,1792]{1,0:T(8,128)(2,1)}, bf16[48,1792]{1,0:T(8,128)(2,1)S(1)}, u32[]{:S(2)}, u32[]{:S(2)}) collective-permute-start(bf16[48,1792]{1,0:T(8,128)(2,1)} %get-tuple-element.59), channel_id=1, source_target_pairs={{0,32},{8,40},{16,48},{24,56},{32,0},{40,8},{48,16},{56,24},{1,33}... | collective-permute-start | bytes 516104 | tf_op jit(solution)/shard_map/ppermute | solution.py:398
  233.1 5.2 %collective-permute-done.21 = bf16[48,1792]{1,0:T(8,128)(2,1)S(1)} collective-permute-done((bf16[48,1792]{1,0:T(8,128)(2,1)}, bf16[48,1792]{1,0:T(8,128)(2,1)S(1)}, u32[]{:S(2)}, u32[]{:S(2)}) %collective-permute-start.21) | collective-permute-done | bytes 172064 | tf_op jit(solution)/shard_map/ppermute | solution.py:398
  238.3 3.0 %collective-permute-done.22 = bf16[48,1792]{1,0:T(8,128)(2,1)S(1)} collective-permute-done((bf16[48,1792]{1,0:T(8,128)(2,1)}, bf16[48,1792]{1,0:T(8,128)(2,1)S(1)}, u32[]{:S(2)}, u32[]{:S(2)}) %collective-permute-start.22) | collective-permute-done | bytes 172064 | tf_op jit(solution)/shard_map/ppermute | solution.py:398
  241.3 4.3 %collective-permute-done.23 = bf16[48,1792]{1,0:T(8,128)(2,1)S(1)} collective-permute-done((bf16[48,1792]{1,0:T(8,128)(2,1)}, bf16[48,1792]{1,0:T(8,128)(2,1)S(1)}, u32[]{:S(2)}, u32[]{:S(2)}) %collective-permute-start.23) | collective-permute-done | bytes 172064 | tf_op jit(solution)/shard_map/ppermute | solution.py:398
  245.6 8.8 %collective-permute-done.24 = bf16[48,1792]{1,0:T(8,128)(2,1)S(1)} collective-permute-done((bf16[48,1792]{1,0:T(8,128)(2,1)}, bf16[48,1792]{1,0:T(8,128)(2,1)S(1)}, u32[]{:S(2)}, u32[]{:S(2)}) %collective-permute-start.24) | collective-permute-done | bytes 172064 | tf_op jit(solution)/shard_map/ppermute | solution.py:398
  254.3 0.9 add_convert_fusion.4
  (103 shorter events, 10.1 us)
Async XLA Ops:
  3.0 15.8 %copy-start.4 = (bf16[48,1920]{1,0:T(8,128)(2,1)}, bf16[48,1920]{1,0:T(8,128)(2,1)S(1)}, u32[]{:S(2)}) copy-start(bf16[48,1920]{1,0:T(8,128)(2,1)S(1)} %fusion.1.refs_4_.refs_0_) | copy-start | bytes 552964
  3.1 12.3 %collective-permute-start.6 = (bf16[48,1920]{1,0:T(8,128)(2,1)S(1)}, bf16[48,1920]{1,0:T(8,128)(2,1)S(1)}, u32[]{:S(2)}, u32[]{:S(2)}) collective-permute-start(bf16[48,1920]{1,0:T(8,128)(2,1)S(1)} %fusion.1.refs_4_.refs_0_), channel_id=1, source_target_pairs={{0,48},{8,56},{16,0},{24,8},{32,16},{40,24},{48,32},{56,40},{1,49}... | collective-permute-start | bytes 552968 | tf_op jit(solution)/shard_map/ppermute | solution.py:398
  8.5 6.8 %collective-permute-start.5 = (bf16[48,1920]{1,0:T(8,128)(2,1)S(1)}, bf16[48,1920]{1,0:T(8,128)(2,1)S(1)}, u32[]{:S(2)}, u32[]{:S(2)}) collective-permute-start(bf16[48,1920]{1,0:T(8,128)(2,1)S(1)} %fusion.1.refs_4_.refs_0_), channel_id=1, source_target_pairs={{0,8},{8,16},{16,24},{24,32},{32,40},{40,48},{48,56},{56,0},{1,9},... | collective-permute-start | bytes 552968 | tf_op jit(solution)/shard_map/ppermute | solution.py:398
  8.5 10.3 %collective-permute-start.4 = (bf16[48,1920]{1,0:T(8,128)(2,1)S(1)}, bf16[48,1920]{1,0:T(8,128)(2,1)S(1)}, u32[]{:S(2)}, u32[]{:S(2)}) collective-permute-start(bf16[48,1920]{1,0:T(8,128)(2,1)S(1)} %fusion.1.refs_4_.refs_0_), channel_id=1, source_target_pairs={{0,56},{8,0},{16,8},{24,16},{32,24},{40,32},{48,40},{56,48},{1,57}... | collective-permute-start | bytes 552968 | tf_op jit(solution)/shard_map/ppermute | solution.py:398
  15.3 3.5 %copy-start.8 = (bf16[48,1920]{1,0:T(8,128)(2,1)}, bf16[48,1920]{1,0:T(8,128)(2,1)S(1)}, u32[]{:S(2)}) copy-start(bf16[48,1920]{1,0:T(8,128)(2,1)S(1)} %collective-permute-done.6.refs_7_.refs_3_) | copy-start | bytes 552964
  15.3 3.5 %copy-start.9 = (bf16[48,1920]{1,0:T(8,128)(2,1)}, bf16[48,1920]{1,0:T(8,128)(2,1)S(1)}, u32[]{:S(2)}) copy-start(bf16[48,1920]{1,0:T(8,128)(2,1)S(1)} %collective-permute-done.5.refs_6_.refs_2_) | copy-start | bytes 552964
  23.1 4.6 %copy-start.5 = (bf16[48,1920]{1,0:T(8,128)(2,1)S(1)}, bf16[48,1920]{1,0:T(8,128)(2,1)}, u32[]{:S(2)}) copy-start(bf16[48,1920]{1,0:T(8,128)(2,1)} %copy-done.4) | copy-start | bytes 552964
  23.1 66.7 %all-to-all-start = ((bf16[8,48,1792]{2,1,0:T(8,128)(2,1)}), bf16[8,48,1792]{2,1,0:T(8,128)(2,1)S(1)}, u32[]{:S(2)}, u32[]{:S(2)}) async-start(bf16[8,48,1792]{2,1,0:T(8,128)(2,1)} %get-tuple-element.41), calls=%async_computation | async-start | bytes 2752512 | tf_op jit(solution)/shard_map/all_to_all | solution.py:412
  27.7 15.7 %collective-permute-start.3 = (bf16[48,1920]{1,0:T(8,128)(2,1)S(1)}, bf16[48,1920]{1,0:T(8,128)(2,1)S(1)}, u32[]{:S(2)}, u32[]{:S(2)}) collective-permute-start(bf16[48,1920]{1,0:T(8,128)(2,1)S(1)} %copy-done.5), channel_id=1, source_target_pairs={{0,32},{8,40},{16,48},{24,56},{32,0},{40,8},{48,16},{56,24},{1,33}... | collective-permute-start | bytes 552968 | tf_op jit(solution)/shard_map/ppermute | solution.py:398
  33.0 20.7 %collective-permute-start.2 = (bf16[48,1920]{1,0:T(8,128)(2,1)S(1)}, bf16[48,1920]{1,0:T(8,128)(2,1)S(1)}, u32[]{:S(2)}, u32[]{:S(2)}) collective-permute-start(bf16[48,1920]{1,0:T(8,128)(2,1)S(1)} %copy-done.5), channel_id=1, source_target_pairs={{0,24},{8,32},{16,40},{24,48},{32,56},{40,0},{48,8},{56,16},{1,25}... | collective-permute-start | bytes 552968 | tf_op jit(solution)/shard_map/ppermute | solution.py:398
  34.7 19.0 %collective-permute-start.1 = (bf16[48,1920]{1,0:T(8,128)(2,1)S(1)}, bf16[48,1920]{1,0:T(8,128)(2,1)S(1)}, u32[]{:S(2)}, u32[]{:S(2)}) collective-permute-start(bf16[48,1920]{1,0:T(8,128)(2,1)S(1)} %copy-done.5), channel_id=1, source_target_pairs={{0,40},{8,48},{16,56},{24,0},{32,8},{40,16},{48,24},{56,32},{1,41}... | collective-permute-start | bytes 552968 | tf_op jit(solution)/shard_map/ppermute | solution.py:398
  38.1 23.5 %collective-permute-start = (bf16[48,1920]{1,0:T(8,128)(2,1)S(1)}, bf16[48,1920]{1,0:T(8,128)(2,1)S(1)}, u32[]{:S(2)}, u32[]{:S(2)}) collective-permute-start(bf16[48,1920]{1,0:T(8,128)(2,1)S(1)} %copy-done.5), channel_id=1, source_target_pairs={{0,16},{8,24},{16,32},{24,40},{32,48},{40,56},{48,0},{56,8},{1,17}... | collective-permute-start | bytes 552968 | tf_op jit(solution)/shard_map/ppermute | solution.py:398
  43.4 18.2 %copy-start.28 = (bf16[48,1920]{1,0:T(8,128)(2,1)}, bf16[48,1920]{1,0:T(8,128)(2,1)S(1)}, u32[]{:S(2)}) copy-start(bf16[48,1920]{1,0:T(8,128)(2,1)S(1)} %collective-permute-done.3.refs_3_) | copy-start | bytes 552964
  53.8 7.8 %copy-start.29 = (bf16[48,1920]{1,0:T(8,128)(2,1)}, bf16[48,1920]{1,0:T(8,128)(2,1)S(1)}, u32[]{:S(2)}) copy-start(bf16[48,1920]{1,0:T(8,128)(2,1)S(1)} %collective-permute-done.2.refs_2_) | copy-start | bytes 552964
  53.8 7.8 %copy-start.30 = (bf16[48,1920]{1,0:T(8,128)(2,1)}, bf16[48,1920]{1,0:T(8,128)(2,1)S(1)}, u32[]{:S(2)}) copy-start(bf16[48,1920]{1,0:T(8,128)(2,1)S(1)} %collective-permute-done.1.refs_1_) | copy-start | bytes 552964
  66.3 6.2 %collective-permute-start.7 = (bf16[56,1792]{1,0:T(8,128)(2,1)}, bf16[56,1792]{1,0:T(8,128)(2,1)S(1)}, u32[]{:S(2)}, u32[]{:S(2)}) collective-permute-start(bf16[56,1792]{1,0:T(8,128)(2,1)} %get-tuple-element.43), channel_id=1, source_target_pairs={{0,4},{4,0},{64,68},{68,64},{128,132},{132,128},{192,196},{196,192... | collective-permute-start | bytes 602120 | tf_op jit(solution)/shard_map/ppermute | solution.py:408
  66.4 9.3 %collective-permute-start.8 = (bf16[56,1792]{1,0:T(8,128)(2,1)}, bf16[56,1792]{1,0:T(8,128)(2,1)S(1)}, u32[]{:S(2)}, u32[]{:S(2)}) collective-permute-start(bf16[56,1792]{1,0:T(8,128)(2,1)} %get-tuple-element.44), channel_id=1, source_target_pairs={{0,64},{4,68},{64,128},{68,132},{128,192},{132,196},{192,0},{196,4... | collective-permute-start | bytes 602120 | tf_op jit(solution)/shard_map/ppermute | solution.py:408
  68.1 10.8 %collective-permute-start.9 = (bf16[56,1792]{1,0:T(8,128)(2,1)}, bf16[56,1792]{1,0:T(8,128)(2,1)S(1)}, u32[]{:S(2)}, u32[]{:S(2)}) collective-permute-start(bf16[56,1792]{1,0:T(8,128)(2,1)} %get-tuple-element.45), channel_id=1, source_target_pairs={{0,68},{4,64},{64,132},{68,128},{128,196},{132,192},{192,4},{196,0... | collective-permute-start | bytes 602120 | tf_op jit(solution)/shard_map/ppermute | solution.py:408
  69.3 16.1 %collective-permute-start.10 = (bf16[56,1792]{1,0:T(8,128)(2,1)}, bf16[56,1792]{1,0:T(8,128)(2,1)S(1)}, u32[]{:S(2)}, u32[]{:S(2)}) collective-permute-start(bf16[56,1792]{1,0:T(8,128)(2,1)} %get-tuple-element.46), channel_id=1, source_target_pairs={{0,128},{4,132},{64,192},{68,196},{128,0},{132,4},{192,64},{196,68... | collective-permute-start | bytes 602120 | tf_op jit(solution)/shard_map/ppermute | solution.py:408
  70.9 17.7 %collective-permute-start.11 = (bf16[56,1792]{1,0:T(8,128)(2,1)}, bf16[56,1792]{1,0:T(8,128)(2,1)S(1)}, u32[]{:S(2)}, u32[]{:S(2)}) collective-permute-start(bf16[56,1792]{1,0:T(8,128)(2,1)} %get-tuple-element.47), channel_id=1, source_target_pairs={{0,132},{4,128},{64,196},{68,192},{128,4},{132,0},{192,68},{196,64... | collective-permute-start | bytes 602120 | tf_op jit(solution)/shard_map/ppermute | solution.py:408
  72.6 17.2 %copy-start.11 = (bf16[56,1792]{1,0:T(8,128)(2,1)}, bf16[56,1792]{1,0:T(8,128)(2,1)S(1)}, u32[]{:S(2)}) copy-start(bf16[56,1792]{1,0:T(8,128)(2,1)S(1)} %collective-permute-done.7.refs_1_) | copy-start | bytes 602116
  72.6 16.1 %collective-permute-start.12 = (bf16[56,1792]{1,0:T(8,128)(2,1)}, bf16[56,1792]{1,0:T(8,128)(2,1)S(1)}, u32[]{:S(2)}, u32[]{:S(2)}) collective-permute-start(bf16[56,1792]{1,0:T(8,128)(2,1)} %get-tuple-element.48), channel_id=1, source_target_pairs={{0,192},{4,196},{64,0},{68,4},{128,64},{132,68},{192,128},{196,132... | collective-permute-start | bytes 602120 | tf_op jit(solution)/shard_map/ppermute | solution.py:408
  75.8 14.0 %copy-start.12 = (bf16[56,1792]{1,0:T(8,128)(2,1)}, bf16[56,1792]{1,0:T(8,128)(2,1)S(1)}, u32[]{:S(2)}) copy-start(bf16[56,1792]{1,0:T(8,128)(2,1)S(1)} %collective-permute-done.8.refs_2_) | copy-start | bytes 602116
  75.8 14.0 %collective-permute-start.13 = (bf16[56,1792]{1,0:T(8,128)(2,1)}, bf16[56,1792]{1,0:T(8,128)(2,1)S(1)}, u32[]{:S(2)}, u32[]{:S(2)}) collective-permute-start(bf16[56,1792]{1,0:T(8,128)(2,1)} %get-tuple-element.49), channel_id=1, source_target_pairs={{0,196},{4,192},{64,4},{68,0},{128,68},{132,64},{192,132},{196,128... | collective-permute-start | bytes 602120 | tf_op jit(solution)/shard_map/ppermute | solution.py:408
  79.0 10.8 %copy-start.13 = (bf16[56,1792]{1,0:T(8,128)(2,1)}, bf16[56,1792]{1,0:T(8,128)(2,1)S(1)}, u32[]{:S(2)}) copy-start(bf16[56,1792]{1,0:T(8,128)(2,1)S(1)} %collective-permute-done.9.refs_3_) | copy-start | bytes 602116
  85.5 4.3 %copy-start.14 = (bf16[56,1792]{1,0:T(8,128)(2,1)}, bf16[56,1792]{1,0:T(8,128)(2,1)S(1)}, u32[]{:S(2)}) copy-start(bf16[56,1792]{1,0:T(8,128)(2,1)S(1)} %collective-permute-done.10.refs_4_) | copy-start | bytes 602116
  88.7 1.2 copy-start.15
  88.7 1.2 copy-start.16
  89.8 1.1 copy-start.1
  111.1 28.4 %copy-start.33 = (bf16[192,1024]{1,0:T(8,128)(2,1)S(1)}, bf16[192,1024]{1,0:T(8,128)(2,1)}, u32[]{:S(2)}) copy-start(bf16[192,1024]{1,0:T(8,128)(2,1)} %get-tuple-element.53) | copy-start | bytes 1179652
  111.1 12.9 %collective-permute-start.25 = (bf16[192,1024]{1,0:T(8,128)(2,1)}, bf16[192,1024]{1,0:T(8,128)(2,1)S(1)}, u32[]{:S(2)}, u32[]{:S(2)}) collective-permute-start(bf16[192,1024]{1,0:T(8,128)(2,1)} %get-tuple-element.64), channel_id=1, source_target_pairs={{0,1},{1,2},{2,3},{3,0},{4,5},{5,6},{6,7},{7,4},{8,9},{9,10},{10,1... | collective-permute-start | bytes 1179656 | tf_op jit(solution)/shard_map/ppermute | solution.py:398
  112.7 12.7 %collective-permute-start.27 = (bf16[192,1024]{1,0:T(8,128)(2,1)}, bf16[192,1024]{1,0:T(8,128)(2,1)S(1)}, u32[]{:S(2)}, u32[]{:S(2)}) collective-permute-start(bf16[192,1024]{1,0:T(8,128)(2,1)} %get-tuple-element.65), channel_id=1, source_target_pairs={{0,3},{1,0},{2,1},{3,2},{4,7},{5,4},{6,5},{7,6},{8,11},{9,8},{10,9... | collective-permute-start | bytes 1179656 | tf_op jit(solution)/shard_map/ppermute | solution.py:398
  125.0 7.9 %collective-permute-start.26 = (bf16[96,1024]{1,0:T(8,128)(2,1)S(1)}, bf16[96,1024]{1,0:T(8,128)(2,1)S(1)}, u32[]{:S(2)}, u32[]{:S(2)}) collective-permute-start(bf16[96,1024]{1,0:T(8,128)(2,1)S(1)} %add_convert_fusion.1), channel_id=1, source_target_pairs={{0,1},{1,2},{2,3},{3,0},{4,5},{5,6},{6,7},{7,4},{8,9},{9,10},{10,1... | collective-permute-start | bytes 589832 | tf_op jit(solution)/shard_map/ppermute | solution.py:398
  126.4 6.6 %collective-permute-start.28 = (bf16[96,1024]{1,0:T(8,128)(2,1)S(1)}, bf16[96,1024]{1,0:T(8,128)(2,1)S(1)}, u32[]{:S(2)}, u32[]{:S(2)}) collective-permute-start(bf16[96,1024]{1,0:T(8,128)(2,1)S(1)} %add_convert_fusion), channel_id=1, source_target_pairs={{0,3},{1,0},{2,1},{3,2},{4,7},{5,4},{6,5},{7,6},{8,11},{9,8},{10,9... | collective-permute-start | bytes 589832 | tf_op jit(solution)/shard_map/ppermute | solution.py:398
  129.4 29.7 %collective-permute-start.14 = (bf16[192,1024]{1,0:T(8,128)(2,1)}, bf16[192,1024]{1,0:T(8,128)(2,1)S(1)}, u32[]{:S(2)}, u32[]{:S(2)}) collective-permute-start(bf16[192,1024]{1,0:T(8,128)(2,1)} %get-tuple-element.52), channel_id=1, source_target_pairs={{0,1},{1,2},{2,3},{3,0},{4,5},{5,6},{6,7},{7,4},{8,9},{9,10},{10,1... | collective-permute-start | bytes 1179656 | tf_op jit(solution)/shard_map/ppermute | solution.py:398
  134.3 15.3 %copy-start.6 = (bf16[96,1024]{1,0:T(8,128)(2,1)}, bf16[96,1024]{1,0:T(8,128)(2,1)S(1)}, u32[]{:S(2)}) copy-start(bf16[96,1024]{1,0:T(8,128)(2,1)S(1)} %multiply_convert_fusion.refs_0_) | copy-start | bytes 589828
  134.3 15.3 %collective-permute-start.31 = (bf16[96,1024]{1,0:T(8,128)(2,1)S(1)}, bf16[96,1024]{1,0:T(8,128)(2,1)S(1)}, u32[]{:S(2)}, u32[]{:S(2)}) collective-permute-start(bf16[96,1024]{1,0:T(8,128)(2,1)S(1)} %multiply_convert_fusion.refs_0_), channel_id=1, source_target_pairs={{0,1},{1,2},{2,3},{3,0},{4,5},{5,6},{6,7},{7,4},{8,9},{9,10},{10,1... | collective-permute-start | bytes 589832 | tf_op jit(solution)/shard_map/ppermute | solution.py:398
  135.4 14.2 %collective-permute-start.30 = (bf16[96,1024]{1,0:T(8,128)(2,1)S(1)}, bf16[96,1024]{1,0:T(8,128)(2,1)S(1)}, u32[]{:S(2)}, u32[]{:S(2)}) collective-permute-start(bf16[96,1024]{1,0:T(8,128)(2,1)S(1)} %multiply_convert_fusion.refs_0_), channel_id=1, source_target_pairs={{0,2},{1,3},{2,0},{3,1},{4,6},{5,7},{6,4},{7,5},{8,10},{9,11},{10,... | collective-permute-start | bytes 589832 | tf_op jit(solution)/shard_map/ppermute | solution.py:398
  139.5 10.0 %collective-permute-start.29 = (bf16[96,1024]{1,0:T(8,128)(2,1)S(1)}, bf16[96,1024]{1,0:T(8,128)(2,1)S(1)}, u32[]{:S(2)}, u32[]{:S(2)}) collective-permute-start(bf16[96,1024]{1,0:T(8,128)(2,1)S(1)} %multiply_convert_fusion.refs_0_), channel_id=1, source_target_pairs={{0,3},{1,0},{2,1},{3,2},{4,7},{5,4},{6,5},{7,6},{8,11},{9,8},{10,9... | collective-permute-start | bytes 589832 | tf_op jit(solution)/shard_map/ppermute | solution.py:398
  139.5 19.8 %collective-permute-start.16 = (bf16[192,1024]{1,0:T(8,128)(2,1)S(1)}, bf16[192,1024]{1,0:T(8,128)(2,1)S(1)}, u32[]{:S(2)}, u32[]{:S(2)}) collective-permute-start(bf16[192,1024]{1,0:T(8,128)(2,1)S(1)} %copy-done.33), channel_id=1, source_target_pairs={{0,3},{1,0},{2,1},{3,2},{4,7},{5,4},{6,5},{7,6},{8,11},{9,8},{10,9... | collective-permute-start | bytes 1179656 | tf_op jit(solution)/shard_map/ppermute | solution.py:398
  155.0 4.1 %copy-start.25 = (bf16[96,1024]{1,0:T(8,128)(2,1)S(1)}, bf16[96,1024]{1,0:T(8,128)(2,1)}, u32[]{:S(2)}) copy-start(bf16[96,1024]{1,0:T(8,128)(2,1)} %get-tuple-element.51) | copy-start | bytes 589828
  155.0 4.3 %copy-start.24 = (bf16[96,1024]{1,0:T(8,128)(2,1)S(1)}, bf16[96,1024]{1,0:T(8,128)(2,1)}, u32[]{:S(2)}) copy-start(bf16[96,1024]{1,0:T(8,128)(2,1)} %get-tuple-element.55) | copy-start | bytes 589828
  155.0 16.2 %all-to-all-start.2 = ((bf16[8,24,1792]{2,1,0:T(8,128)(2,1)}), bf16[8,24,1792]{2,1,0:T(8,128)(2,1)S(1)}, u32[]{:S(2)}, u32[]{:S(2)}) async-start(bf16[8,24,1792]{2,1,0:T(8,128)(2,1)} %get-tuple-element.68), calls=%async_computation.2 | async-start | bytes 1376256 | tf_op jit(solution)/shard_map/all_to_all | solution.py:412
  159.1 15.6 %copy-start.26 = (bf16[96,1024]{1,0:T(8,128)(2,1)S(1)}, bf16[96,1024]{1,0:T(8,128)(2,1)}, u32[]{:S(2)}) copy-start(bf16[96,1024]{1,0:T(8,128)(2,1)} %get-tuple-element.50) | copy-start | bytes 589828
  159.1 15.7 %copy-start.27 = (bf16[96,1024]{1,0:T(8,128)(2,1)S(1)}, bf16[96,1024]{1,0:T(8,128)(2,1)}, u32[]{:S(2)}) copy-start(bf16[96,1024]{1,0:T(8,128)(2,1)} %get-tuple-element.54) | copy-start | bytes 589828
  159.2 15.5 %collective-permute-start.15 = (bf16[96,1024]{1,0:T(8,128)(2,1)S(1)}, bf16[96,1024]{1,0:T(8,128)(2,1)S(1)}, u32[]{:S(2)}, u32[]{:S(2)}) collective-permute-start(bf16[96,1024]{1,0:T(8,128)(2,1)S(1)} %add_convert_fusion.3), channel_id=1, source_target_pairs={{0,1},{1,2},{2,3},{3,0},{4,5},{5,6},{6,7},{7,4},{8,9},{9,10},{10,1... | collective-permute-start | bytes 589832 | tf_op jit(solution)/shard_map/ppermute | solution.py:398
  159.4 15.4 %collective-permute-start.17 = (bf16[96,1024]{1,0:T(8,128)(2,1)S(1)}, bf16[96,1024]{1,0:T(8,128)(2,1)S(1)}, u32[]{:S(2)}, u32[]{:S(2)}) collective-permute-start(bf16[96,1024]{1,0:T(8,128)(2,1)S(1)} %add_convert_fusion.2), channel_id=1, source_target_pairs={{0,3},{1,0},{2,1},{3,2},{4,7},{5,4},{6,5},{7,6},{8,11},{9,8},{10,9... | collective-permute-start | bytes 589832 | tf_op jit(solution)/shard_map/ppermute | solution.py:398
  171.2 3.8 %copy-start.2 = (bf16[8,24,1792]{2,1,0:T(8,128)(2,1)}, bf16[8,24,1792]{2,1,0:T(8,128)(2,1)S(1)}, u32[]{:S(2)}) copy-start(bf16[8,24,1792]{2,1,0:T(8,128)(2,1)S(1)} %all-to-all-done.2) | copy-start | bytes 2064388
  171.2 22.6 %all-to-all-start.3 = ((bf16[8,24,1792]{2,1,0:T(8,128)(2,1)}), bf16[8,24,1792]{2,1,0:T(8,128)(2,1)S(1)}, u32[]{:S(2)}, u32[]{:S(2)}) async-start(bf16[8,24,1792]{2,1,0:T(8,128)(2,1)} %get-tuple-element.72), calls=%async_computation.3 | async-start | bytes 1376256 | tf_op jit(solution)/shard_map/all_to_all | solution.py:412
  175.0 13.3 %copy-start.7 = (bf16[96,1024]{1,0:T(8,128)(2,1)}, bf16[96,1024]{1,0:T(8,128)(2,1)S(1)}, u32[]{:S(2)}) copy-start(bf16[96,1024]{1,0:T(8,128)(2,1)S(1)} %multiply_convert_fusion.1.refs_0_) | copy-start | bytes 589828
  175.1 12.7 %collective-permute-start.20 = (bf16[96,1024]{1,0:T(8,128)(2,1)S(1)}, bf16[96,1024]{1,0:T(8,128)(2,1)S(1)}, u32[]{:S(2)}, u32[]{:S(2)}) collective-permute-start(bf16[96,1024]{1,0:T(8,128)(2,1)S(1)} %multiply_convert_fusion.1.refs_0_), channel_id=1, source_target_pairs={{0,1},{1,2},{2,3},{3,0},{4,5},{5,6},{6,7},{7,4},{8,9},{9,10},{10,1... | collective-permute-start | bytes 589832 | tf_op jit(solution)/shard_map/ppermute | solution.py:398
  175.1 12.6 %collective-permute-start.19 = (bf16[96,1024]{1,0:T(8,128)(2,1)S(1)}, bf16[96,1024]{1,0:T(8,128)(2,1)S(1)}, u32[]{:S(2)}, u32[]{:S(2)}) collective-permute-start(bf16[96,1024]{1,0:T(8,128)(2,1)S(1)} %multiply_convert_fusion.1.refs_0_), channel_id=1, source_target_pairs={{0,2},{1,3},{2,0},{3,1},{4,6},{5,7},{6,4},{7,5},{8,10},{9,11},{10,... | collective-permute-start | bytes 589832 | tf_op jit(solution)/shard_map/ppermute | solution.py:398
  177.0 11.4 %collective-permute-start.18 = (bf16[96,1024]{1,0:T(8,128)(2,1)S(1)}, bf16[96,1024]{1,0:T(8,128)(2,1)S(1)}, u32[]{:S(2)}, u32[]{:S(2)}) collective-permute-start(bf16[96,1024]{1,0:T(8,128)(2,1)S(1)} %multiply_convert_fusion.1.refs_0_), channel_id=1, source_target_pairs={{0,3},{1,0},{2,1},{3,2},{4,7},{5,4},{6,5},{7,6},{8,11},{9,8},{10,9... | collective-permute-start | bytes 589832 | tf_op jit(solution)/shard_map/ppermute | solution.py:398
  193.8 0.8 copy-start.3
  194.6 23.9 %all-to-all-start.1 = ((bf16[8,48,1792]{2,1,0:T(8,128)(2,1)}), bf16[8,48,1792]{2,1,0:T(8,128)(2,1)S(1)}, u32[]{:S(2)}, u32[]{:S(2)}) async-start(bf16[8,48,1792]{2,1,0:T(8,128)(2,1)} %bitcast.16), calls=%async_computation.1 | async-start | bytes 2752512 | tf_op jit(solution)/shard_map/all_to_all | solution.py:412
  201.2 53.1 %copy-start.32 = (bf16[48,1792]{1,0:T(8,128)(2,1)S(1)}, bf16[48,1792]{1,0:T(8,128)(2,1)}, u32[]{:S(2)}) copy-start(bf16[48,1792]{1,0:T(8,128)(2,1)} %get-tuple-element.73) | copy-start | bytes 516100
  201.2 26.1 %collective-permute-start.34 = (bf16[48,1792]{1,0:T(8,128)(2,1)}, bf16[48,1792]{1,0:T(8,128)(2,1)S(1)}, u32[]{:S(2)}, u32[]{:S(2)}) collective-permute-start(bf16[48,1792]{1,0:T(8,128)(2,1)} %get-tuple-element.74), channel_id=1, source_target_pairs={{0,8},{8,16},{16,24},{24,32},{32,40},{40,48},{48,56},{56,0},{1,9},... | collective-permute-start | bytes 516104 | tf_op jit(solution)/shard_map/ppermute | solution.py:398
  204.9 25.7 %collective-permute-start.32 = (bf16[48,1792]{1,0:T(8,128)(2,1)}, bf16[48,1792]{1,0:T(8,128)(2,1)S(1)}, u32[]{:S(2)}, u32[]{:S(2)}) collective-permute-start(bf16[48,1792]{1,0:T(8,128)(2,1)} %get-tuple-element.69), channel_id=1, source_target_pairs={{0,56},{8,0},{16,8},{24,16},{32,24},{40,32},{48,40},{56,48},{1,57}... | collective-permute-start | bytes 516104 | tf_op jit(solution)/shard_map/ppermute | solution.py:398
  205.3 27.8 %collective-permute-start.33 = (bf16[48,1792]{1,0:T(8,128)(2,1)}, bf16[48,1792]{1,0:T(8,128)(2,1)S(1)}, u32[]{:S(2)}, u32[]{:S(2)}) collective-permute-start(bf16[48,1792]{1,0:T(8,128)(2,1)} %get-tuple-element.70), channel_id=1, source_target_pairs={{0,16},{8,24},{16,32},{24,40},{32,48},{40,56},{48,0},{56,8},{1,17}... | collective-permute-start | bytes 516104 | tf_op jit(solution)/shard_map/ppermute | solution.py:398
  218.5 1.1 copy-start
  222.2 16.2 %collective-permute-start.21 = (bf16[48,1792]{1,0:T(8,128)(2,1)}, bf16[48,1792]{1,0:T(8,128)(2,1)S(1)}, u32[]{:S(2)}, u32[]{:S(2)}) collective-permute-start(bf16[48,1792]{1,0:T(8,128)(2,1)} %get-tuple-element.56), channel_id=1, source_target_pairs={{0,48},{8,56},{16,0},{24,8},{32,16},{40,24},{48,32},{56,40},{1,49}... | collective-permute-start | bytes 516104 | tf_op jit(solution)/shard_map/ppermute | solution.py:398
  225.5 15.8 %collective-permute-start.22 = (bf16[48,1792]{1,0:T(8,128)(2,1)}, bf16[48,1792]{1,0:T(8,128)(2,1)S(1)}, u32[]{:S(2)}, u32[]{:S(2)}) collective-permute-start(bf16[48,1792]{1,0:T(8,128)(2,1)} %get-tuple-element.57), channel_id=1, source_target_pairs={{0,24},{8,32},{16,40},{24,48},{32,56},{40,0},{48,8},{56,16},{1,25}... | collective-permute-start | bytes 516104 | tf_op jit(solution)/shard_map/ppermute | solution.py:398
  227.3 18.3 %collective-permute-start.23 = (bf16[48,1792]{1,0:T(8,128)(2,1)}, bf16[48,1792]{1,0:T(8,128)(2,1)S(1)}, u32[]{:S(2)}, u32[]{:S(2)}) collective-permute-start(bf16[48,1792]{1,0:T(8,128)(2,1)} %get-tuple-element.58), channel_id=1, source_target_pairs={{0,40},{8,48},{16,56},{24,0},{32,8},{40,16},{48,24},{56,32},{1,41}... | collective-permute-start | bytes 516104 | tf_op jit(solution)/shard_map/ppermute | solution.py:398
  230.5 23.8 %collective-permute-start.24 = (bf16[48,1792]{1,0:T(8,128)(2,1)}, bf16[48,1792]{1,0:T(8,128)(2,1)S(1)}, u32[]{:S(2)}, u32[]{:S(2)}) collective-permute-start(bf16[48,1792]{1,0:T(8,128)(2,1)} %get-tuple-element.59), channel_id=1, source_target_pairs={{0,32},{8,40},{16,48},{24,56},{32,0},{40,8},{48,16},{56,24},{1,33}... | collective-permute-start | bytes 516104 | tf_op jit(solution)/shard_map/ppermute | solution.py:398
  (9 other events, 6.4 us)
